TPU v7x, 32 devices: a whole 2x2x4 slice. The times are simulated.
32 devices in a mesh: gy: 8 (over z, x), gx: 4 (over y, core).
Axes of the slice: x: 2, y: 2, z: 4, core: 2. Of those that a mesh axis runs over, the one named last changes fastest.
Arguments:
- ensemble: bfloat16 [32, 2, 512, 512], P(None, None, 'gy', 'gx'), may hold values from -1.1953125 to 1.1953125
- obs_cell: int32 [8, 4, 2048], P('gy', 'gx'), may hold values from 0 to 8191
- obs_level: int32 [8, 4, 2048], P('gy', 'gx'), may hold values from 0 to 1
- innovation: float32 [8, 4, 2048], P('gy', 'gx'), may hold values from -6 to 6
- obs_weight: float32 [8, 4, 2048], P('gy', 'gx'), may hold values from 0.5 to 4
Outputs:
- control: float32 [32, 2, 512, 512], P(None, None, 'gy', 'gx')
- increment: float32 [2, 512, 512], P(None, 'gy', 'gx')
Inputs may be any that keep to these rules, and one draw needn't show every extreme that they name: obs_cell holds row * 128 + column of the observation within its device's block of 64 x 128 cells.
All inputs are finite; a program needn't handle non-finite values.
Results may differ from a plain program's by a relative error of at most 0.0003.
Values sent between devices are 32-bit elements; how exact they have to be, the bound alone decides.
No kernel may reach another device: no remote copies, remote signals or barrier semaphores. Data moves between devices by JAX's collectives and lax.ppermute only.
A program may use at most 128 MiB of HBM per device.

v0:
```python
import jax
import jax.numpy as jnp
from jax import lax
from jax.sharding import PartitionSpec as P

SWEEPS = 4


KAPPA = 0.2
EPS = 1e-06


def with_halo(cells, sides, width):
    for axis, dim in sides:
        count = lax.axis_size(axis)
        ends = count - 1
        head = lax.slice_in_dim(cells, 0, width, axis=dim)
        tail = lax.slice_in_dim(cells, cells.shape[dim] - width, cells.shape[dim], axis=dim)
        cells = jnp.concatenate(
            [
                lax.ppermute(tail, axis, [(i, (i + 1) % count) for i in range(ends)]),
                cells,
                lax.ppermute(head, axis, [((i + 1) % count, i) for i in range(ends)]),
            ],
            axis=dim,
        )
    return cells


def filtered(field):
    rows = field.shape[2]
    cols = field.shape[3]
    padded = with_halo(field, (("gy", 2), ("gx", 3)), SWEEPS)
    row_pos = lax.axis_index("gy") * rows - SWEEPS + jnp.arange(rows + 2 * SWEEPS, dtype=jnp.int32)
    col_pos = lax.axis_index("gx") * cols - SWEEPS + jnp.arange(cols + 2 * SWEEPS, dtype=jnp.int32)
    row_mask = ((row_pos >= 0) & (row_pos < rows * lax.axis_size("gy"))).astype(jnp.float32)
    col_mask = ((col_pos >= 0) & (col_pos < cols * lax.axis_size("gx"))).astype(jnp.float32)
    for sweep in range(1, SWEEPS + 1):
        inner = padded[:, :, 1:-1, 1:-1]
        beside_all = (
            padded[:, :, 2:, 1:-1]
            + padded[:, :, :-2, 1:-1]
            + padded[:, :, 1:-1, 2:]
            + padded[:, :, 1:-1, :-2]
        )
        padded = inner + KAPPA * (beside_all - 4.0 * inner)
        row_keep = row_mask[sweep : rows + 2 * SWEEPS - sweep]
        col_keep = col_mask[sweep : cols + 2 * SWEEPS - sweep]
        padded = padded * (row_keep[:, None] * col_keep[None, :])
    return padded


def on_device(ensemble, obs_cell, obs_level, innovation, obs_weight):
    levels = ensemble.shape[1]
    rows = ensemble.shape[2]
    cols = ensemble.shape[3]
    points = (obs_level * (rows * cols) + obs_cell).reshape(-1)
    weights = obs_weight.reshape(-1)

    def adjoint_obs(values):
        state = jnp.zeros((levels * rows * cols,), jnp.float32).at[points].add(values)
        return state.reshape(levels, rows, cols)

    def hessian(vector):
        state = jnp.sum(ensemble * filtered(vector), axis=0)
        seen = state.reshape(-1)[points]
        back = filtered(ensemble * adjoint_obs(weights * seen)[None])
        return (vector + back, state)

    gradient = filtered(ensemble * adjoint_obs(weights * innovation.reshape(-1))[None])
    bnorm = jnp.sqrt(lax.psum(jnp.sum(gradient * gradient), ("gy", "gx")) + EPS)
    first = gradient / bnorm
    image_one, state_one = hessian(first)
    alpha_one = lax.psum(jnp.sum(first * image_one), ("gy", "gx"))
    remain = image_one - alpha_one * first
    beta_sq = lax.psum(jnp.sum(remain * remain), ("gy", "gx"))
    beta = jnp.sqrt(beta_sq + EPS)
    second = remain / beta
    image_two, state_two = hessian(second)
    alpha_two = lax.psum(jnp.sum(second * image_two), ("gy", "gx"))
    determ = alpha_one * alpha_two - beta * beta
    coef_one = bnorm * alpha_two / determ
    coef_two = -bnorm * beta / determ
    control = coef_one * first + coef_two * second
    increment = coef_one * state_one + coef_two * state_two
    return (control, increment)


def solution(mesh):
    return jax.shard_map(
        on_device,
        mesh=mesh,
        in_specs=(
            P(None, None, "gy", "gx"),
            P("gy", "gx", None),
            P("gy", "gx", None),
            P("gy", "gx", None),
            P("gy", "gx", None),
        ),
        out_specs=(P(None, None, "gy", "gx"), P(None, "gy", "gx")),
        check_vma=False,
    )
```

profile of v0, /device:TPU:0, one launch (start us, length us, event | category | flops | bytes accessed | tf_op | source)
XLA Modules:
  0.0 534.0 jit_solution(15424019485142856667)
XLA Ops:
  2.1 11.3 %scatter_custom_fusion = f32[16384]{0:T(1024)S(1)} fusion(s32[2048]{0:T(1024)S(1)} %bitcast.18, f32[2048]{0:T(1024)S(1)} %mul.242, f32[]{:T(128)} %constant.14.clone.1), kind=kCustom, calls=%fused_computation.181 | custom fusion | flops 2048 | bytes 65540 | tf_op jit(solution)/shard_map/scatter-add | solution.py:61
  15.3 4.9 collective-permute-start
  45.4 5.0 pad_maximum_fusion
  50.4 5.0 fusion.19
  55.4 4.8 fusion.39
  60.2 4.7 fusion.59
  67.7 44.1 %psum.28 = f32[]{:T(128)} all-reduce(f32[]{:T(128)} %get-tuple-element.12), channel_id=1, replica_groups=mesh['gy'=8,'gx'=4] {'gy','gx'}, use_global_device_ids=true, to_apply=%region_2.0 | all-reduce | flops 1 | bytes 8 | tf_op jit(solution)/shard_map/psum | solution.py:71
  141.7 4.8 pad_maximum_fusion.1
  146.5 5.0 fusion.15
  151.5 4.8 fusion.35
  156.3 4.7 fusion.55
  163.3 11.8 %gather_fusion = f32[2048]{0:T(1024)S(1)} fusion(f32[16384]{0:T(1024)S(1)} %bitcast.10, s32[2048]{0:T(1024)S(1)} %broadcast_clamp_fusion), kind=kCustom, calls=%fused_computation | custom fusion | bytes 24576 | tf_op jit(solution)/shard_map/gather | solution.py:66
  175.7 11.8 %scatter_custom_fusion.1 = f32[16384]{0:T(1024)S(1)} fusion(s32[2048]{0:T(1024)S(1)} %bitcast.20, f32[2048]{0:T(1024)} %mul.290, f32[]{:T(128)} %constant.14.clone.1), kind=kCustom, calls=%fused_computation.179 | custom fusion | flops 2048 | bytes 66048 | tf_op jit(solution)/shard_map/scatter-add | solution.py:61
  206.2 4.7 collective-permute-start.10
  223.8 4.9 pad_maximum_fusion.2
  228.7 5.0 fusion.11
  233.6 4.8 fusion.31
  238.4 4.7 fusion.51
  247.1 42.5 %psum.29 = f32[]{:T(128)} all-reduce(f32[]{:T(128)} %get-tuple-element.10), channel_id=1, replica_groups=mesh['gy'=8,'gx'=4] {'gy','gx'}, use_global_device_ids=true, to_apply=%region_6.0 | all-reduce | flops 1 | bytes 8 | tf_op jit(solution)/shard_map/psum | solution.py:74
  293.0 39.4 %psum.30 = f32[]{:T(128)} all-reduce(f32[]{:T(128)} %multiply_reduce_fusion), channel_id=1, replica_groups=mesh['gy'=8,'gx'=4] {'gy','gx'}, use_global_device_ids=true, to_apply=%region_8.0 | all-reduce | flops 1 | bytes 8 | tf_op jit(solution)/shard_map/psum | solution.py:76
  369.2 5.1 pad_maximum_fusion.3
  374.2 5.0 fusion.7
  379.2 4.8 fusion.27
  384.0 4.7 fusion.47
  391.0 20.6 %gather_fusion.1 = f32[2048]{0:T(1024)} fusion(f32[16384]{0:T(1024)S(1)} %bitcast.11, s32[2048]{0:T(1024)S(1)} %broadcast_clamp_fusion), kind=kCustom, calls=%fused_computation.1 | custom fusion | bytes 24576 | tf_op jit(solution)/shard_map/gather | solution.py:66
  412.2 12.2 %scatter_custom_fusion.2 = f32[16384]{0:T(1024)} fusion(s32[2048]{0:T(1024)S(1)} %bitcast.21, f32[2048]{0:T(1024)S(1)} %mul.630, f32[]{:T(128)} %constant.14.clone.1), kind=kCustom, calls=%fused_computation.177 | custom fusion | flops 2048 | bytes 65540 | tf_op jit(solution)/shard_map/scatter-add | solution.py:61
  432.5 4.4 collective-permute-done.17
  458.3 5.0 pad_maximum_fusion.4
  463.3 5.0 fusion.3
  468.2 4.8 fusion.23
  473.0 4.7 fusion.43
  480.7 42.8 %psum.31 = f32[]{:T(128)} all-reduce(f32[]{:T(128)} %fusion.60), channel_id=1, replica_groups=mesh['gy'=8,'gx'=4] {'gy','gx'}, use_global_device_ids=true, to_apply=%region_12.0 | all-reduce | flops 1 | bytes 8 | tf_op jit(solution)/shard_map/psum | solution.py:80
  (130 shorter events, 181.8 us)
Async XLA Ops:
  15.3 7.6 %collective-permute-start = (f32[32,2,4,128]{3,0,2,1:T(8,128)S(1)}, f32[32,2,4,128]{3,0,2,1:T(8,128)S(1)}, u32[]{:S(2)}, u32[]{:S(2)}) collective-permute-start(f32[32,2,4,128]{3,0,2,1:T(8,128)S(1)} %get-tuple-element.32), channel_id=1, source_target_pairs={{0,4},{4,8},{8,12},{12,16},{16,20},{20,24},{24,28},{1,5},{5,9},{9,... | collective-permute-start | bytes 393224 | tf_op jit(solution)/shard_map/ppermute | solution.py:21
  20.2 6.9 %collective-permute-start.1 = (f32[32,2,4,128]{3,0,2,1:T(8,128)S(1)}, f32[32,2,4,128]{3,0,2,1:T(8,128)S(1)}, u32[]{:S(2)}, u32[]{:S(2)}) collective-permute-start(f32[32,2,4,128]{3,0,2,1:T(8,128)S(1)} %get-tuple-element.33), channel_id=1, source_target_pairs={{4,0},{8,4},{12,8},{16,12},{20,16},{24,20},{28,24},{5,1},{9,5},{13... | collective-permute-start | bytes 393224 | tf_op jit(solution)/shard_map/ppermute | solution.py:23
  33.1 5.5 %collective-permute-start.2 = (f32[32,2,72,4]{2,0,3,1:T(8,128)S(1)}, f32[32,2,72,4]{2,0,3,1:T(8,128)S(1)}, u32[]{:S(2)}, u32[]{:S(2)}) collective-permute-start(f32[32,2,72,4]{2,0,3,1:T(8,128)S(1)} %copy.40), channel_id=1, source_target_pairs={{0,1},{1,2},{2,3},{4,5},{5,6},{6,7},{8,9},{9,10},{10,11},{12,13},{... | collective-permute-start | bytes 221192 | tf_op jit(solution)/shard_map/ppermute | solution.py:21
  37.2 5.0 collective-permute-start.3
  112.7 11.1 %copy-start.4 = (f32[32,2,64,128]{3,0,2,1:T(8,128)}, f32[32,2,64,128]{3,0,2,1:T(8,128)S(1)}, u32[]{:S(2)}) copy-start(f32[32,2,64,128]{3,0,2,1:T(8,128)S(1)} %broadcast_divide_fusion.1) | copy-start | bytes 6291460
  112.8 8.1 %collective-permute-start.4 = (f32[32,2,4,128]{3,0,2,1:T(8,128)S(1)}, f32[32,2,4,128]{3,0,2,1:T(8,128)S(1)}, u32[]{:S(2)}, u32[]{:S(2)}) collective-permute-start(f32[32,2,4,128]{3,0,2,1:T(8,128)S(1)} %get-tuple-element.30), channel_id=1, source_target_pairs={{0,4},{4,8},{8,12},{12,16},{16,20},{20,24},{24,28},{1,5},{5,9},{9,... | collective-permute-start | bytes 393224 | tf_op jit(solution)/shard_map/ppermute | solution.py:21
  117.0 6.9 %collective-permute-start.5 = (f32[32,2,4,128]{3,0,2,1:T(8,128)S(1)}, f32[32,2,4,128]{3,0,2,1:T(8,128)S(1)}, u32[]{:S(2)}, u32[]{:S(2)}) collective-permute-start(f32[32,2,4,128]{3,0,2,1:T(8,128)S(1)} %get-tuple-element.31), channel_id=1, source_target_pairs={{4,0},{8,4},{12,8},{16,12},{20,16},{24,20},{28,24},{5,1},{9,5},{13... | collective-permute-start | bytes 393224 | tf_op jit(solution)/shard_map/ppermute | solution.py:23
  129.9 5.4 %collective-permute-start.6 = (f32[32,2,72,4]{2,0,3,1:T(8,128)S(1)}, f32[32,2,72,4]{2,0,3,1:T(8,128)S(1)}, u32[]{:S(2)}, u32[]{:S(2)}) collective-permute-start(f32[32,2,72,4]{2,0,3,1:T(8,128)S(1)} %copy.44), channel_id=1, source_target_pairs={{0,1},{1,2},{2,3},{4,5},{5,6},{6,7},{8,9},{9,10},{10,11},{12,13},{... | collective-permute-start | bytes 221192 | tf_op jit(solution)/shard_map/ppermute | solution.py:21
  134.0 4.5 collective-permute-start.7
  156.3 4.7 copy-start.2
  163.2 11.8 %copy-start.10 = (f32[1,1,2048]{2,1,0:T(1,128)S(1)}, f32[1,1,2048]{2,1,0:T(1,128)}, u32[]{:S(2)}) copy-start(f32[1,1,2048]{2,1,0:T(1,128)} %param.9) | copy-start | bytes 24580
  188.2 10.6 %copy-start.5 = (f32[32,2,64,128]{3,0,2,1:T(8,128)}, f32[32,2,64,128]{3,0,2,1:T(8,128)S(1)}, u32[]{:S(2)}) copy-start(f32[32,2,64,128]{3,0,2,1:T(8,128)S(1)} %convert_multiply_fusion.2) | copy-start | bytes 6291460
  188.3 6.2 %collective-permute-start.8 = (f32[32,2,4,128]{3,0,2,1:T(8,128)S(1)}, f32[32,2,4,128]{3,0,2,1:T(8,128)S(1)}, u32[]{:S(2)}, u32[]{:S(2)}) collective-permute-start(f32[32,2,4,128]{3,0,2,1:T(8,128)S(1)} %get-tuple-element.28), channel_id=1, source_target_pairs={{0,4},{4,8},{8,12},{12,16},{16,20},{20,24},{24,28},{1,5},{5,9},{9,... | collective-permute-start | bytes 393224 | tf_op jit(solution)/shard_map/ppermute | solution.py:21
  192.0 6.9 %collective-permute-start.9 = (f32[32,2,4,128]{3,0,2,1:T(8,128)S(1)}, f32[32,2,4,128]{3,0,2,1:T(8,128)S(1)}, u32[]{:S(2)}, u32[]{:S(2)}) collective-permute-start(f32[32,2,4,128]{3,0,2,1:T(8,128)S(1)} %get-tuple-element.29), channel_id=1, source_target_pairs={{4,0},{8,4},{12,8},{16,12},{20,16},{24,20},{28,24},{5,1},{9,5},{13... | collective-permute-start | bytes 393224 | tf_op jit(solution)/shard_map/ppermute | solution.py:23
  194.5 4.4 copy-start.6
  198.8 0.6 copy-start.8
  206.2 9.4 %collective-permute-start.10 = (f32[32,2,72,4]{2,0,3,1:T(8,128)}, f32[32,2,72,4]{2,0,3,1:T(8,128)}, u32[]{:S(2)}, u32[]{:S(2)}) collective-permute-start(f32[32,2,72,4]{2,0,3,1:T(8,128)} %copy.50), channel_id=1, source_target_pairs={{0,1},{1,2},{2,3},{4,5},{5,6},{6,7},{8,9},{9,10},{10,11},{12,13},{... | collective-permute-start | bytes 221192 | tf_op jit(solution)/shard_map/ppermute | solution.py:21
  214.3 5.4 %collective-permute-start.11 = (f32[32,2,72,4]{2,0,3,1:T(8,128)}, f32[32,2,72,4]{2,0,3,1:T(8,128)}, u32[]{:S(2)}, u32[]{:S(2)}) collective-permute-start(f32[32,2,72,4]{2,0,3,1:T(8,128)} %copy.51), channel_id=1, source_target_pairs={{1,0},{2,1},{3,2},{5,4},{6,5},{7,6},{9,8},{10,9},{11,10},{13,12},{... | collective-permute-start | bytes 221192 | tf_op jit(solution)/shard_map/ppermute | solution.py:23
  335.9 11.1 %copy-start = (f32[32,2,64,128]{3,0,2,1:T(8,128)}, f32[32,2,64,128]{3,0,2,1:T(8,128)S(1)}, u32[]{:S(2)}) copy-start(f32[32,2,64,128]{3,0,2,1:T(8,128)S(1)} %broadcast_divide_fusion) | copy-start | bytes 6291460
  335.9 6.7 %collective-permute-start.12 = (f32[32,2,4,128]{3,0,2,1:T(8,128)S(1)}, f32[32,2,4,128]{3,0,2,1:T(8,128)S(1)}, u32[]{:S(2)}, u32[]{:S(2)}) collective-permute-start(f32[32,2,4,128]{3,0,2,1:T(8,128)S(1)} %get-tuple-element.26), channel_id=1, source_target_pairs={{0,4},{4,8},{8,12},{12,16},{16,20},{20,24},{24,28},{1,5},{5,9},{9,... | collective-permute-start | bytes 393224 | tf_op jit(solution)/shard_map/ppermute | solution.py:21
  340.1 6.9 %collective-permute-start.13 = (f32[32,2,4,128]{3,0,2,1:T(8,128)S(1)}, f32[32,2,4,128]{3,0,2,1:T(8,128)S(1)}, u32[]{:S(2)}, u32[]{:S(2)}) collective-permute-start(f32[32,2,4,128]{3,0,2,1:T(8,128)S(1)} %get-tuple-element.27), channel_id=1, source_target_pairs={{4,0},{8,4},{12,8},{16,12},{20,16},{24,20},{28,24},{5,1},{9,5},{13... | collective-permute-start | bytes 393224 | tf_op jit(solution)/shard_map/ppermute | solution.py:23
  342.6 4.4 copy-start.7
  347.0 0.6 copy-start.9
  354.3 6.7 %collective-permute-start.14 = (f32[32,2,72,4]{2,0,3,1:T(8,128)}, f32[32,2,72,4]{2,0,3,1:T(8,128)}, u32[]{:S(2)}, u32[]{:S(2)}) collective-permute-start(f32[32,2,72,4]{2,0,3,1:T(8,128)} %copy.54), channel_id=1, source_target_pairs={{0,1},{1,2},{2,3},{4,5},{5,6},{6,7},{8,9},{9,10},{10,11},{12,13},{... | collective-permute-start | bytes 221192 | tf_op jit(solution)/shard_map/ppermute | solution.py:21
  359.7 5.4 %collective-permute-start.15 = (f32[32,2,72,4]{2,0,3,1:T(8,128)}, f32[32,2,72,4]{2,0,3,1:T(8,128)}, u32[]{:S(2)}, u32[]{:S(2)}) collective-permute-start(f32[32,2,72,4]{2,0,3,1:T(8,128)} %copy.55), channel_id=1, source_target_pairs={{1,0},{2,1},{3,2},{5,4},{6,5},{7,6},{9,8},{10,9},{11,10},{13,12},{... | collective-permute-start | bytes 221192 | tf_op jit(solution)/shard_map/ppermute | solution.py:23
  426.0 10.9 %copy-start.3 = (f32[32,2,64,128]{3,0,2,1:T(8,128)}, f32[32,2,64,128]{3,0,2,1:T(8,128)S(1)}, u32[]{:S(2)}) copy-start(f32[32,2,64,128]{3,0,2,1:T(8,128)S(1)} %convert_multiply_fusion) | copy-start | bytes 6291460
  426.0 6.5 %collective-permute-start.16 = (f32[32,2,4,128]{3,0,2,1:T(8,128)S(1)}, f32[32,2,4,128]{3,0,2,1:T(8,128)S(1)}, u32[]{:S(2)}, u32[]{:S(2)}) collective-permute-start(f32[32,2,4,128]{3,0,2,1:T(8,128)S(1)} %get-tuple-element.24), channel_id=1, source_target_pairs={{0,4},{4,8},{8,12},{12,16},{16,20},{20,24},{24,28},{1,5},{5,9},{9,... | collective-permute-start | bytes 393224 | tf_op jit(solution)/shard_map/ppermute | solution.py:21
  430.0 6.9 %collective-permute-start.17 = (f32[32,2,4,128]{3,0,2,1:T(8,128)S(1)}, f32[32,2,4,128]{3,0,2,1:T(8,128)S(1)}, u32[]{:S(2)}, u32[]{:S(2)}) collective-permute-start(f32[32,2,4,128]{3,0,2,1:T(8,128)S(1)} %get-tuple-element.25), channel_id=1, source_target_pairs={{4,0},{8,4},{12,8},{16,12},{20,16},{24,20},{28,24},{5,1},{9,5},{13... | collective-permute-start | bytes 393224 | tf_op jit(solution)/shard_map/ppermute | solution.py:23
  442.9 8.2 %collective-permute-start.18 = (f32[32,2,72,4]{2,0,3,1:T(8,128)S(1)}, f32[32,2,72,4]{2,0,3,1:T(8,128)S(1)}, u32[]{:S(2)}, u32[]{:S(2)}) collective-permute-start(f32[32,2,72,4]{2,0,3,1:T(8,128)S(1)} %copy.60), channel_id=1, source_target_pairs={{0,1},{1,2},{2,3},{4,5},{5,6},{6,7},{8,9},{9,10},{10,11},{12,13},{... | collective-permute-start | bytes 221192 | tf_op jit(solution)/shard_map/ppermute | solution.py:21
  449.8 5.3 collective-permute-start.19
  473.0 4.7 copy-start.1
where the time goes:
time: 542 us; the launch traced here: 534 us
  blocking collectives  169 us (31%)
  other arithmetic  165 us (30%)
  local copies, waits for them, and re-layouts  121 us (22%)
  starting transfers between devices  47.1 us (9%)
  waiting for transfers between devices  28 us (5%)
    mul x19, other arithmetic, filtered(): padded = padded * (row_keep[:, None] * col_keep[None, :])  72.4 us
    psum x1, blocking collectives, on_device(): bnorm = jnp.sqrt(lax.psum(jnp.sum(gradient * gradient), ('gy', 'gx')) + EPS)  44.1 us
    psum x1, blocking collectives, on_device(): alpha_two = lax.psum(jnp.sum(second * image_two), ('gy', 'gx'))  42.8 us
    psum x1, blocking collectives, on_device(): alpha_one = lax.psum(jnp.sum(first * image_one), ('gy', 'gx'))  42.5 us
    psum x1, blocking collectives, on_device(): beta_sq = lax.psum(jnp.sum(remain * remain), ('gy', 'gx'))  39.4 us
    scatter-add x3, other arithmetic, adjoint_obs(): jnp.zeros((levels * rows * cols,), jnp.float32).at[points].add(values)  35.3 us
    ppermute x10, starting transfers between devices, with_halo(): lax.ppermute(tail, axis, [(i, (i + 1) % count) for i in range(ends)])  34.1 us
    gather x2, local copies, waits for them, and re-layouts, hessian(): seen = state.reshape(-1)[points]  32.3 us
  transfers between devices with their start and end apart: 20, of which 12 were waited for; matrix products, arithmetic and copies ran while one was open for 6% of the time, Pallas kernels for 0%

commit v1 on v0

v1 whole, which is shorter than its diff:
```python
import functools
import math

import jax
import jax.numpy as jnp
import numpy as np
from jax import lax
from jax.experimental import pallas as pl
from jax.experimental.pallas import tpu as pltpu
from jax.sharding import PartitionSpec as P

SWEEPS = 4
KAPPA = 0.2
EPS = 1e-06
HALO = 2 * SWEEPS
SLOT = 4 * HALO
VMEM = pl.BlockSpec(memory_space=pltpu.VMEM)
F32 = jnp.float32
BF16 = jnp.bfloat16


def band_matrices(lanes):
    out = np.zeros((4, 2, lanes, SWEEPS * lanes), np.float32)
    lane = np.arange(lanes)
    for variant in range(4):
        for kind in range(2):
            col = lane - HALO if kind == 0 else lanes - 3 * HALO + lane % SLOT
            inside = np.ones(lanes, bool)
            if variant % 2:
                inside &= col >= 0
            if variant // 2:
                inside &= col < lanes
            near = np.abs(lane[:, None] - lane[None, :]) <= 1
            if kind == 1:
                near &= (lane[:, None] // SLOT) == (lane[None, :] // SLOT)
            band = (near & inside[:, None] & inside[None, :]).astype(np.float64)
            unit = np.diag(inside.astype(np.float64))
            power = [unit]
            for _ in range(SWEEPS):
                power.append(power[-1] @ band)
            for j in range(SWEEPS):
                q = sum(
                    math.comb(SWEEPS, k) * math.comb(SWEEPS - k, (SWEEPS - k - j) // 2) * power[k]
                    for k in range(SWEEPS - j + 1)
                    if (SWEEPS - k - j) % 2 == 0
                )
                out[variant, kind, :, j * lanes : (j + 1) * lanes] = q
    return out


def shift(x, axis, step):
    count = lax.axis_size(axis)
    return lax.ppermute(x, axis, [(i, i + step) for i in range(count) if 0 <= i + step < count])


def scatter_kernel(ens, cell, level, innov, weight, grid, up, down):
    members, levels, rows, cols = ens.shape
    obs = cell.shape[1]
    span = 256
    row_iota = lax.broadcasted_iota(jnp.int32, (levels * rows, span), 0)
    col_iota = lax.broadcasted_iota(jnp.int32, (cols, span), 0)
    acc = jnp.zeros((4 * levels * rows, cols), F32)
    for start in range(0, obs, span):
        at = slice(start, start + span)
        point = level[:, at] * rows + cell[:, at] // cols
        here = row_iota == point
        w = weight[:, at]
        parts = []
        for value in (w * innov[:, at], w):
            high = value.astype(BF16).astype(F32)
            parts += [high, value - high]
        left = jnp.concatenate([jnp.where(here, part, 0.0).astype(BF16) for part in parts], axis=0)
        right = jnp.where(col_iota == cell[:, at] % cols, 1.0, 0.0).astype(BF16)
        acc += lax.dot_general(left, right, (((1,), (1,)), ((), ())), preferred_element_type=F32)
    n = levels * rows
    g = acc[:n] + acc[n : 2 * n]
    d = acc[2 * n : 3 * n] + acc[3 * n :]
    fields = members * levels
    for l in range(levels):
        grid[0, l] = g[l * rows : (l + 1) * rows]
        grid[1, l] = d[l * rows : (l + 1) * rows]
        up[fields + l] = g[l * rows : l * rows + HALO]
        down[fields + l] = g[(l + 1) * rows - HALO : (l + 1) * rows]

    def edge(m, _):
        for l in range(levels):
            up[l * members + m] = ens[m, l, 0:16, :].astype(F32)[:HALO]
            down[l * members + m] = ens[m, l, rows - 16 : rows, :].astype(F32)[16 - HALO :]
        return 0

    lax.fori_loop(0, members, edge, 0)


def slot_lane(t):
    return SLOT * (t % 4) + HALO * (t // 4)


def reflect(ext, first, count, rows, sign):
    me = lax.axis_index("gy")

    def one(f, base, step):
        for j in range(1, HALO):
            ext[f, pl.ds(base - step * j, 1), :] = sign * ext[f, pl.ds(base + step * j, 1), :]
        if sign < 0:
            ext[f, pl.ds(base, 1), :] = jnp.zeros((1, ext.shape[2]), F32)

    def loop(base, step):
        def body(f, _):
            one(first + f, base, step)
            return 0

        lax.fori_loop(0, count, body, 0)

    pl.when(me == 0)(lambda: loop(HALO - 1, 1))
    pl.when(me == lax.axis_size("gy") - 1)(lambda: loop(HALO + rows, -1))


def pack_sides(ext, fields, lane):
    west = jnp.zeros(ext.shape[1:], F32)
    east = west
    for t, f in enumerate(fields):
        base = slot_lane(t)
        here = (lane >= base) & (lane < base + HALO)
        x = ext[f]
        west = jnp.where(here, pltpu.roll(x, base, 1) if base else x, west)
        east = jnp.where(here, pltpu.roll(x, (base + HALO) % x.shape[1], 1), east)
    return west, east


def sides_kernel(ens, grid, north, south, ext, west, east):
    members, levels, rows, cols = ens.shape
    fields = members * levels
    reach = rows + 2 * HALO

    def fill(m, _):
        for l in range(levels):
            ext[l * members + m, HALO : HALO + rows, :] = ens[m, l].astype(F32)
        return 0

    lax.fori_loop(0, members, fill, 0)
    for l in range(levels):
        ext[fields + l, HALO : HALO + rows, :] = grid[0, l]

    def ends(f, _):
        ext[f, 0:HALO, :] = north[f]
        ext[f, HALO + rows : reach, :] = south[f]
        return 0

    lax.fori_loop(0, fields + levels, ends, 0)
    reflect(ext, 0, fields, rows, 1.0)
    reflect(ext, fields, levels, rows, -1.0)
    lane = lax.broadcasted_iota(jnp.int32, (reach, cols), 1)

    def pack(p, _):
        w, e = pack_sides(ext, [p * 16 + t for t in range(16)], lane)
        west[p] = w
        east[p] = e
        return 0

    lax.fori_loop(0, fields // 16, pack, 0)
    w, e = pack_sides(ext, [fields + l for l in range(levels)], lane)
    west[fields // 16] = w
    east[fields // 16] = e


def grid_sides_kernel(p, north, south, ext, west, east):
    levels, rows, cols = p.shape
    for l in range(levels):
        ext[l, HALO : HALO + rows, :] = p[l]
        ext[l, 0:HALO, :] = north[l]
        ext[l, HALO + rows :, :] = south[l]
    reflect(ext, 0, levels, rows, -1.0)
    lane = lax.broadcasted_iota(jnp.int32, ext.shape[1:], 1)
    west[...], east[...] = pack_sides(ext, list(range(levels)), lane)


def spread_grid(gbuf, g, west, east, lane, l, scale):
    base = slot_lane(l)
    cols = g.shape[1]
    main = jnp.where(lane < HALO, pltpu.roll(west, (cols - base) % cols, 1) if base else west, pltpu.roll(g, HALO, 1))
    gbuf[l, 0] = main * scale
    one = jnp.where(lane < 3 * HALO, pltpu.roll(g, 3 * HALO, 1), pltpu.roll(east, (3 * HALO - base) % cols, 1))
    one = jnp.where(lane < SLOT, one, 0.0)
    one = one + pltpu.roll(one, SLOT, 1)
    gbuf[l, 1] = (one + pltpu.roll(one, 2 * SLOT, 1)) * scale


def band_products(lhs, bands, kind, out, count):
    lanes = lhs.shape[1] // 2
    for half in range(SWEEPS // 2):
        r = jnp.dot(
            lhs[0:count, :],
            bands[kind, :, half * 2 * lanes : (half + 1) * 2 * lanes],
            preferred_element_type=F32,
        )
        out[2 * half, 0:count, :] = r[:, :lanes]
        out[2 * half + 1, 0:count, :] = r[:, lanes:]


def split_into(lhs, start, x):
    count, lanes = x.shape
    high = x.astype(BF16)
    lhs[start : start + count, 0:lanes] = high
    lhs[start : start + count, lanes : 2 * lanes] = (x - high.astype(F32)).astype(BF16)


def combine(prod, start, src, f, count):
    def part(k, off):
        return prod[k, pl.ds(start + off, count), :]

    s = SWEEPS
    total = src[f, pl.ds(2 * s, count), :] + src[f, pl.ds(0, count), :]
    for k in range(1, s):
        total += part(k, s + k) + part(k, s - k)
    return total + part(0, s)


def covariance(pack, bands, gbuf, z, fbuf, prod, lhs, xacc, batch, build):
    total, reach, lanes = pack.shape
    inner = reach - HALO
    rows = reach - 2 * HALO
    levels = gbuf.shape[0]
    xacc[...] = jnp.zeros_like(xacc)

    def run(b, kind, level_of):
        for i in range(batch):
            if build is not None:
                pack[b * batch + i] = build(b, i, kind)
            f = pack[b * batch + i] * gbuf[level_of(i), kind]
            fbuf[i] = f
            split_into(lhs, i * reach, f)
        band_products(lhs, bands, kind, prod, batch * reach)
        for i in range(batch):
            v = combine(prod, i * reach, fbuf, i, inner)
            z[b * batch + i] = v
            split_into(lhs, i * inner, v)
        band_products(lhs, bands, kind, prod, batch * inner)
        for i in range(batch):
            v = combine(prod, i * inner, z, b * batch + i, rows)
            xacc[level_of(i), kind] += v * pack[b * batch + i, HALO : HALO + rows, :]

    windows = total // 5
    mains = total - windows
    per_level = mains // levels // batch

    def step(b, _):
        run(b, 0, lambda i: b // per_level)
        return 0

    lax.fori_loop(0, mains // batch, step, 0)
    for b in range(mains // batch, total // batch):
        run(b, 1, lambda i, b=b: (b * batch + i - mains) * levels // windows)


def gather_state(xacc, l, lane):
    main, win = xacc[l, 0], xacc[l, 1]
    cols = main.shape[1]
    win = win + pltpu.roll(win, 2 * SLOT, 1)
    win = win + pltpu.roll(win, SLOT, 1)
    return KAPPA**SWEEPS * jnp.where(lane < cols - 2 * HALO, pltpu.roll(main, cols - HALO, 1), pltpu.roll(win, HALO, 1))


def first_kernel(ext, grid, west, east, bands, pack, z, x, p, up, down, sums, gbuf, fbuf, prod, lhs, xacc, *, batch):
    fields = ext.shape[0] - grid.shape[1]
    levels = grid.shape[1]
    members = fields // levels
    reach, cols = ext.shape[1:]
    rows = reach - 2 * HALO
    lane = lax.broadcasted_iota(jnp.int32, (reach, cols), 1)
    lane_in = lane[:rows]
    for l in range(levels):
        spread_grid(gbuf, ext[fields + l], west[fields // 16], east[fields // 16], lane, l, KAPPA**SWEEPS)

    def build(b, i, kind):
        if kind == 0:
            base = slot_lane(i)
            side = west[b]
            side = pltpu.roll(side, cols - base, 1) if base else side
            return jnp.where(lane < HALO, side, pltpu.roll(ext[b * batch + i], HALO, 1))
        w = b * batch + i - fields
        first = 4 * w
        side = east[w // 4]
        turn = (3 * HALO - HALO * (w % 4)) % cols
        out = pltpu.roll(side, turn, 1) if turn else side
        for q in range(4):
            here = (lane >= SLOT * q) & (lane < SLOT * q + 3 * HALO)
            out = jnp.where(here, pltpu.roll(ext[first + q], (SLOT * q + 3 * HALO) % cols, 1), out)
        return out

    covariance(pack, bands, gbuf, z, fbuf, prod, lhs, xacc, batch, build)
    norm = jnp.zeros((8, cols), F32)
    curve = norm
    for l in range(levels):
        state = gather_state(xacc, l, lane_in)
        push = grid[1, l] * state
        x[l] = state
        p[l] = push
        up[l] = push[:HALO]
        down[l] = push[rows - HALO :]
        norm += jnp.sum((grid[0, l] * state).reshape(rows // 8, 8, cols), axis=0)
        curve += jnp.sum((push * state).reshape(rows // 8, 8, cols), axis=0)
    sums[0] = norm
    sums[1] = curve


def second_kernel(pack, ext, grid, west, east, bands, sums, z, x, share, gbuf, fbuf, prod, lhs, xacc, *, batch):
    levels = grid.shape[1]
    reach, cols = ext.shape[1:]
    rows = reach - 2 * HALO
    lane = lax.broadcasted_iota(jnp.int32, (reach, cols), 1)
    lane_in = lane[:rows]
    for l in range(levels):
        spread_grid(gbuf, ext[l], west[...], east[...], lane, l, KAPPA**SWEEPS)
    covariance(pack, bands, gbuf, z, fbuf, prod, lhs, xacc, batch, None)
    cross = jnp.zeros((8, cols), F32)
    curve = cross
    for l in range(levels):
        state = gather_state(xacc, l, lane_in)
        x[l] = state
        cross += jnp.sum((ext[l, HALO : HALO + rows, :] * state).reshape(rows // 8, 8, cols), axis=0)
        curve += jnp.sum((grid[1, l] * state * state).reshape(rows // 8, 8, cols), axis=0)
    out = jnp.zeros((1, cols), F32)
    place = lax.broadcasted_iota(jnp.int32, (1, cols), 1)
    for i, part in enumerate((sums[0], sums[1], cross, curve)):
        out = jnp.where(place == i, jnp.sum(jnp.sum(part, axis=0, keepdims=True), axis=1, keepdims=True), out)
    share[...] = jnp.broadcast_to(out, share.shape)


def final_kernel(share, z_one, z_two, x_one, x_two, control, increment):
    level = pl.program_id(0)
    group = pl.program_id(1)
    batch, _, rows, cols = control.shape
    total = jnp.sum(share[...], axis=0, keepdims=True)
    place = lax.broadcasted_iota(jnp.int32, (1, cols), 1)
    n0, c1, c2, c3 = (jnp.sum(jnp.where(place == i, total, 0.0), axis=1, keepdims=True) for i in range(4))
    bn2 = n0 + EPS
    alpha_one = (n0 + c1) / bn2
    t = (EPS - c1) / bn2
    rr = jnp.maximum((c2 + 2.0 * t * c1 + t * t * n0) / bn2, 0.0)
    beta_sq = rr + EPS
    alpha_two = (rr + jnp.maximum((c3 + 2.0 * t * c2 + t * t * c1) / bn2, 0.0)) / beta_sq
    det = alpha_one * alpha_two - beta_sq
    coef_b = -1.0 / det
    coef_a = (alpha_two - t) / det
    lane = lax.broadcasted_iota(jnp.int32, (rows, cols), 1)
    levels = x_one.shape[0]
    mains = z_one.shape[0] * 4 // 5
    groups = mains // levels // batch

    def mixed(f):
        return coef_a * z_one[f, SWEEPS : SWEEPS + rows, :] + coef_b * z_two[f, SWEEPS : SWEEPS + rows, :]

    first = (level * groups + group) * batch
    for w in range(batch // 4):
        win = mixed(mains + first // 4 + w)
        for q in range(4):
            i = 4 * w + q
            turn = (cols - 3 * HALO - SLOT * q) % cols
            side = pltpu.roll(win, turn, 1) if turn else win
            control[i, 0] = jnp.where(
                lane < cols - 2 * HALO, pltpu.roll(mixed(first + i), cols - HALO, 1), side
            )

    @pl.when((level == 0) & (group == 0))
    def _():
        for l in range(levels):
            increment[l] = coef_a * x_one[l] + coef_b * x_two[l]


def on_device(ensemble, obs_cell, obs_level, innovation, obs_weight):
    members, levels, rows, cols = ensemble.shape
    fields = members * levels
    reach = rows + 2 * HALO
    batch = 16
    packed = fields + fields // 4
    sides = fields // 16
    devices = lax.axis_size("gy") * lax.axis_size("gx")

    def struct(*shape):
        return jax.ShapeDtypeStruct(shape, F32)

    def call(kernel, outs, n_in, scratch=(), limit=32, **kw):
        return pl.pallas_call(
            kernel,
            out_shape=outs,
            in_specs=[VMEM] * n_in,
            out_specs=jax.tree.map(lambda _: VMEM, outs),
            scratch_shapes=scratch,
            compiler_params=pltpu.CompilerParams(vmem_limit_bytes=limit * 2**20),
            **kw,
        )

    gx = lax.axis_index("gx")
    variant = (gx == 0).astype(jnp.int32) + 2 * (gx == lax.axis_size("gx") - 1).astype(jnp.int32)
    bands = lax.dynamic_index_in_dim(jnp.asarray(band_matrices(cols), BF16), variant, 0, keepdims=False)
    bands = jnp.concatenate([bands, bands], axis=1)

    flat = [a.reshape(1, -1) for a in (obs_cell, obs_level, innovation, obs_weight)]
    grid, up, down = call(
        scatter_kernel,
        (struct(2, levels, rows, cols), struct(fields + levels, HALO, cols), struct(fields + levels, HALO, cols)),
        5,
    )(ensemble, *flat)
    north, south = shift(down, "gy", 1), shift(up, "gy", -1)
    ext, west, east = call(
        sides_kernel,
        (struct(fields + levels, reach, cols), struct(sides + 1, reach, cols), struct(sides + 1, reach, cols)),
        4,
    )(ensemble, grid, north, south)
    from_west, from_east = shift(east, "gx", 1), shift(west, "gx", -1)
    scratch = (
        pltpu.VMEM((levels, 2, reach, cols), F32),
        pltpu.VMEM((batch, reach, cols), F32),
        pltpu.VMEM((SWEEPS, batch * reach, cols), F32),
        pltpu.VMEM((batch * reach, 2 * cols), BF16),
        pltpu.VMEM((levels, 2, rows, cols), F32),
    )
    pack, z_one, x_one, p, up, down, sums = call(
        functools.partial(first_kernel, batch=batch),
        (
            struct(packed, reach, cols),
            struct(packed, reach - HALO, cols),
            struct(levels, rows, cols),
            struct(levels, rows, cols),
            struct(levels, HALO, cols),
            struct(levels, HALO, cols),
            struct(2, 8, cols),
        ),
        5,
        scratch,
    )(ext, grid, from_west, from_east, bands)
    north, south = shift(down, "gy", 1), shift(up, "gy", -1)
    p_ext, west, east = call(
        grid_sides_kernel, (struct(levels, reach, cols), struct(reach, cols), struct(reach, cols)), 3
    )(p, north, south)
    from_west, from_east = shift(east, "gx", 1), shift(west, "gx", -1)
    z_two, x_two, share = call(
        functools.partial(second_kernel, batch=batch),
        (struct(packed, reach - HALO, cols), struct(levels, rows, cols), struct(devices, cols)),
        7,
        scratch,
    )(pack, p_ext, grid, from_west, from_east, bands, sums)
    share = lax.all_to_all(share, ("gy", "gx"), 0, 0, tiled=True)
    return pl.pallas_call(
        final_kernel,
        grid=(levels, members // batch),
        out_shape=(struct(members, levels, rows, cols), struct(levels, rows, cols)),
        in_specs=[VMEM] * 5,
        out_specs=(
            pl.BlockSpec((batch, 1, rows, cols), lambda l, g: (g, l, 0, 0)),
            pl.BlockSpec((levels, rows, cols), lambda l, g: (0, 0, 0)),
        ),
        compiler_params=pltpu.CompilerParams(vmem_limit_bytes=32 * 2**20),
    )(share, z_one, z_two, x_one, x_two)


def solution(mesh):
    return jax.shard_map(
        on_device,
        mesh=mesh,
        in_specs=(
            P(None, None, "gy", "gx"),
            P("gy", "gx", None),
            P("gy", "gx", None),
            P("gy", "gx", None),
            P("gy", "gx", None),
        ),
        out_specs=(P(None, None, "gy", "gx"), P(None, "gy", "gx")),
        check_vma=False,
    )
```

time: 542 us -> 83.3 us (0.15); the launches traced: 534 us -> 82.7 us
  other arithmetic: 165 us -> 0.04 us
  blocking collectives: 169 us -> 14.6 us
  local copies, waits for them, and re-layouts: 121 us -> 6.21 us
  starting transfers between devices: 47.1 us -> 20.3 us
  Pallas kernels: 0 us -> 20.9 us
  waiting for transfers between devices: 28 us -> 19.9 us
    psum x4 -> x0, blocking collectives: 169 us -> none  [the longest x1 44.1 us: on_device(): bnorm = jnp.sqrt(lax.psum(jnp.sum(gradient * gradient), ('gy', 'gx')) + EPS)]
    mul x25 -> x0, other arithmetic: 78.7 us -> none  [the longest x19 72.4 us: filtered(): padded = padded * (row_keep[:, None] * col_keep[None, :])]
    slice x28 -> x0, local copies, waits for them, and re-layouts: 46.6 us -> none  [the longest x15 30.5 us: with_halo(): lax.slice_in_dim(cells, cells.shape[dim] - width, cells.shape[dim], axis=...]
    scatter-add x3 -> x0, other arithmetic: 35.3 us -> none  [adjoint_obs(): jnp.zeros((levels * rows * cols,), jnp.float32).at[points].add(values)]
    ppermute x10 -> x0, local copies, waits for them, and re-layouts: 35.3 us -> none  [the longest x5 17.7 us: with_halo(): lax.ppermute(head, axis, [((i + 1) % count, i) for i in range(ends)])]
    gather x2 -> x0, local copies, waits for them, and re-layouts: 32.3 us -> none  [hessian(): seen = state.reshape(-1)[points]]
    ppermute x20 -> x8, starting transfers between devices: 47.1 us -> 20.3 us  [shift(): lax.ppermute(x, axis, [(i, i + step) for i in range(count) if 0 <= i + st...]
    concatenate x10 -> x1, other arithmetic: 25.9 us -> 0.04 us  [on_device(): bands = jnp.concatenate([bands, bands], axis=1)]
  transfers between devices with their start and end apart: 20 -> 8, of which waited for: 12 -> 4; matrix products, arithmetic and copies ran while one was open for 6% -> 1% of each run, Pallas kernels for 0% -> 0%
where the time goes in v1:
time: 83.3 us; the launch traced here: 82.7 us
  Pallas kernels  20.9 us (25%)
  starting transfers between devices  20.3 us (24%)
  waiting for transfers between devices  19.9 us (24%)
  blocking collectives  14.6 us (18%)
  local copies, waits for them, and re-layouts  6.21 us (7%)
    ppermute x8, starting transfers between devices, shift(): lax.ppermute(x, axis, [(i, i + step) for i in range(count) if 0 <= i + st...  20.3 us
    ppermute x8, waiting for transfers between devices, shift(): lax.ppermute(x, axis, [(i, i + step) for i in range(count) if 0 <= i + st...  19.9 us
    all_to_all x1, blocking collectives, on_device(): share = lax.all_to_all(share, ('gy', 'gx'), 0, 0, tiled=True)  14.6 us
    pallas_call x1, Pallas kernels, on_device(): call(functools.partial(first_kernel, batch=batch), (struct(packed, reach,...  7.44 us
    pallas_call x1, Pallas kernels, on_device(): call(functools.partial(second_kernel, batch=batch), (struct(packed, reach...  6.64 us
    unnamed x12, local copies, waits for them, and re-layouts  5.23 us
    pallas_call x1, Pallas kernels, on_device(): pl.pallas_call(final_kernel, grid=(levels, members // batch), out_shape=(...  3 us
    pallas_call x1, Pallas kernels, on_device(): call(sides_kernel, (struct(fields + levels, reach, cols), struct(sides +...  2.8 us
  transfers between devices with their start and end apart: 8, of which 4 were waited for; matrix products, arithmetic and copies ran while one was open for 1% of the time, Pallas kernels for 0%

profile of v1, /device:TPU:0, one launch (start us, length us, event | category | flops | bytes accessed | tf_op | source)
XLA Modules:
  0.0 82.7 jit_solution(1444676143290966008)
XLA Ops:
  0.6 0.0 copy-start
  0.6 1.2 %copy-done = bf16[32,2,64,128]{3,2,1,0:T(8,128)(2,1)S(1)} copy-done((bf16[32,2,64,128]{3,2,1,0:T(8,128)(2,1)S(1)}, bf16[32,2,64,128]{3,2,1,0:T(8,128)(2,1)}, u32[]{:S(2)}) %copy-start) | copy-done | bytes 1048600
  1.9 0.0 copy-start.2
  1.9 0.7 copy-done.2
  2.6 0.7 copy-done.3
  3.3 0.7 copy-done.4
  4.0 0.7 copy-done.5
  4.6 0.9 %shard_map.77 = (f32[2,2,64,128]{3,2,1,0:T(8,128)S(1)}, f32[66,8,128]{2,1,0:T(8,128)S(1)}, f32[66,8,128]{2,1,0:T(8,128)S(1)}) custom-call(bf16[32,2,64,128]{3,2,1,0:T(8,128)(2,1)S(1)} %copy-done, s32[1,2048]{1,0:T(1,128)S(1)} %bitcast.12, s32[1,2048]{1,0:T(1,128)S(1)} %bitcast.13, f32[1,2048]{1,0:T(1,128)S(1)} %bitcast.14, f32[1,2048]{1,0:T(1,128)S(1)} %bitcast.15), custom_call_target="tpu_custom_call" | custom-call | tf_op jit(solution)/shard_map/pallas_call | solution.py:399
  5.6 4.9 %collective-permute-start = (f32[66,8,128]{2,1,0:T(8,128)S(1)}, f32[66,8,128]{2,1,0:T(8,128)S(1)}, u32[]{:S(2)}, u32[]{:S(2)}) collective-permute-start(f32[66,8,128]{2,1,0:T(8,128)S(1)} %get-tuple-element.22), channel_id=1, source_target_pairs={{0,4},{4,8},{8,12},{12,16},{16,20},{20,24},{24,28},{1,5},{5,9},{9,... | collective-permute-start | bytes 811016 | tf_op jit(solution)/shard_map/ppermute | solution.py:53
  10.5 1.3 %collective-permute-start.1 = (f32[66,8,128]{2,1,0:T(8,128)S(1)}, f32[66,8,128]{2,1,0:T(8,128)S(1)}, u32[]{:S(2)}, u32[]{:S(2)}) collective-permute-start(f32[66,8,128]{2,1,0:T(8,128)S(1)} %get-tuple-element.23), channel_id=1, source_target_pairs={{4,0},{8,4},{12,8},{16,12},{20,16},{24,20},{28,24},{5,1},{9,5},{13... | collective-permute-start | bytes 811016 | tf_op jit(solution)/shard_map/ppermute | solution.py:53
  11.8 10.2 %collective-permute-done.north = f32[66,8,128]{2,1,0:T(8,128)S(1)} collective-permute-done((f32[66,8,128]{2,1,0:T(8,128)S(1)}, f32[66,8,128]{2,1,0:T(8,128)S(1)}, u32[]{:S(2)}, u32[]{:S(2)}) %collective-permute-start) | collective-permute-done | bytes 270368 | tf_op jit(solution)/shard_map/ppermute | solution.py:53
  22.0 0.0 collective-permute-done.1.south
  22.0 1.2 %copy-done.1 = bf16[32,2,64,128]{3,2,1,0:T(8,128)(2,1)S(1)} copy-done((bf16[32,2,64,128]{3,2,1,0:T(8,128)(2,1)S(1)}, bf16[32,2,64,128]{3,2,1,0:T(8,128)(2,1)}, u32[]{:S(2)}) %copy-start.1) | copy-done | bytes 1048600
  23.2 2.8 %shard_map.78 = (f32[66,80,128]{2,1,0:T(8,128)S(1)}, f32[5,80,128]{2,1,0:T(8,128)S(1)}, f32[5,80,128]{2,1,0:T(8,128)S(1)}) custom-call(bf16[32,2,64,128]{3,2,1,0:T(8,128)(2,1)S(1)} %copy-done.1, f32[2,2,64,128]{3,2,1,0:T(8,128)S(1)} %get-tuple-element.21.grid, f32[66,8,128]{2,1,0:T(8,128)S(1)} %collective-permute-done.north, ...), custom_call_target="tpu_custom_call" | custom-call | tf_op jit(solution)/shard_map/pallas_call | solution.py:405
  26.0 1.3 %collective-permute-start.2 = (f32[5,80,128]{2,1,0:T(8,128)S(1)}, f32[5,80,128]{2,1,0:T(8,128)S(1)}, u32[]{:S(2)}, u32[]{:S(2)}) collective-permute-start(f32[5,80,128]{2,1,0:T(8,128)S(1)} %get-tuple-element.25), channel_id=1, source_target_pairs={{0,1},{1,2},{2,3},{4,5},{5,6},{6,7},{8,9},{9,10},{10,11},{12,13},{... | collective-permute-start | bytes 614408 | tf_op jit(solution)/shard_map/ppermute | solution.py:53
  27.3 1.3 %collective-permute-start.3 = (f32[5,80,128]{2,1,0:T(8,128)S(1)}, f32[5,80,128]{2,1,0:T(8,128)S(1)}, u32[]{:S(2)}, u32[]{:S(2)}) collective-permute-start(f32[5,80,128]{2,1,0:T(8,128)S(1)} %get-tuple-element.26), channel_id=1, source_target_pairs={{1,0},{2,1},{3,2},{5,4},{6,5},{7,6},{9,8},{10,9},{11,10},{13,12},{... | collective-permute-start | bytes 614408 | tf_op jit(solution)/shard_map/ppermute | solution.py:53
  28.6 1.0 %dynamic-slice_bitcast_fusion = bf16[2,128,512]{2,1,0:T(8,128)(2,1)S(1)} fusion(bf16[4,2,128,512]{3,2,1,0:T(8,128)(2,1)} %constant.18.clone, s32[]{:T(128)S(6)} %select_n.4), kind=kLoop, calls=%fused_computation.1 | loop fusion | bytes 524292 | tf_op jit(solution)/shard_map/jit(dynamic_index_in_dim)/squeeze | solution.py:395
  29.6 0.0 collective-permute-done.2.west
  29.6 2.8 %collective-permute-done.3.east = f32[5,80,128]{2,1,0:T(8,128)S(1)} collective-permute-done((f32[5,80,128]{2,1,0:T(8,128)S(1)}, f32[5,80,128]{2,1,0:T(8,128)S(1)}, u32[]{:S(2)}, u32[]{:S(2)}) %collective-permute-start.3) | collective-permute-done | bytes 204832 | tf_op jit(solution)/shard_map/ppermute | solution.py:53
  32.4 7.4 %shard_map.79 = (f32[80,80,128]{2,1,0:T(8,128)S(1)}, f32[80,72,128]{2,1,0:T(8,128)S(1)}, f32[2,64,128]{2,1,0:T(8,128)S(1)}, f32[2,64,128]{2,1,0:T(8,128)S(1)}, f...) custom-call(f32[66,80,128]{2,1,0:T(8,128)S(1)} %get-tuple-element.24.ext, ...), custom_call_target="tpu_custom_call" | custom-call | tf_op jit(solution)/shard_map/pallas_call | solution.py:418
  39.9 3.9 %collective-permute-start.4 = (f32[2,8,128]{2,1,0:T(8,128)S(1)}, f32[2,8,128]{2,1,0:T(8,128)S(1)}, u32[]{:S(2)}, u32[]{:S(2)}) collective-permute-start(f32[2,8,128]{2,1,0:T(8,128)S(1)} %get-tuple-element.29), channel_id=1, source_target_pairs={{0,4},{4,8},{8,12},{12,16},{16,20},{20,24},{24,28},{1,5},{5,9},{9,... | collective-permute-start | bytes 24584 | tf_op jit(solution)/shard_map/ppermute | solution.py:53
  43.8 1.3 %collective-permute-start.5 = (f32[2,8,128]{2,1,0:T(8,128)S(1)}, f32[2,8,128]{2,1,0:T(8,128)S(1)}, u32[]{:S(2)}, u32[]{:S(2)}) collective-permute-start(f32[2,8,128]{2,1,0:T(8,128)S(1)} %get-tuple-element.30), channel_id=1, source_target_pairs={{4,0},{8,4},{12,8},{16,12},{20,16},{24,20},{28,24},{5,1},{9,5},{13... | collective-permute-start | bytes 24584 | tf_op jit(solution)/shard_map/ppermute | solution.py:53
  45.1 0.0 collective-permute-done.4.north
  45.1 4.6 %collective-permute-done.5.south = f32[2,8,128]{2,1,0:T(8,128)S(1)} collective-permute-done((f32[2,8,128]{2,1,0:T(8,128)S(1)}, f32[2,8,128]{2,1,0:T(8,128)S(1)}, u32[]{:S(2)}, u32[]{:S(2)}) %collective-permute-start.5) | collective-permute-done | bytes 8224 | tf_op jit(solution)/shard_map/ppermute | solution.py:53
  49.8 0.1 shard_map.80
  49.9 5.0 %collective-permute-start.6 = (f32[80,128]{1,0:T(8,128)S(1)}, f32[80,128]{1,0:T(8,128)S(1)}, u32[]{:S(2)}, u32[]{:S(2)}) collective-permute-start(f32[80,128]{1,0:T(8,128)S(1)} %get-tuple-element.32), channel_id=1, source_target_pairs={{0,1},{1,2},{2,3},{4,5},{5,6},{6,7},{8,9},{9,10},{10,11},{12,13},{... | collective-permute-start | bytes 122888 | tf_op jit(solution)/shard_map/ppermute | solution.py:53
  54.9 1.3 %collective-permute-start.7 = (f32[80,128]{1,0:T(8,128)S(1)}, f32[80,128]{1,0:T(8,128)S(1)}, u32[]{:S(2)}, u32[]{:S(2)}) collective-permute-start(f32[80,128]{1,0:T(8,128)S(1)} %get-tuple-element.33), channel_id=1, source_target_pairs={{1,0},{2,1},{3,2},{5,4},{6,5},{7,6},{9,8},{10,9},{11,10},{13,12},{... | collective-permute-start | bytes 122888 | tf_op jit(solution)/shard_map/ppermute | solution.py:53
  56.2 0.0 collective-permute-done.6.west
  56.2 2.3 %collective-permute-done.7.east = f32[80,128]{1,0:T(8,128)S(1)} collective-permute-done((f32[80,128]{1,0:T(8,128)S(1)}, f32[80,128]{1,0:T(8,128)S(1)}, u32[]{:S(2)}, u32[]{:S(2)}) %collective-permute-start.7) | collective-permute-done | bytes 40992 | tf_op jit(solution)/shard_map/ppermute | solution.py:53
  58.5 6.6 %shard_map.81 = (f32[80,72,128]{2,1,0:T(8,128)S(1)}, f32[2,64,128]{2,1,0:T(8,128)S(1)}, f32[32,128]{1,0:T(8,128)S(1)}) custom-call(f32[80,80,128]{2,1,0:T(8,128)S(1)} %get-tuple-element.27.pack, f32[2,80,128]{2,1,0:T(8,128)S(1)} %get-tuple-element.31.ext, f32[2,2,64,128]{3,2,1,0:T(8,128)S(1)} %get-tuple-element.21.grid, ...), custom_call_target="tpu_custom_call" | custom-call | tf_op jit(solution)/shard_map/pallas_call | solution.py:437
  65.1 14.6 %all_to_all.11 = f32[32,1,128]{2,1,0:T(1,128)S(1)} all-to-all(f32[32,1,128]{2,1,0:T(1,128)S(1)} %bitcast.11), channel_id=1, replica_groups=mesh['gy'=8,'gx'=4] {'gy','gx'}, dimensions={0} | all-to-all | bytes 32768 | tf_op jit(solution)/shard_map/all_to_all | solution.py:443
  79.7 3.0 %shard_map.82 = (f32[32,2,64,128]{3,2,1,0:T(8,128)}, f32[2,64,128]{2,1,0:T(8,128)}) custom-call(f32[32,128]{1,0:T(8,128)S(1)} %bitcast.10, f32[80,72,128]{2,1,0:T(8,128)S(1)} %get-tuple-element.36.z_one, f32[80,72,128]{2,1,0:T(8,128)S(1)} %get-tuple-element.37.z_two, f32[2,64,128]{2,1,0:T(8,128)S(1)} %get-tuple-element.38.x_one, ...), custom_call_target="tpu_custom_call" | custom-call | tf_op jit(solution)/shard_map/pallas_call | solution.py:444
  (5 shorter events, 0.0 us)
Async XLA Ops:
  0.6 1.2 %copy-start = (bf16[32,2,64,128]{3,2,1,0:T(8,128)(2,1)S(1)}, bf16[32,2,64,128]{3,2,1,0:T(8,128)(2,1)}, u32[]{:S(2)}) copy-start(bf16[32,2,64,128]{3,2,1,0:T(8,128)(2,1)} %ens.3) | copy-start | bytes 3145732
  1.9 0.7 copy-start.2
  2.6 0.7 copy-start.3
  3.3 0.7 copy-start.4
  4.0 0.7 copy-start.5
  5.6 16.4 %collective-permute-start = (f32[66,8,128]{2,1,0:T(8,128)S(1)}, f32[66,8,128]{2,1,0:T(8,128)S(1)}, u32[]{:S(2)}, u32[]{:S(2)}) collective-permute-start(f32[66,8,128]{2,1,0:T(8,128)S(1)} %get-tuple-element.22), channel_id=1, source_target_pairs={{0,4},{4,8},{8,12},{12,16},{16,20},{20,24},{24,28},{1,5},{5,9},{9,... | collective-permute-start | bytes 811016 | tf_op jit(solution)/shard_map/ppermute | solution.py:53
  10.5 11.5 %collective-permute-start.1 = (f32[66,8,128]{2,1,0:T(8,128)S(1)}, f32[66,8,128]{2,1,0:T(8,128)S(1)}, u32[]{:S(2)}, u32[]{:S(2)}) collective-permute-start(f32[66,8,128]{2,1,0:T(8,128)S(1)} %get-tuple-element.23), channel_id=1, source_target_pairs={{4,0},{8,4},{12,8},{16,12},{20,16},{24,20},{28,24},{5,1},{9,5},{13... | collective-permute-start | bytes 811016 | tf_op jit(solution)/shard_map/ppermute | solution.py:53
  22.0 1.2 %copy-start.1 = (bf16[32,2,64,128]{3,2,1,0:T(8,128)(2,1)S(1)}, bf16[32,2,64,128]{3,2,1,0:T(8,128)(2,1)}, u32[]{:S(2)}) copy-start(bf16[32,2,64,128]{3,2,1,0:T(8,128)(2,1)} %ens.3) | copy-start | bytes 3145732
  26.0 3.6 %collective-permute-start.2 = (f32[5,80,128]{2,1,0:T(8,128)S(1)}, f32[5,80,128]{2,1,0:T(8,128)S(1)}, u32[]{:S(2)}, u32[]{:S(2)}) collective-permute-start(f32[5,80,128]{2,1,0:T(8,128)S(1)} %get-tuple-element.25), channel_id=1, source_target_pairs={{0,1},{1,2},{2,3},{4,5},{5,6},{6,7},{8,9},{9,10},{10,11},{12,13},{... | collective-permute-start | bytes 614408 | tf_op jit(solution)/shard_map/ppermute | solution.py:53
  27.3 5.1 %collective-permute-start.3 = (f32[5,80,128]{2,1,0:T(8,128)S(1)}, f32[5,80,128]{2,1,0:T(8,128)S(1)}, u32[]{:S(2)}, u32[]{:S(2)}) collective-permute-start(f32[5,80,128]{2,1,0:T(8,128)S(1)} %get-tuple-element.26), channel_id=1, source_target_pairs={{1,0},{2,1},{3,2},{5,4},{6,5},{7,6},{9,8},{10,9},{11,10},{13,12},{... | collective-permute-start | bytes 614408 | tf_op jit(solution)/shard_map/ppermute | solution.py:53
  39.9 5.3 %collective-permute-start.4 = (f32[2,8,128]{2,1,0:T(8,128)S(1)}, f32[2,8,128]{2,1,0:T(8,128)S(1)}, u32[]{:S(2)}, u32[]{:S(2)}) collective-permute-start(f32[2,8,128]{2,1,0:T(8,128)S(1)} %get-tuple-element.29), channel_id=1, source_target_pairs={{0,4},{4,8},{8,12},{12,16},{16,20},{20,24},{24,28},{1,5},{5,9},{9,... | collective-permute-start | bytes 24584 | tf_op jit(solution)/shard_map/ppermute | solution.py:53
  43.8 6.0 %collective-permute-start.5 = (f32[2,8,128]{2,1,0:T(8,128)S(1)}, f32[2,8,128]{2,1,0:T(8,128)S(1)}, u32[]{:S(2)}, u32[]{:S(2)}) collective-permute-start(f32[2,8,128]{2,1,0:T(8,128)S(1)} %get-tuple-element.30), channel_id=1, source_target_pairs={{4,0},{8,4},{12,8},{16,12},{20,16},{24,20},{28,24},{5,1},{9,5},{13... | collective-permute-start | bytes 24584 | tf_op jit(solution)/shard_map/ppermute | solution.py:53
  49.9 6.3 %collective-permute-start.6 = (f32[80,128]{1,0:T(8,128)S(1)}, f32[80,128]{1,0:T(8,128)S(1)}, u32[]{:S(2)}, u32[]{:S(2)}) collective-permute-start(f32[80,128]{1,0:T(8,128)S(1)} %get-tuple-element.32), channel_id=1, source_target_pairs={{0,1},{1,2},{2,3},{4,5},{5,6},{6,7},{8,9},{9,10},{10,11},{12,13},{... | collective-permute-start | bytes 122888 | tf_op jit(solution)/shard_map/ppermute | solution.py:53
  54.9 3.6 %collective-permute-start.7 = (f32[80,128]{1,0:T(8,128)S(1)}, f32[80,128]{1,0:T(8,128)S(1)}, u32[]{:S(2)}, u32[]{:S(2)}) collective-permute-start(f32[80,128]{1,0:T(8,128)S(1)} %get-tuple-element.33), channel_id=1, source_target_pairs={{1,0},{2,1},{3,2},{5,4},{6,5},{7,6},{9,8},{10,9},{11,10},{13,12},{... | collective-permute-start | bytes 122888 | tf_op jit(solution)/shard_map/ppermute | solution.py:53

commit v2 on v1

v2 whole, which is shorter than its diff:
```python
import functools
import math

import jax
import jax.numpy as jnp
import numpy as np
from jax import lax
from jax.experimental import pallas as pl
from jax.experimental.pallas import tpu as pltpu
from jax.sharding import PartitionSpec as P

SWEEPS = 4
KAPPA = 0.2
EPS = 1e-06
HALO = 2 * SWEEPS
WIDE = 2 * HALO
PAIR = 4 * WIDE
VMEM = pl.BlockSpec(memory_space=pltpu.VMEM)
F32 = jnp.float32
BF16 = jnp.bfloat16


def band_matrices(lanes):
    out = np.zeros((4, 2, lanes, SWEEPS * lanes), np.float32)
    lane = np.arange(lanes)
    for variant in range(4):
        for kind in range(2):
            col, part = lane, 0 * lane
            if kind == 1:
                j = lane % PAIR
                col = np.where(j < 2 * WIDE, j - WIDE, lanes - 3 * WIDE + j)
                part = lane // (2 * WIDE)
            inside = np.ones(lanes, bool)
            if variant % 2:
                inside &= col >= 0
            if variant // 2:
                inside &= col < lanes
            near = (np.abs(lane[:, None] - lane[None, :]) <= 1) & (part[:, None] == part[None, :])
            band = (near & inside[:, None] & inside[None, :]).astype(np.float64)
            power = [np.diag(inside.astype(np.float64))]
            for _ in range(SWEEPS):
                power.append(power[-1] @ band)
            for j in range(SWEEPS):
                q = sum(
                    math.comb(SWEEPS, k) * math.comb(SWEEPS - k, (SWEEPS - k - j) // 2) * power[k]
                    for k in range(SWEEPS - j + 1)
                    if (SWEEPS - k - j) % 2 == 0
                )
                out[variant, kind, :, j * lanes : (j + 1) * lanes] = q
    return out


def shift(x, axis, step):
    count = lax.axis_size(axis)
    return lax.ppermute(x, axis, [(i, i + step) for i in range(count) if 0 <= i + step < count])


def turn(x, amount):
    amount %= x.shape[-1]
    return pltpu.roll(x, amount, x.ndim - 1) if amount else x


def lanes_of(x):
    return lax.broadcasted_iota(jnp.int32, x.shape, x.ndim - 1)


def scatter_kernel(ens, cell_in, level_in, innov_in, weight_in, grid, up, down, cell, level, innov, weight, first, last, sem):
    members, levels, rows, cols = ens.shape
    obs = cell.shape[-1]
    copies = [
        pltpu.make_async_copy(a, b, sem.at[i])
        for i, (a, b) in enumerate(
            (
                (cell_in, cell),
                (level_in, level),
                (innov_in, innov),
                (weight_in, weight),
                (ens.at[:, :, 0:16, :], first),
                (ens.at[:, :, rows - 16 : rows, :], last),
            )
        )
    ]
    for c in copies:
        c.start()
    for c in copies[:4]:
        c.wait()
    span = 256
    row_iota = lax.broadcasted_iota(jnp.int32, (levels * rows, span), 0)
    col_iota = lax.broadcasted_iota(jnp.int32, (cols, span), 0)
    acc = jnp.zeros((4 * levels * rows, cols), F32)
    for start in range(0, obs, span):
        at = slice(start, start + span)
        spot = cell[0, :, at]
        here = row_iota == level[0, :, at] * rows + spot // cols
        w = weight[0, :, at]
        parts = []
        for value in (w * innov[0, :, at], w):
            high = value.astype(BF16).astype(F32)
            parts += [high, value - high]
        left = jnp.concatenate([jnp.where(here, part, 0.0).astype(BF16) for part in parts], axis=0)
        right = jnp.where(col_iota == spot % cols, 1.0, 0.0).astype(BF16)
        acc += lax.dot_general(left, right, (((1,), (1,)), ((), ())), preferred_element_type=F32)
    n = levels * rows
    g = acc[:n] + acc[n : 2 * n]
    d = acc[2 * n : 3 * n] + acc[3 * n :]
    fields = members * levels
    for l in range(levels):
        grid[0, l] = g[l * rows : (l + 1) * rows]
        grid[1, l] = d[l * rows : (l + 1) * rows]
        up[fields + l] = g[l * rows : l * rows + HALO]
        down[fields + l] = g[(l + 1) * rows - HALO : (l + 1) * rows]
    for c in copies[4:]:
        c.wait()

    def edge(m, _):
        for l in range(levels):
            up[l * members + m] = first[m, l].astype(F32)[:HALO]
            down[l * members + m] = last[m, l].astype(F32)[16 - HALO :]
        return 0

    lax.fori_loop(0, members, edge, 0)


def arrange(u, get, mains, wins, west, east, spans):
    xs = [get(8 * u + t) for t in range(8)]
    lane = lanes_of(xs[0])

    def put(ref, f, value):
        at = 0
        for start, count in spans:
            ref[f, start : start + count, :] = value[at : at + count]
            at += count

    w_strip = e_strip = jnp.zeros_like(xs[0])
    for t, x in enumerate(xs):
        put(mains, 8 * u + t, x)
        here = (lane >= WIDE * t) & (lane < WIDE * (t + 1))
        w_strip = jnp.where(here, turn(x, WIDE * t), w_strip)
        e_strip = jnp.where(here, turn(x, WIDE * (t + 1)), e_strip)
    put(west, u, w_strip)
    put(east, u, e_strip)
    for v in range(4):
        win = jnp.zeros_like(xs[0])
        for q in range(2):
            x = xs[2 * v + q]
            at = lane - PAIR * q
            win = jnp.where((at >= WIDE) & (at < 2 * WIDE), turn(x, PAIR * q + WIDE), win)
            win = jnp.where((at >= 2 * WIDE) & (at < 3 * WIDE), turn(x, PAIR * q + 3 * WIDE), win)
        put(wins, 4 * u + v, win)


def strip_grid(fields, west, east, at, spans):
    w_strip = e_strip = jnp.zeros_like(fields[0])
    lane = lanes_of(w_strip)
    for t, x in enumerate(fields):
        here = (lane >= WIDE * t) & (lane < WIDE * (t + 1))
        w_strip = jnp.where(here, turn(x, WIDE * t), w_strip)
        e_strip = jnp.where(here, turn(x, WIDE * (t + 1)), e_strip)
    row = 0
    for start, count in spans:
        west[at, start : start + count, :] = w_strip[row : row + count]
        east[at, start : start + count, :] = e_strip[row : row + count]
        row += count


def own_kernel(ens_in, grid, bands_in, mains, wins, west, east, g_ext, mirror, bands, ens, sem):
    members, levels, rows, cols = ens.shape
    fields = members * levels
    gx = lax.axis_index("gx")
    variant = jnp.where(gx == 0, 1, 0) + jnp.where(gx == lax.axis_size("gx") - 1, 2, 0)
    copies = [pltpu.make_async_copy(ens_in, ens, sem.at[0])]
    for half in range(2):
        part = bands.at[:, half * cols : (half + 1) * cols, :]
        copies.append(pltpu.make_async_copy(bands_in.at[variant], part, sem.at[1 + half]))
    for c in copies:
        c.start()
    for c in copies:
        c.wait()
    spans = ((HALO, rows),)

    def group(u, _):
        l = 8 * u // members
        arrange(u, lambda f: ens[f - l * members, l].astype(F32), mains, wins, west, east, spans)
        return 0

    lax.fori_loop(0, fields // 8, group, 0)
    strip_grid([grid[k, l] for k in range(2) for l in range(levels)], west, east, fields // 8, spans)
    for l in range(levels):
        g_ext[l, HALO : HALO + rows, :] = grid[0, l]
    mirror[...] = jnp.zeros_like(mirror)
    me = lax.axis_index("gy")
    row = lax.broadcasted_iota(jnp.int32, (HALO, cols), 0)

    def flip(x, step):
        out = jnp.zeros((HALO, cols), F32)
        for j in range(1, HALO):
            if step > 0:
                out = jnp.where(row == HALO - 1 - j, x[j - 1 : j], out)
            else:
                out = jnp.where(row == j, x[HALO - j : HALO - j + 1], out)
        return out

    def side(step):
        at = 0 if step > 0 else rows - HALO
        slot = 0 if step > 0 else 1
        start = 0 if step > 0 else rows - 16
        skip = 0 if step > 0 else 16 - HALO

        def body(m, _):
            for l in range(levels):
                x = ens[m, l, start : start + 16, :].astype(F32)[skip : skip + HALO]
                mirror[slot, l * members + m] = flip(x, step)
            return 0

        lax.fori_loop(0, members, body, 0)
        for l in range(levels):
            mirror[slot, fields + l] = -flip(grid[0, l, at : at + HALO, :], step)

    pl.when(me == 0)(lambda: side(1))
    pl.when(me == lax.axis_size("gy") - 1)(lambda: side(-1))


def halo_kernel(north, south, mirror, *refs):
    mains, wins, west, east, g_ext = refs[5:]
    levels, reach, cols = g_ext.shape
    fields = north.shape[0] - levels
    spans = ((0, HALO), (reach - HALO, HALO))

    def get(f):
        return jnp.concatenate([north[f] + mirror[0, f], south[f] + mirror[1, f]], axis=0)

    def group(u, _):
        arrange(u, get, mains, wins, west, east, spans)
        return 0

    lax.fori_loop(0, fields // 8, group, 0)
    ends = [get(fields + l) for l in range(levels)]
    strip_grid(ends, west, east, fields // 8, spans)
    for l in range(levels):
        g_ext[l, 0:HALO, :] = ends[l][:HALO]
        g_ext[l, reach - HALO :, :] = ends[l][HALO:]


def band_products(lhs, bands, kind, out, count):
    lanes = lhs.shape[1] // 2
    for half in range(SWEEPS // 2):
        r = jnp.dot(
            lhs[0:count, :],
            bands[kind, :, half * 2 * lanes : (half + 1) * 2 * lanes],
            preferred_element_type=F32,
        )
        out[2 * half, 0:count, :] = r[:, :lanes]
        out[2 * half + 1, 0:count, :] = r[:, lanes:]


def split_into(lhs, start, x):
    count, lanes = x.shape
    high = x.astype(BF16)
    lhs[start : start + count, 0:lanes] = high
    lhs[start : start + count, lanes : 2 * lanes] = (x - high.astype(F32)).astype(BF16)


def combine(prod, start, src, f, count):
    def part(k, off):
        return prod[k, pl.ds(start + off, count), :]

    s = SWEEPS
    total = src[f, pl.ds(2 * s, count), :] + src[f, pl.ds(0, count), :]
    for k in range(1, s):
        total += part(k, s + k) + part(k, s - k)
    return total + part(0, s)


def covariance(pack, bands, kind, g, z, xacc, fbuf, prod, lhs, batch, build=None):
    count, reach, _ = pack.shape
    inner, rows = reach - HALO, reach - 2 * HALO
    per_level = count // g.shape[0]
    xacc[...] = jnp.zeros_like(xacc)

    def step(b, _):
        level = b * batch // per_level
        for i in range(batch):
            at = b * batch + i
            if build is not None:
                pack[at] = build(b, i, pack[at])
            f = pack[at] * g[level]
            fbuf[i] = f
            split_into(lhs, i * reach, f)
        band_products(lhs, bands, kind, prod, batch * reach)
        for i in range(batch):
            v = combine(prod, i * reach, fbuf, i, inner)
            z[b * batch + i] = v
            split_into(lhs, i * inner, v)
        band_products(lhs, bands, kind, prod, batch * inner)
        for i in range(batch):
            v = combine(prod, i * inner, z, b * batch + i, rows)
            xacc[level] += v * pack[b * batch + i, HALO : HALO + rows, :]
        return 0

    lax.fori_loop(0, count // batch, step, 0)


def window_grid(g, west, east):
    lane = lanes_of(g)
    win = jnp.where(lane < WIDE, west, turn(g, WIDE))
    win = jnp.where(lane < 2 * WIDE, win, turn(g, 3 * WIDE))
    win = jnp.where(lane < 3 * WIDE, win, turn(east, 3 * WIDE))
    win = jnp.where(lane < PAIR, win, 0.0)
    return (win + turn(win, PAIR)) * KAPPA**SWEEPS


def fold(x):
    return jnp.sum(x.reshape(x.shape[0] // 8, 8, x.shape[1]), axis=0)


def main_kernel(pack, g_ext, bands, z, xacc, gbuf, fbuf, prod, lhs, *, batch):
    gbuf[...] = g_ext[...] * KAPPA**SWEEPS
    covariance(pack, bands, 0, gbuf, z, xacc, fbuf, prod, lhs, batch)


def join(main, win, cols):
    win = (win + turn(win, PAIR)) * KAPPA**SWEEPS
    lane = lanes_of(win)
    state = jnp.where(lane < HALO, turn(win, -WIDE), main * KAPPA**SWEEPS)
    return jnp.where(lane < cols - HALO, state, turn(win, cols - 3 * WIDE)), win


def first_kernel(pack_in, g_ext, grid, west, east, bands, xmain, pack, z, x, p, up, down, side, sums, gbuf, fbuf, prod, lhs, xacc, *, batch):
    del pack_in
    levels, reach, cols = g_ext.shape
    rows = reach - 2 * HALO
    last = west.shape[0] - 1
    for l in range(levels):
        gbuf[l] = window_grid(g_ext[l], turn(west[last], -WIDE * l), turn(east[last], -WIDE * l))
    lane = lax.broadcasted_iota(jnp.int32, (reach, cols), 1)

    def window(b, i, old):
        u = b * (batch // 4) + i // 4
        for q in range(2):
            slot = WIDE * (2 * (i % 4) + q)
            at = lane - PAIR * q
            old = jnp.where((at >= 0) & (at < WIDE), turn(west[u], PAIR * q - slot), old)
            old = jnp.where((at >= 3 * WIDE) & (at < PAIR), turn(east[u], PAIR * q + 3 * WIDE - slot), old)
        return old

    covariance(pack, bands, 1, gbuf, z, xacc, fbuf, prod, lhs, batch, window)
    norm = jnp.zeros((8, cols), F32)
    curve = norm
    lane = lane[:rows]
    d_west, d_east = west[last, HALO : HALO + rows, :], east[last, HALO : HALO + rows, :]
    sides = jnp.zeros((rows, cols), F32)
    for l in range(levels):
        state, win = join(xmain[l], xacc[l], cols)
        push = grid[1, l] * state
        x[l] = state
        p[l] = push
        up[l] = push[:HALO]
        down[l] = push[rows - HALO :]
        norm += fold(grid[0, l] * state)
        curve += fold(push * state)
        base = WIDE * l
        far = WIDE * (levels + l)
        beside = turn(win, base - HALO) * turn(d_west, base - far - HALO)
        sides = jnp.where((lane >= base) & (lane < base + HALO), beside, sides)
        beside = turn(win, base + HALO - 3 * WIDE) * turn(d_east, base + HALO - far)
        sides = jnp.where((lane >= base + HALO) & (lane < base + WIDE), beside, sides)
    side[...] = sides
    up[levels] = sides[:HALO]
    down[levels] = sides[rows - HALO :]
    sums[0] = norm
    sums[1] = curve


def second_kernel(mains, wins, p, side, north, south, grid, bands, sums, zm, zw, x, share, ext, gbuf, fbuf, prod, lhs, xacc, *, batch):
    levels, rows, cols = p.shape
    reach = rows + 2 * HALO
    for l in range(levels + 1):
        ext[l, HALO : HALO + rows, :] = p[l] if l < levels else side[...]
        ext[l, 0:HALO, :] = north[l]
        ext[l, HALO + rows :, :] = south[l]
    me = lax.axis_index("gy")

    def reflect(base, step):
        for l in range(levels + 1):
            for j in range(1, HALO):
                ext[l, base - step * j : base - step * j + 1, :] = -ext[l, base + step * j : base + step * j + 1, :]

    pl.when(me == 0)(lambda: reflect(HALO - 1, 1))
    pl.when(me == lax.axis_size("gy") - 1)(lambda: reflect(HALO + rows, -1))
    lane = lax.broadcasted_iota(jnp.int32, (reach, cols), 1)
    for l in range(levels):
        gbuf[0, l] = ext[l] * KAPPA**SWEEPS
        west = jnp.where(lane < HALO, 0.0, turn(ext[levels], HALO - WIDE * l))
        east = jnp.where(lane < HALO, turn(ext[levels], -HALO - WIDE * l), 0.0)
        gbuf[1, l] = window_grid(ext[l], west, east)
    covariance(mains, bands, 0, gbuf.at[0], zm, xacc.at[0], fbuf, prod, lhs, batch)
    covariance(wins, bands, 1, gbuf.at[1], zw, xacc.at[1], fbuf, prod, lhs, batch)
    cross = jnp.zeros((8, cols), F32)
    curve = cross
    for l in range(levels):
        state, _ = join(xacc[0, l], xacc[1, l], cols)
        x[l] = state
        cross += fold(p[l] * state)
        curve += fold(grid[1, l] * state * state)
    out = jnp.zeros((1, cols), F32)
    place = lax.broadcasted_iota(jnp.int32, (1, cols), 1)
    for i, part in enumerate((sums[0], sums[1], cross, curve)):
        out = jnp.where(place == i, jnp.sum(jnp.sum(part, axis=0, keepdims=True), axis=1, keepdims=True), out)
    share[...] = jnp.broadcast_to(out, share.shape)


def final_kernel(share, zm_one, zw_one, zm_two, zw_two, x_one, x_two, control, increment):
    level = pl.program_id(0)
    group = pl.program_id(1)
    batch, _, rows, cols = control.shape
    total = jnp.sum(share[...], axis=0, keepdims=True)
    place = lax.broadcasted_iota(jnp.int32, (1, cols), 1)
    n0, c1, c2, c3 = (jnp.sum(jnp.where(place == i, total, 0.0), axis=1, keepdims=True) for i in range(4))
    bn2 = n0 + EPS
    alpha_one = (n0 + c1) / bn2
    t = (EPS - c1) / bn2
    rr = jnp.maximum((c2 + 2.0 * t * c1 + t * t * n0) / bn2, 0.0)
    beta_sq = rr + EPS
    alpha_two = (rr + jnp.maximum((c3 + 2.0 * t * c2 + t * t * c1) / bn2, 0.0)) / beta_sq
    det = alpha_one * alpha_two - beta_sq
    coef_b = -1.0 / det
    coef_a = (alpha_two - t) / det
    lane = lax.broadcasted_iota(jnp.int32, (rows, cols), 1)
    groups = zm_one.shape[0] // x_one.shape[0] // batch

    def mixed(one, two, f):
        return coef_a * one[f, SWEEPS : SWEEPS + rows, :] + coef_b * two[f, SWEEPS : SWEEPS + rows, :]

    first = (level * groups + group) * batch
    for w in range(batch // 2):
        win = mixed(zw_one, zw_two, first // 2 + w)
        for q in range(2):
            i = 2 * w + q
            main = jnp.where(lane < HALO, turn(win, -WIDE - PAIR * q), mixed(zm_one, zm_two, first + i))
            control[i, 0] = jnp.where(lane < cols - HALO, main, turn(win, cols - 3 * WIDE - PAIR * q))

    @pl.when((level == 0) & (group == 0))
    def _():
        for l in range(x_one.shape[0]):
            increment[l] = coef_a * x_one[l] + coef_b * x_two[l]


def on_device(ensemble, obs_cell, obs_level, innovation, obs_weight):
    members, levels, rows, cols = ensemble.shape
    fields = members * levels
    reach = rows + 2 * HALO
    batch = 16
    strips = fields // 8 + 1
    devices = lax.axis_size("gy") * lax.axis_size("gx")
    hbm = pl.BlockSpec(memory_space=pltpu.HBM)

    def struct(*shape):
        return jax.ShapeDtypeStruct(shape, F32)

    def call(kernel, outs, ins, scratch=(), limit=16, work=2, **kw):
        return pl.pallas_call(
            kernel,
            out_shape=outs,
            in_specs=[VMEM] * ins if isinstance(ins, int) else ins,
            out_specs=jax.tree.map(lambda _: VMEM, outs),
            scratch_shapes=scratch,
            compiler_params=pltpu.CompilerParams(vmem_limit_bytes=limit * 2**20),
            cost_estimate=pl.CostEstimate(flops=work * 10**9, bytes_accessed=10**6, transcendentals=0),
            **kw,
        )

    bands = jnp.asarray(band_matrices(cols), BF16)
    obs = obs_cell.shape
    edge = pltpu.VMEM((members, levels, 16, cols), BF16)
    grid, up, down = call(
        scatter_kernel,
        (struct(2, levels, rows, cols), struct(fields + levels, HALO, cols), struct(fields + levels, HALO, cols)),
        [hbm] * 5,
        [pltpu.VMEM(obs, jnp.int32)] * 2 + [pltpu.VMEM(obs, F32)] * 2 + [edge, edge, pltpu.SemaphoreType.DMA((6,))],
        limit=60,
    )(ensemble, obs_cell, obs_level, innovation, obs_weight)
    north, south = shift(down, "gy", 1), shift(up, "gy", -1)
    main_shape, win_shape = struct(fields, reach, cols), struct(fields // 2, reach, cols)
    laid = (
        main_shape,
        win_shape,
        struct(strips, reach, cols),
        struct(strips, reach, cols),
        struct(levels, reach, cols),
    )
    *own, mirror, bands = call(
        own_kernel,
        (
            *laid,
            struct(2, fields + levels, HALO, cols),
            jax.ShapeDtypeStruct((2, 2 * cols, SWEEPS * cols), BF16),
        ),
        [hbm, VMEM, hbm],
        [pltpu.VMEM(ensemble.shape, BF16), pltpu.SemaphoreType.DMA((3,))],
    )(ensemble, grid, bands)
    mains, wins, west, east, g_ext = call(halo_kernel, laid, 8, input_output_aliases={3 + i: i for i in range(5)})(
        north, south, mirror, *own
    )
    from_west, from_east = shift(east, "gx", 1), shift(west, "gx", -1)
    work = (
        pltpu.VMEM((batch, reach, cols), F32),
        pltpu.VMEM((SWEEPS, batch * reach, cols), F32),
        pltpu.VMEM((batch * reach, 2 * cols), BF16),
    )
    gbuf = pltpu.VMEM((levels, reach, cols), F32)
    zm_shape, zw_shape = struct(fields, reach - HALO, cols), struct(fields // 2, reach - HALO, cols)
    zm_one, xmain = call(
        functools.partial(main_kernel, batch=batch), (zm_shape, struct(levels, rows, cols)), 3, (gbuf, *work)
    )(mains, g_ext, bands)
    wins, zw_one, x_one, p, up, down, side, sums = call(
        functools.partial(first_kernel, batch=batch),
        (
            win_shape,
            zw_shape,
            struct(levels, rows, cols),
            struct(levels, rows, cols),
            struct(levels + 1, HALO, cols),
            struct(levels + 1, HALO, cols),
            struct(rows, cols),
            struct(2, 8, cols),
        ),
        7,
        (gbuf, *work, pltpu.VMEM((levels, rows, cols), F32)),
        input_output_aliases={0: 0},
    )(wins, g_ext, grid, from_west, from_east, bands, xmain)
    north, south = shift(down, "gy", 1), shift(up, "gy", -1)
    zm_two, zw_two, x_two, share = call(
        functools.partial(second_kernel, batch=batch),
        (zm_shape, zw_shape, struct(levels, rows, cols), struct(devices, cols)),
        9,
        (
            pltpu.VMEM((levels + 1, reach, cols), F32),
            pltpu.VMEM((2, levels, reach, cols), F32),
            *work,
            pltpu.VMEM((2, levels, rows, cols), F32),
        ),
    )(mains, wins, p, side, north, south, grid, bands, sums)
    share = lax.all_to_all(share, ("gy", "gx"), 0, 0, tiled=True)
    return pl.pallas_call(
        final_kernel,
        grid=(levels, members // batch),
        out_shape=(struct(members, levels, rows, cols), struct(levels, rows, cols)),
        in_specs=[VMEM] * 7,
        out_specs=(
            pl.BlockSpec((batch, 1, rows, cols), lambda l, g: (g, l, 0, 0)),
            pl.BlockSpec((levels, rows, cols), lambda l, g: (0, 0, 0)),
        ),
        compiler_params=pltpu.CompilerParams(vmem_limit_bytes=32 * 2**20),
    )(share, zm_one, zw_one, zm_two, zw_two, x_one, x_two)


def solution(mesh):
    return jax.shard_map(
        on_device,
        mesh=mesh,
        in_specs=(
            P(None, None, "gy", "gx"),
            P("gy", "gx", None),
            P("gy", "gx", None),
            P("gy", "gx", None),
            P("gy", "gx", None),
        ),
        out_specs=(P(None, None, "gy", "gx"), P(None, "gy", "gx")),
        check_vma=False,
    )
```

time: 83.3 us -> 69.3 us (0.83)
  waiting for transfers between devices: 19.9 us -> 12.9 us
  starting transfers between devices: 20.3 us -> 14.3 us
  local copies, waits for them, and re-layouts: 6.21 us -> 0.91 us
  Pallas kernels: 20.9 us -> 24.1 us
  blocking collectives: 14.6 us -> 16 us
    ppermute x8 -> x6, waiting for transfers between devices: 19.9 us -> 12.9 us  [shift(): lax.ppermute(x, axis, [(i, i + step) for i in range(count) if 0 <= i + st...]
    ppermute x8 -> x6, starting transfers between devices: 20.3 us -> 14.3 us  [shift(): lax.ppermute(x, axis, [(i, i + step) for i in range(count) if 0 <= i + st...]
    unnamed x12 -> x6, local copies, waits for them, and re-layouts: 5.23 us -> 0.91 us
    pallas_call x1, Pallas kernels: 0.91 us -> 2.73 us  [on_device(): call(scatter_kernel, (struct(2, levels, rows, cols), struct(fields + leve...]
    all_to_all x1, blocking collectives: 14.6 us -> 16 us  [on_device(): share = lax.all_to_all(share, ('gy', 'gx'), 0, 0, tiled=True)]
    pallas_call x4 -> x5, Pallas kernels: 17 us -> 18.3 us  [the longest x1 7.28 us: on_device(): call(functools.partial(second_kernel, batch=batch), (zm_shape, zw_shape,...]
    squeeze x1 -> x0, local copies, waits for them, and re-layouts: 0.97 us -> none  [on_device(): lax.dynamic_index_in_dim(jnp.asarray(band_matrices(cols), BF16), variant,...]
  transfers between devices with their start and end apart: 8 -> 6, of which waited for: 4 -> 3; matrix products, arithmetic and copies ran while one was open for 1% -> 0% of each run, Pallas kernels for 0% -> 9%
where the time goes in v2:
time: 69.3 us; the launch traced here: 69 us
  Pallas kernels  24.1 us (35%)
  blocking collectives  16 us (23%)
  starting transfers between devices  14.3 us (21%)
  waiting for transfers between devices  12.9 us (19%)
  local copies, waits for them, and re-layouts  0.91 us (1%)
  between operations  0.77 us (1%)
    all_to_all x1, blocking collectives, on_device(): share = lax.all_to_all(share, ('gy', 'gx'), 0, 0, tiled=True)  16 us
    ppermute x6, starting transfers between devices, shift(): lax.ppermute(x, axis, [(i, i + step) for i in range(count) if 0 <= i + st...  14.3 us
    ppermute x6, waiting for transfers between devices, shift(): lax.ppermute(x, axis, [(i, i + step) for i in range(count) if 0 <= i + st...  12.9 us
    pallas_call x1, Pallas kernels, on_device(): call(functools.partial(second_kernel, batch=batch), (zm_shape, zw_shape,...  7.28 us
    pallas_call x1, Pallas kernels, on_device(): call(functools.partial(main_kernel, batch=batch), (zm_shape, struct(level...  4.51 us
    pallas_call x1, Pallas kernels, on_device(): call(functools.partial(first_kernel, batch=batch), (win_shape, zw_shape,...  3.45 us
    pallas_call x1, Pallas kernels, on_device(): pl.pallas_call(final_kernel, grid=(levels, members // batch), out_shape=(...  3 us
    pallas_call x1, Pallas kernels, on_device(): call(scatter_kernel, (struct(2, levels, rows, cols), struct(fields + leve...  2.73 us
  transfers between devices with their start and end apart: 6, of which 3 were waited for; matrix products, arithmetic and copies ran while one was open for 0% of the time, Pallas kernels for 9%

profile of v2, /device:TPU:0, one launch (start us, length us, event | category | flops | bytes accessed | tf_op | source)
XLA Modules:
  0.0 69.0 jit_solution(17010090040917644)
XLA Ops:
  0.6 0.0 copy-start.1
  0.6 0.0 copy-start
  0.7 2.7 %shard_map.77 = (f32[2,2,64,128]{3,2,1,0:T(8,128)}, f32[66,8,128]{2,1,0:T(8,128)}, f32[66,8,128]{2,1,0:T(8,128)}) custom-call(bf16[32,2,64,128]{3,2,1,0:T(8,128)(2,1)} %ens_in.1, s32[1,1,2048]{2,1,0:T(1,128)} %cell_in.1, s32[1,1,2048]{2,1,0:T(1,128)} %level_in.1, f32[1,1,2048]{2,1,0:T(1,128)} %innov_in.1, f32[1,1,2048]{2,1,0:T(1,128)} %weight_in.1), custom_call_target="tpu_custom_call" | custom-call | flops 2000000000 | bytes 1000000 | tf_op jit(solution)/shard_map/pallas_call | solution.py:475
  3.4 4.9 %collective-permute-start = (f32[66,8,128]{2,1,0:T(8,128)}, f32[66,8,128]{2,1,0:T(8,128)S(1)}, u32[]{:S(2)}, u32[]{:S(2)}) collective-permute-start(f32[66,8,128]{2,1,0:T(8,128)} %get-tuple-element.31), channel_id=1, source_target_pairs={{0,4},{4,8},{8,12},{12,16},{16,20},{20,24},{24,28},{1,5},{5,9},{9,... | collective-permute-start | bytes 811016 | tf_op jit(solution)/shard_map/ppermute | solution.py:55
  8.3 1.3 %collective-permute-start.1 = (f32[66,8,128]{2,1,0:T(8,128)}, f32[66,8,128]{2,1,0:T(8,128)S(1)}, u32[]{:S(2)}, u32[]{:S(2)}) collective-permute-start(f32[66,8,128]{2,1,0:T(8,128)} %get-tuple-element.32), channel_id=1, source_target_pairs={{4,0},{8,4},{12,8},{16,12},{20,16},{24,20},{28,24},{5,1},{9,5},{13... | collective-permute-start | bytes 811016 | tf_op jit(solution)/shard_map/ppermute | solution.py:55
  9.6 0.0 copy-done.1
  9.6 0.0 copy-done
  9.6 0.0 copy-start.2
  9.6 0.9 %copy-done.2 = f32[2,2,64,128]{3,2,1,0:T(8,128)S(1)} copy-done((f32[2,2,64,128]{3,2,1,0:T(8,128)S(1)}, f32[2,2,64,128]{3,2,1,0:T(8,128)}, u32[]{:S(2)}) %copy-start.2) | copy-done | bytes 131096
  10.5 2.0 %shard_map.78 = (f32[64,80,128]{2,1,0:T(8,128)S(1)}, f32[32,80,128]{2,1,0:T(8,128)S(1)}, f32[9,80,128]{2,1,0:T(8,128)S(1)}, f32[9,80,128]{2,1,0:T(8,128)S(1)}, f...) custom-call(bf16[32,2,64,128]{3,2,1,0:T(8,128)(2,1)S(1)} %copy-done, ...), custom_call_target="tpu_custom_call" | custom-call | flops 2000000000 | bytes 1000000 | tf_op jit(solution)/shard_map/pallas_call | solution.py:491
  12.5 7.6 %collective-permute-done.north = f32[66,8,128]{2,1,0:T(8,128)S(1)} collective-permute-done((f32[66,8,128]{2,1,0:T(8,128)}, f32[66,8,128]{2,1,0:T(8,128)S(1)}, u32[]{:S(2)}, u32[]{:S(2)}) %collective-permute-start) | collective-permute-done | bytes 270368 | tf_op jit(solution)/shard_map/ppermute | solution.py:55
  20.1 0.0 collective-permute-done.1.south
  20.1 1.1 %shard_map.79 = (f32[64,80,128]{2,1,0:T(8,128)S(1)}, f32[32,80,128]{2,1,0:T(8,128)S(1)}, f32[9,80,128]{2,1,0:T(8,128)S(1)}, f32[9,80,128]{2,1,0:T(8,128)S(1)}, f32[2,80,128]{2,1,0:T(8,128)S(1)}) custom-call(f32[66,8,128]{2,1,0:T(8,128)S(1)} %collective-permute-done.north, ...), custom_call_target="tpu_custom_call", output_to_operand_aliasing={{0}: (3, {}), {1}: (4, {}), {2}: (5, {}), {3}: (6, {}), {4}... | custom-call | flops 2000000000 | bytes 1000000 | tf_op jit(solution)/shard_map/pallas_call | solution.py:501
  21.2 1.3 %collective-permute-start.2 = (f32[9,80,128]{2,1,0:T(8,128)S(1)}, f32[9,80,128]{2,1,0:T(8,128)S(1)}, u32[]{:S(2)}, u32[]{:S(2)}) collective-permute-start(f32[9,80,128]{2,1,0:T(8,128)S(1)} %get-tuple-element.43), channel_id=1, source_target_pairs={{0,1},{1,2},{2,3},{4,5},{5,6},{6,7},{8,9},{9,10},{10,11},{12,13},{... | collective-permute-start | bytes 1105928 | tf_op jit(solution)/shard_map/ppermute | solution.py:55
  22.5 1.3 %collective-permute-start.3 = (f32[9,80,128]{2,1,0:T(8,128)S(1)}, f32[9,80,128]{2,1,0:T(8,128)S(1)}, u32[]{:S(2)}, u32[]{:S(2)}) collective-permute-start(f32[9,80,128]{2,1,0:T(8,128)S(1)} %get-tuple-element.44), channel_id=1, source_target_pairs={{1,0},{2,1},{3,2},{5,4},{6,5},{7,6},{9,8},{10,9},{11,10},{13,12},{... | collective-permute-start | bytes 1105928 | tf_op jit(solution)/shard_map/ppermute | solution.py:55
  23.8 4.5 %shard_map.80 = (f32[64,72,128]{2,1,0:T(8,128)S(1)}, f32[2,64,128]{2,1,0:T(8,128)S(1)}) custom-call(f32[64,80,128]{2,1,0:T(8,128)S(1)} %get-tuple-element.40.pack.mains, f32[2,80,128]{2,1,0:T(8,128)S(1)} %get-tuple-element.42.g_ext, bf16[2,256,512]{2,1,0:T(8,128)(2,1)S(1)} %get-tuple-element.45.bands), custom_call_target="tpu_custom_call" | custom-call | flops 2000000000 | bytes 1000000 | tf_op jit(solution)/shard_map/pallas_call | solution.py:512
  28.3 0.0 collective-permute-done.2.west
  28.3 0.0 collective-permute-done.3.east
  28.3 3.4 %shard_map.81 = (f32[32,80,128]{2,1,0:T(8,128)S(1)}, f32[32,72,128]{2,1,0:T(8,128)S(1)}, f32[2,64,128]{2,1,0:T(8,128)S(1)}, f32[2,64,128]{2,1,0:T(8,128)S(1)}, f...) custom-call(f32[32,80,128]{2,1,0:T(8,128)S(1)} %get-tuple-element.41, ...), custom_call_target="tpu_custom_call", output_to_operand_aliasing={{0}: (0, {})} | custom-call | flops 2000000000 | bytes 1000000 | tf_op jit(solution)/shard_map/pallas_call | solution.py:515
  31.8 4.3 %collective-permute-start.4 = (f32[3,8,128]{2,1,0:T(8,128)S(1)}, f32[3,8,128]{2,1,0:T(8,128)S(1)}, u32[]{:S(2)}, u32[]{:S(2)}) collective-permute-start(f32[3,8,128]{2,1,0:T(8,128)S(1)} %get-tuple-element.50), channel_id=1, source_target_pairs={{0,4},{4,8},{8,12},{12,16},{16,20},{20,24},{24,28},{1,5},{5,9},{9,... | collective-permute-start | bytes 36872 | tf_op jit(solution)/shard_map/ppermute | solution.py:55
  36.1 1.3 %collective-permute-start.5 = (f32[3,8,128]{2,1,0:T(8,128)S(1)}, f32[3,8,128]{2,1,0:T(8,128)S(1)}, u32[]{:S(2)}, u32[]{:S(2)}) collective-permute-start(f32[3,8,128]{2,1,0:T(8,128)S(1)} %get-tuple-element.51), channel_id=1, source_target_pairs={{4,0},{8,4},{12,8},{16,12},{20,16},{24,20},{28,24},{5,1},{9,5},{13... | collective-permute-start | bytes 36872 | tf_op jit(solution)/shard_map/ppermute | solution.py:55
  37.4 0.1 collective-permute-done.4.north
  37.5 5.3 %collective-permute-done.5.south = f32[3,8,128]{2,1,0:T(8,128)S(1)} collective-permute-done((f32[3,8,128]{2,1,0:T(8,128)S(1)}, f32[3,8,128]{2,1,0:T(8,128)S(1)}, u32[]{:S(2)}, u32[]{:S(2)}) %collective-permute-start.5) | collective-permute-done | bytes 12320 | tf_op jit(solution)/shard_map/ppermute | solution.py:55
  42.7 7.3 %shard_map.82 = (f32[64,72,128]{2,1,0:T(8,128)S(1)}, f32[32,72,128]{2,1,0:T(8,128)S(1)}, f32[2,64,128]{2,1,0:T(8,128)S(1)}, f32[32,128]{1,0:T(8,128)S(1)}) custom-call(f32[64,80,128]{2,1,0:T(8,128)S(1)} %get-tuple-element.40.pack.mains, f32[32,80,128]{2,1,0:T(8,128)S(1)} %get-tuple-element.47.wins, f32[2,64,128]{2,1,0:T(8,128)S(1)} %get-tuple-element.48.p, ...), custom_call_target="tpu_custom_call" | custom-call | flops 2000000000 | bytes 1000000 | tf_op jit(solution)/shard_map/pallas_call | solution.py:532
  50.0 16.0 %all_to_all.11 = f32[32,1,128]{2,1,0:T(1,128)S(1)} all-to-all(f32[32,1,128]{2,1,0:T(1,128)S(1)} %bitcast.5), channel_id=1, replica_groups=mesh['gy'=8,'gx'=4] {'gy','gx'}, dimensions={0} | all-to-all | bytes 32768 | tf_op jit(solution)/shard_map/all_to_all | solution.py:543
  66.0 3.0 %shard_map.83 = (f32[32,2,64,128]{3,2,1,0:T(8,128)}, f32[2,64,128]{2,1,0:T(8,128)}) custom-call(f32[32,128]{1,0:T(8,128)S(1)} %bitcast.4, f32[64,72,128]{2,1,0:T(8,128)S(1)} %get-tuple-element.54.zm_one, f32[32,72,128]{2,1,0:T(8,128)S(1)} %get-tuple-element.55.zw_one, f32[64,72,128]{2,1,0:T(8,128)S(1)} %get-tuple-element.56.zm_two, ...), custom_call_target="tpu_custom_call" | custom-call | tf_op jit(solution)/shard_map/pallas_call | solution.py:544
Async XLA Ops:
  0.6 9.0 %copy-start.1 = (bf16[4,2,128,512]{3,2,1,0:T(8,128)(2,1)S(1)}, bf16[4,2,128,512]{3,2,1,0:T(8,128)(2,1)}, u32[]{:S(2)}) copy-start(bf16[4,2,128,512]{3,2,1,0:T(8,128)(2,1)} %constant.2.clone.bands_in) | copy-start | bytes 3145732
  0.6 8.9 %copy-start = (bf16[32,2,64,128]{3,2,1,0:T(8,128)(2,1)S(1)}, bf16[32,2,64,128]{3,2,1,0:T(8,128)(2,1)}, u32[]{:S(2)}) copy-start(bf16[32,2,64,128]{3,2,1,0:T(8,128)(2,1)} %ens_in.1) | copy-start | bytes 3145732
  3.4 16.7 %collective-permute-start = (f32[66,8,128]{2,1,0:T(8,128)}, f32[66,8,128]{2,1,0:T(8,128)S(1)}, u32[]{:S(2)}, u32[]{:S(2)}) collective-permute-start(f32[66,8,128]{2,1,0:T(8,128)} %get-tuple-element.31), channel_id=1, source_target_pairs={{0,4},{4,8},{8,12},{12,16},{16,20},{20,24},{24,28},{1,5},{5,9},{9,... | collective-permute-start | bytes 811016 | tf_op jit(solution)/shard_map/ppermute | solution.py:55
  8.3 11.8 %collective-permute-start.1 = (f32[66,8,128]{2,1,0:T(8,128)}, f32[66,8,128]{2,1,0:T(8,128)S(1)}, u32[]{:S(2)}, u32[]{:S(2)}) collective-permute-start(f32[66,8,128]{2,1,0:T(8,128)} %get-tuple-element.32), channel_id=1, source_target_pairs={{4,0},{8,4},{12,8},{16,12},{20,16},{24,20},{28,24},{5,1},{9,5},{13... | collective-permute-start | bytes 811016 | tf_op jit(solution)/shard_map/ppermute | solution.py:55
  9.6 0.9 %copy-start.2 = (f32[2,2,64,128]{3,2,1,0:T(8,128)S(1)}, f32[2,2,64,128]{3,2,1,0:T(8,128)}, u32[]{:S(2)}) copy-start(f32[2,2,64,128]{3,2,1,0:T(8,128)} %get-tuple-element.33.grid) | copy-start | bytes 393220
  21.2 7.1 %collective-permute-start.2 = (f32[9,80,128]{2,1,0:T(8,128)S(1)}, f32[9,80,128]{2,1,0:T(8,128)S(1)}, u32[]{:S(2)}, u32[]{:S(2)}) collective-permute-start(f32[9,80,128]{2,1,0:T(8,128)S(1)} %get-tuple-element.43), channel_id=1, source_target_pairs={{0,1},{1,2},{2,3},{4,5},{5,6},{6,7},{8,9},{9,10},{10,11},{12,13},{... | collective-permute-start | bytes 1105928 | tf_op jit(solution)/shard_map/ppermute | solution.py:55
  22.5 5.8 %collective-permute-start.3 = (f32[9,80,128]{2,1,0:T(8,128)S(1)}, f32[9,80,128]{2,1,0:T(8,128)S(1)}, u32[]{:S(2)}, u32[]{:S(2)}) collective-permute-start(f32[9,80,128]{2,1,0:T(8,128)S(1)} %get-tuple-element.44), channel_id=1, source_target_pairs={{1,0},{2,1},{3,2},{5,4},{6,5},{7,6},{9,8},{10,9},{11,10},{13,12},{... | collective-permute-start | bytes 1105928 | tf_op jit(solution)/shard_map/ppermute | solution.py:55
  31.8 5.7 %collective-permute-start.4 = (f32[3,8,128]{2,1,0:T(8,128)S(1)}, f32[3,8,128]{2,1,0:T(8,128)S(1)}, u32[]{:S(2)}, u32[]{:S(2)}) collective-permute-start(f32[3,8,128]{2,1,0:T(8,128)S(1)} %get-tuple-element.50), channel_id=1, source_target_pairs={{0,4},{4,8},{8,12},{12,16},{16,20},{20,24},{24,28},{1,5},{5,9},{9,... | collective-permute-start | bytes 36872 | tf_op jit(solution)/shard_map/ppermute | solution.py:55
  36.1 6.7 %collective-permute-start.5 = (f32[3,8,128]{2,1,0:T(8,128)S(1)}, f32[3,8,128]{2,1,0:T(8,128)S(1)}, u32[]{:S(2)}, u32[]{:S(2)}) collective-permute-start(f32[3,8,128]{2,1,0:T(8,128)S(1)} %get-tuple-element.51), channel_id=1, source_target_pairs={{4,0},{8,4},{12,8},{16,12},{20,16},{24,20},{28,24},{5,1},{9,5},{13... | collective-permute-start | bytes 36872 | tf_op jit(solution)/shard_map/ppermute | solution.py:55

commit v3 on v2

--- a/solution.py
+++ b/solution.py
@@ -50,9 +50,14 @@
     return out
 
 
-def shift(x, axis, step):
+def swap(x, axis, odd):
     count = lax.axis_size(axis)
-    return lax.ppermute(x, axis, [(i, i + step) for i in range(count) if 0 <= i + step < count])
+    return lax.ppermute(x, axis, [(i + a, i + 1 - a) for i in range(odd, count - 1, 2) for a in range(2)])
+
+
+def by_parity(axis, even, odd):
+    me = jnp.full(even.shape, lax.axis_index(axis), jnp.int32)
+    return jnp.where((me & 1) == 0, even, odd)
 
 
 def turn(x, amount):
@@ -64,7 +69,7 @@
     return lax.broadcasted_iota(jnp.int32, x.shape, x.ndim - 1)
 
 
-def scatter_kernel(ens, cell_in, level_in, innov_in, weight_in, grid, up, down, cell, level, innov, weight, first, last, sem):
+def scatter_kernel(ens, cell_in, level_in, innov_in, weight_in, grid, near, far, cell, level, innov, weight, first, last, sem):
     members, levels, rows, cols = ens.shape
     obs = cell.shape[-1]
     copies = [
@@ -107,21 +112,41 @@
     for l in range(levels):
         grid[0, l] = g[l * rows : (l + 1) * rows]
         grid[1, l] = d[l * rows : (l + 1) * rows]
-        up[fields + l] = g[l * rows : l * rows + HALO]
-        down[fields + l] = g[(l + 1) * rows - HALO : (l + 1) * rows]
+        up = g[l * rows : l * rows + HALO]
+        down = g[(l + 1) * rows - HALO : (l + 1) * rows]
+        near[fields + l] = by_parity("gy", down, up)
+        far[fields + l] = by_parity("gy", up, down)
     for c in copies[4:]:
         c.wait()
 
     def edge(m, _):
         for l in range(levels):
-            up[l * members + m] = first[m, l].astype(F32)[:HALO]
-            down[l * members + m] = last[m, l].astype(F32)[16 - HALO :]
+            up = first[m, l].astype(F32)[:HALO]
+            down = last[m, l].astype(F32)[16 - HALO :]
+            near[l * members + m] = by_parity("gy", down, up)
+            far[l * members + m] = by_parity("gy", up, down)
         return 0
 
     lax.fori_loop(0, members, edge, 0)
 
 
-def arrange(u, get, mains, wins, west, east, spans):
+def slot_lane(t):
+    return PAIR * (t % 2) + WIDE * (t // 2)
+
+
+def strip(xs, at, near, far):
+    lane = lanes_of(xs[0])
+    west = east = jnp.zeros_like(xs[0])
+    for t, x in enumerate(xs):
+        base = slot_lane(t)
+        here = (lane >= base) & (lane < base + WIDE)
+        west = jnp.where(here, turn(x, base), west)
+        east = jnp.where(here, turn(x, base + WIDE), east)
+    near[at] = by_parity("gx", east, west)
+    far[at] = by_parity("gx", west, east)
+
+
+def arrange(u, get, mains, wins, near, far, spans):
     xs = [get(8 * u + t) for t in range(8)]
     lane = lanes_of(xs[0])
 
@@ -131,14 +156,9 @@
             ref[f, start : start + count, :] = value[at : at + count]
             at += count
 
-    w_strip = e_strip = jnp.zeros_like(xs[0])
     for t, x in enumerate(xs):
         put(mains, 8 * u + t, x)
-        here = (lane >= WIDE * t) & (lane < WIDE * (t + 1))
-        w_strip = jnp.where(here, turn(x, WIDE * t), w_strip)
-        e_strip = jnp.where(here, turn(x, WIDE * (t + 1)), e_strip)
-    put(west, u, w_strip)
-    put(east, u, e_strip)
+    strip(xs, u, near, far)
     for v in range(4):
         win = jnp.zeros_like(xs[0])
         for q in range(2):
@@ -149,21 +169,7 @@
         put(wins, 4 * u + v, win)
 
 
-def strip_grid(fields, west, east, at, spans):
-    w_strip = e_strip = jnp.zeros_like(fields[0])
-    lane = lanes_of(w_strip)
-    for t, x in enumerate(fields):
-        here = (lane >= WIDE * t) & (lane < WIDE * (t + 1))
-        w_strip = jnp.where(here, turn(x, WIDE * t), w_strip)
-        e_strip = jnp.where(here, turn(x, WIDE * (t + 1)), e_strip)
-    row = 0
-    for start, count in spans:
-        west[at, start : start + count, :] = w_strip[row : row + count]
-        east[at, start : start + count, :] = e_strip[row : row + count]
-        row += count
-
-
-def own_kernel(ens_in, grid, bands_in, mains, wins, west, east, g_ext, mirror, bands, ens, sem):
+def own_kernel(ens_in, grid, bands_in, mains, wins, near, far, g_ext, mirror, bands, ens, sem):
     members, levels, rows, cols = ens.shape
     fields = members * levels
     gx = lax.axis_index("gx")
@@ -180,11 +186,11 @@
 
     def group(u, _):
         l = 8 * u // members
-        arrange(u, lambda f: ens[f - l * members, l].astype(F32), mains, wins, west, east, spans)
+        arrange(u, lambda f: ens[f - l * members, l].astype(F32), mains, wins, near, far, spans)
         return 0
 
     lax.fori_loop(0, fields // 8, group, 0)
-    strip_grid([grid[k, l] for k in range(2) for l in range(levels)], west, east, fields // 8, spans)
+    strip([grid[k, l] for k in range(2) for l in range(levels)], fields // 8, near, far)
     for l in range(levels):
         g_ext[l, HALO : HALO + rows, :] = grid[0, l]
     mirror[...] = jnp.zeros_like(mirror)
@@ -220,22 +226,23 @@
     pl.when(me == lax.axis_size("gy") - 1)(lambda: side(-1))
 
 
-def halo_kernel(north, south, mirror, *refs):
-    mains, wins, west, east, g_ext = refs[5:]
+def halo_kernel(from_near, from_far, mirror, *refs):
+    mains, wins, g_ext, near, far = refs[3:]
     levels, reach, cols = g_ext.shape
-    fields = north.shape[0] - levels
+    fields = mirror.shape[1] - levels
     spans = ((0, HALO), (reach - HALO, HALO))
 
     def get(f):
-        return jnp.concatenate([north[f] + mirror[0, f], south[f] + mirror[1, f]], axis=0)
+        a, b = from_near[f], from_far[f]
+        return jnp.concatenate([by_parity("gy", b, a) + mirror[0, f], by_parity("gy", a, b) + mirror[1, f]], axis=0)
 
     def group(u, _):
-        arrange(u, get, mains, wins, west, east, spans)
+        arrange(u, get, mains, wins, near, far, spans)
         return 0
 
     lax.fori_loop(0, fields // 8, group, 0)
     ends = [get(fields + l) for l in range(levels)]
-    strip_grid(ends, west, east, fields // 8, spans)
+    strip(ends, fields // 8, near, far)
     for l in range(levels):
         g_ext[l, 0:HALO, :] = ends[l][:HALO]
         g_ext[l, reach - HALO :, :] = ends[l][HALO:]
@@ -271,7 +278,7 @@
     return total + part(0, s)
 
 
-def covariance(pack, bands, kind, g, z, xacc, fbuf, prod, lhs, batch, build=None):
+def covariance(pack, bands, kind, g, z, xacc, fbuf, prod, lhs, batch, build=None, also=None):
     count, reach, _ = pack.shape
     inner, rows = reach - HALO, reach - 2 * HALO
     per_level = count // g.shape[0]
@@ -291,6 +298,8 @@
             v = combine(prod, i * reach, fbuf, i, inner)
             z[b * batch + i] = v
             split_into(lhs, i * inner, v)
+            if also is not None:
+                also(b, i, v)
         band_products(lhs, bands, kind, prod, batch * inner)
         for i in range(batch):
             v = combine(prod, i * inner, z, b * batch + i, rows)
@@ -325,23 +334,30 @@
     return jnp.where(lane < cols - HALO, state, turn(win, cols - 3 * WIDE)), win
 
 
-def first_kernel(pack_in, g_ext, grid, west, east, bands, xmain, pack, z, x, p, up, down, side, sums, gbuf, fbuf, prod, lhs, xacc, *, batch):
+def first_kernel(
+    pack_in, g_ext, grid, near, far, near_ends, far_ends, bands, xmain,
+    pack, z, x, p, near_out, far_out, side, sums,
+    gbuf, fbuf, prod, lhs, xacc, west, east, *, batch,
+):
     del pack_in
     levels, reach, cols = g_ext.shape
     rows = reach - 2 * HALO
     last = west.shape[0] - 1
+    west[:, HALO : HALO + rows, :] = by_parity("gx", far[...], near[...])
+    east[:, HALO : HALO + rows, :] = by_parity("gx", near[...], far[...])
+    for start, at in ((0, 0), (HALO + rows, HALO)):
+        a, b = near_ends[:, at : at + HALO, :], far_ends[:, at : at + HALO, :]
+        west[:, start : start + HALO, :] = by_parity("gx", b, a)
+        east[:, start : start + HALO, :] = by_parity("gx", a, b)
     for l in range(levels):
-        gbuf[l] = window_grid(g_ext[l], turn(west[last], -WIDE * l), turn(east[last], -WIDE * l))
+        gbuf[l] = window_grid(g_ext[l], turn(west[last], -slot_lane(l)), turn(east[last], -slot_lane(l)))
     lane = lax.broadcasted_iota(jnp.int32, (reach, cols), 1)
 
     def window(b, i, old):
         u = b * (batch // 4) + i // 4
-        for q in range(2):
-            slot = WIDE * (2 * (i % 4) + q)
-            at = lane - PAIR * q
-            old = jnp.where((at >= 0) & (at < WIDE), turn(west[u], PAIR * q - slot), old)
-            old = jnp.where((at >= 3 * WIDE) & (at < PAIR), turn(east[u], PAIR * q + 3 * WIDE - slot), old)
-        return old
+        at = lane & (PAIR - 1)
+        old = jnp.where(at < WIDE, turn(west[u], -WIDE * (i % 4)), old)
+        return jnp.where(at >= 3 * WIDE, turn(east[u], 3 * WIDE - WIDE * (i % 4)), old)
 
     covariance(pack, bands, 1, gbuf, z, xacc, fbuf, prod, lhs, batch, window)
     norm = jnp.zeros((8, cols), F32)
@@ -354,30 +370,35 @@
         push = grid[1, l] * state
         x[l] = state
         p[l] = push
-        up[l] = push[:HALO]
-        down[l] = push[rows - HALO :]
+        near_out[l] = by_parity("gy", push[rows - HALO :], push[:HALO])
+        far_out[l] = by_parity("gy", push[:HALO], push[rows - HALO :])
         norm += fold(grid[0, l] * state)
         curve += fold(push * state)
         base = WIDE * l
-        far = WIDE * (levels + l)
-        beside = turn(win, base - HALO) * turn(d_west, base - far - HALO)
+        mine = slot_lane(levels + l)
+        beside = turn(win, base - HALO) * turn(d_west, base - mine - HALO)
         sides = jnp.where((lane >= base) & (lane < base + HALO), beside, sides)
-        beside = turn(win, base + HALO - 3 * WIDE) * turn(d_east, base + HALO - far)
+        beside = turn(win, base + HALO - 3 * WIDE) * turn(d_east, base + HALO - mine)
         sides = jnp.where((lane >= base + HALO) & (lane < base + WIDE), beside, sides)
     side[...] = sides
-    up[levels] = sides[:HALO]
-    down[levels] = sides[rows - HALO :]
+    near_out[levels] = by_parity("gy", sides[rows - HALO :], sides[:HALO])
+    far_out[levels] = by_parity("gy", sides[:HALO], sides[rows - HALO :])
     sums[0] = norm
     sums[1] = curve
 
 
-def second_kernel(mains, wins, p, side, north, south, grid, bands, sums, zm, zw, x, share, ext, gbuf, fbuf, prod, lhs, xacc, *, batch):
+def second_kernel(
+    mains, wins, p, side, near, far, grid, bands, sums, z_one, zw_one,
+    zm, x, share, z_out,
+    ext, gbuf, fbuf, prod, lhs, xacc, zw, *, batch,
+):
+    del z_one
     levels, rows, cols = p.shape
     reach = rows + 2 * HALO
     for l in range(levels + 1):
         ext[l, HALO : HALO + rows, :] = p[l] if l < levels else side[...]
-        ext[l, 0:HALO, :] = north[l]
-        ext[l, HALO + rows :, :] = south[l]
+        ext[l, 0:HALO, :] = by_parity("gy", far[l], near[l])
+        ext[l, HALO + rows :, :] = by_parity("gy", near[l], far[l])
     me = lax.axis_index("gy")
 
     def reflect(base, step):
@@ -393,8 +414,23 @@
         west = jnp.where(lane < HALO, 0.0, turn(ext[levels], HALO - WIDE * l))
         east = jnp.where(lane < HALO, turn(ext[levels], -HALO - WIDE * l), 0.0)
         gbuf[1, l] = window_grid(ext[l], west, east)
-    covariance(mains, bands, 0, gbuf.at[0], zm, xacc.at[0], fbuf, prod, lhs, batch)
-    covariance(wins, bands, 1, gbuf.at[1], zw, xacc.at[1], fbuf, prod, lhs, batch)
+    place = lax.broadcasted_iota(jnp.int32, (rows + HALO, cols), 1)
+
+    def edges(old, win, q):
+        new = jnp.where(place < HALO, turn(win, -WIDE - PAIR * q), old)
+        return jnp.where(place < cols - HALO, new, turn(win, cols - 3 * WIDE - PAIR * q))
+
+    def first_edges(b, i, _):
+        at = b * batch + i
+        z_out[at] = edges(z_out[at], zw_one[b * (batch // 2) + i // 2], i % 2)
+
+    def second_edges(b, i, v):
+        for q in range(2):
+            at = 2 * (b * batch + i) + q
+            zm[at] = edges(zm[at], v, q)
+
+    covariance(mains, bands, 0, gbuf.at[0], zm, xacc.at[0], fbuf, prod, lhs, batch, None, first_edges)
+    covariance(wins, bands, 1, gbuf.at[1], zw, xacc.at[1], fbuf, prod, lhs, batch, None, second_edges)
     cross = jnp.zeros((8, cols), F32)
     curve = cross
     for l in range(levels):
@@ -409,10 +445,8 @@
     share[...] = jnp.broadcast_to(out, share.shape)
 
 
-def final_kernel(share, zm_one, zw_one, zm_two, zw_two, x_one, x_two, control, increment):
-    level = pl.program_id(0)
-    group = pl.program_id(1)
-    batch, _, rows, cols = control.shape
+def final_kernel(share, z_one, z_two, x_one, x_two, control, increment, stage, x_stage, sems):
+    members, levels, rows, cols = control.shape
     total = jnp.sum(share[...], axis=0, keepdims=True)
     place = lax.broadcasted_iota(jnp.int32, (1, cols), 1)
     n0, c1, c2, c3 = (jnp.sum(jnp.where(place == i, total, 0.0), axis=1, keepdims=True) for i in range(4))
@@ -425,24 +459,29 @@
     det = alpha_one * alpha_two - beta_sq
     coef_b = -1.0 / det
     coef_a = (alpha_two - t) / det
-    lane = lax.broadcasted_iota(jnp.int32, (rows, cols), 1)
-    groups = zm_one.shape[0] // x_one.shape[0] // batch
-
-    def mixed(one, two, f):
-        return coef_a * one[f, SWEEPS : SWEEPS + rows, :] + coef_b * two[f, SWEEPS : SWEEPS + rows, :]
-
-    first = (level * groups + group) * batch
-    for w in range(batch // 2):
-        win = mixed(zw_one, zw_two, first // 2 + w)
-        for q in range(2):
-            i = 2 * w + q
-            main = jnp.where(lane < HALO, turn(win, -WIDE - PAIR * q), mixed(zm_one, zm_two, first + i))
-            control[i, 0] = jnp.where(lane < cols - HALO, main, turn(win, cols - 3 * WIDE - PAIR * q))
-
-    @pl.when((level == 0) & (group == 0))
-    def _():
-        for l in range(x_one.shape[0]):
-            increment[l] = coef_a * x_one[l] + coef_b * x_two[l]
+    copies = []
+    part = stage.shape[0] // (sems.shape[0] - 1)
+    for c in range(sems.shape[0] - 1):
+
+        def body(i, _):
+            f = c * part + i
+            one, two = z_one[f, SWEEPS : SWEEPS + rows, :], z_two[f, SWEEPS : SWEEPS + rows, :]
+            stage[f] = coef_a * one + coef_b * two
+            return 0
+
+        lax.fori_loop(0, part, body, 0, unroll=4)
+        level, first = divmod(c * part, members)
+        copies.append(
+            pltpu.make_async_copy(
+                stage.at[pl.ds(c * part, part)], control.at[pl.ds(first, part), level], sems.at[c]
+            )
+        )
+        copies[-1].start()
+    x_stage[...] = coef_a * x_one[...] + coef_b * x_two[...]
+    copies.append(pltpu.make_async_copy(x_stage, increment, sems.at[sems.shape[0] - 1]))
+    copies[-1].start()
+    for copy in copies:
+        copy.wait()
 
 
 def on_device(ensemble, obs_cell, obs_level, innovation, obs_weight):
@@ -472,36 +511,36 @@
     bands = jnp.asarray(band_matrices(cols), BF16)
     obs = obs_cell.shape
     edge = pltpu.VMEM((members, levels, 16, cols), BF16)
-    grid, up, down = call(
+    grid, near, far = call(
         scatter_kernel,
         (struct(2, levels, rows, cols), struct(fields + levels, HALO, cols), struct(fields + levels, HALO, cols)),
         [hbm] * 5,
         [pltpu.VMEM(obs, jnp.int32)] * 2 + [pltpu.VMEM(obs, F32)] * 2 + [edge, edge, pltpu.SemaphoreType.DMA((6,))],
         limit=60,
     )(ensemble, obs_cell, obs_level, innovation, obs_weight)
-    north, south = shift(down, "gy", 1), shift(up, "gy", -1)
+    near, far = swap(near, "gy", 0), swap(far, "gy", 1)
     main_shape, win_shape = struct(fields, reach, cols), struct(fields // 2, reach, cols)
-    laid = (
-        main_shape,
-        win_shape,
-        struct(strips, reach, cols),
-        struct(strips, reach, cols),
-        struct(levels, reach, cols),
-    )
-    *own, mirror, bands = call(
+    g_shape = struct(levels, reach, cols)
+    own_shape, end_shape = struct(strips, rows, cols), struct(strips, 2 * HALO, cols)
+    mains, wins, near_own, far_own, g_ext, mirror, bands = call(
         own_kernel,
         (
-            *laid,
+            main_shape,
+            win_shape,
+            own_shape,
+            own_shape,
+            g_shape,
             struct(2, fields + levels, HALO, cols),
             jax.ShapeDtypeStruct((2, 2 * cols, SWEEPS * cols), BF16),
         ),
         [hbm, VMEM, hbm],
         [pltpu.VMEM(ensemble.shape, BF16), pltpu.SemaphoreType.DMA((3,))],
     )(ensemble, grid, bands)
-    mains, wins, west, east, g_ext = call(halo_kernel, laid, 8, input_output_aliases={3 + i: i for i in range(5)})(
-        north, south, mirror, *own
-    )
-    from_west, from_east = shift(east, "gx", 1), shift(west, "gx", -1)
+    near_own, far_own = swap(near_own, "gx", 0), swap(far_own, "gx", 1)
+    mains, wins, g_ext, near, far = call(
+        halo_kernel, (main_shape, win_shape, g_shape, end_shape, end_shape), 6, input_output_aliases={3: 0, 4: 1, 5: 2}
+    )(near, far, mirror, mains, wins, g_ext)
+    near, far = swap(near, "gx", 0), swap(far, "gx", 1)
     work = (
         pltpu.VMEM((batch, reach, cols), F32),
         pltpu.VMEM((SWEEPS, batch * reach, cols), F32),
@@ -512,7 +551,7 @@
     zm_one, xmain = call(
         functools.partial(main_kernel, batch=batch), (zm_shape, struct(levels, rows, cols)), 3, (gbuf, *work)
     )(mains, g_ext, bands)
-    wins, zw_one, x_one, p, up, down, side, sums = call(
+    wins, zw_one, x_one, p, near, far, side, sums = call(
         functools.partial(first_kernel, batch=batch),
         (
             win_shape,
@@ -524,34 +563,38 @@
             struct(rows, cols),
             struct(2, 8, cols),
         ),
-        7,
-        (gbuf, *work, pltpu.VMEM((levels, rows, cols), F32)),
+        9,
+        (gbuf, *work, pltpu.VMEM((levels, rows, cols), F32), *[pltpu.VMEM((strips, reach, cols), F32)] * 2),
         input_output_aliases={0: 0},
-    )(wins, g_ext, grid, from_west, from_east, bands, xmain)
-    north, south = shift(down, "gy", 1), shift(up, "gy", -1)
-    zm_two, zw_two, x_two, share = call(
+    )(wins, g_ext, grid, near_own, far_own, near, far, bands, xmain)
+    near, far = swap(near, "gy", 0), swap(far, "gy", 1)
+    zm_two, x_two, share, zm_one = call(
         functools.partial(second_kernel, batch=batch),
-        (zm_shape, zw_shape, struct(levels, rows, cols), struct(devices, cols)),
-        9,
+        (zm_shape, struct(levels, rows, cols), struct(devices, cols), zm_shape),
+        11,
         (
             pltpu.VMEM((levels + 1, reach, cols), F32),
             pltpu.VMEM((2, levels, reach, cols), F32),
             *work,
             pltpu.VMEM((2, levels, rows, cols), F32),
+            pltpu.VMEM((fields // 2, reach - HALO, cols), F32),
         ),
-    )(mains, wins, p, side, north, south, grid, bands, sums)
+        input_output_aliases={9: 3},
+    )(mains, wins, p, side, near, far, grid, bands, sums, zm_one, zw_one)
     share = lax.all_to_all(share, ("gy", "gx"), 0, 0, tiled=True)
+    chunks = 8
     return pl.pallas_call(
         final_kernel,
-        grid=(levels, members // batch),
         out_shape=(struct(members, levels, rows, cols), struct(levels, rows, cols)),
-        in_specs=[VMEM] * 7,
-        out_specs=(
-            pl.BlockSpec((batch, 1, rows, cols), lambda l, g: (g, l, 0, 0)),
-            pl.BlockSpec((levels, rows, cols), lambda l, g: (0, 0, 0)),
-        ),
-        compiler_params=pltpu.CompilerParams(vmem_limit_bytes=32 * 2**20),
-    )(share, zm_one, zw_one, zm_two, zw_two, x_one, x_two)
+        in_specs=[VMEM] * 5,
+        out_specs=(hbm, hbm),
+        scratch_shapes=[
+            pltpu.VMEM((fields, rows, cols), F32),
+            pltpu.VMEM((levels, rows, cols), F32),
+            pltpu.SemaphoreType.DMA((chunks + 1,)),
+        ],
+        compiler_params=pltpu.CompilerParams(vmem_limit_bytes=16 * 2**20),
+    )(share, zm_one, zm_two, x_one, x_two)
 
 
 def solution(mesh):

time: 69.3 us -> 58.7 us (0.85)
  starting transfers between devices: 14.3 us -> 8.2 us
  waiting for transfers between devices: 12.9 us -> 8.58 us
  Pallas kernels: 24.1 us -> 22.4 us
  blocking collectives: 16 us -> 17.5 us
    ppermute x6 -> x8, starting transfers between devices: 14.3 us -> 8.2 us  [swap(): lax.ppermute(x, axis, [(i + a, i + 1 - a) for i in range(odd, count - 1,...]
    ppermute x6 -> x8, waiting for transfers between devices: 12.9 us -> 8.58 us  [swap(): lax.ppermute(x, axis, [(i + a, i + 1 - a) for i in range(odd, count - 1,...]
    all_to_all x1, blocking collectives: 16 us -> 17.5 us  [on_device(): share = lax.all_to_all(share, ('gy', 'gx'), 0, 0, tiled=True)]
    pallas_call x4, Pallas kernels: 13.4 us -> 12.3 us  [the longest x1 7.74 us: on_device(): call(functools.partial(second_kernel, batch=batch), (zm_shape, struct(lev...]
  transfers between devices with their start and end apart: 6 -> 8, of which waited for: 3 -> 2; matrix products, arithmetic and copies ran while one was open for 0% -> 0% of each run, Pallas kernels for 9% -> 13%
where the time goes in v3:
time: 58.7 us; the launch traced here: 58.4 us
  Pallas kernels  22.4 us (38%)
  blocking collectives  17.5 us (30%)
  waiting for transfers between devices  8.58 us (15%)
  starting transfers between devices  8.2 us (14%)
  local copies, waits for them, and re-layouts  0.91 us (2%)
  between operations  0.78 us (1%)
    all_to_all x1, blocking collectives, on_device(): share = lax.all_to_all(share, ('gy', 'gx'), 0, 0, tiled=True)  17.5 us
    ppermute x8, waiting for transfers between devices, swap(): lax.ppermute(x, axis, [(i + a, i + 1 - a) for i in range(odd, count - 1,...  8.58 us
    ppermute x8, starting transfers between devices, swap(): lax.ppermute(x, axis, [(i + a, i + 1 - a) for i in range(odd, count - 1,...  8.2 us
    pallas_call x1, Pallas kernels, on_device(): call(functools.partial(second_kernel, batch=batch), (zm_shape, struct(lev...  7.74 us
    pallas_call x1, Pallas kernels, on_device(): call(functools.partial(main_kernel, batch=batch), (zm_shape, struct(level...  4.51 us
    pallas_call x1, Pallas kernels, on_device(): call(functools.partial(first_kernel, batch=batch), (win_shape, zw_shape,...  2.91 us
    pallas_call x1, Pallas kernels, on_device(): call(scatter_kernel, (struct(2, levels, rows, cols), struct(fields + leve...  2.72 us
    pallas_call x1, Pallas kernels, on_device(): call(own_kernel, (main_shape, win_shape, own_shape, own_shape, g_shape, s...  1.92 us
  transfers between devices with their start and end apart: 8, of which 2 were waited for; matrix products, arithmetic and copies ran while one was open for 0% of the time, Pallas kernels for 13%

profile of v3, /device:TPU:0, one launch (start us, length us, event | category | flops | bytes accessed | tf_op | source)
XLA Modules:
  0.0 58.4 jit_solution(2361802492112404681)
XLA Ops:
  0.6 0.0 copy-start.2
  0.6 0.0 copy-start.1
  0.7 2.7 %shard_map.77 = (f32[2,2,64,128]{3,2,1,0:T(8,128)}, f32[66,8,128]{2,1,0:T(8,128)}, f32[66,8,128]{2,1,0:T(8,128)}) custom-call(bf16[32,2,64,128]{3,2,1,0:T(8,128)(2,1)} %ens_in.1, s32[1,1,2048]{2,1,0:T(1,128)} %cell_in.1, s32[1,1,2048]{2,1,0:T(1,128)} %level_in.1, f32[1,1,2048]{2,1,0:T(1,128)} %innov_in.1, f32[1,1,2048]{2,1,0:T(1,128)} %weight_in.1), custom_call_target="tpu_custom_call" | custom-call | flops 2000000000 | bytes 1000000 | tf_op jit(solution)/shard_map/pallas_call | solution.py:514
  3.4 3.0 %collective-permute-start = (f32[66,8,128]{2,1,0:T(8,128)}, f32[66,8,128]{2,1,0:T(8,128)S(1)}, u32[]{:S(2)}, u32[]{:S(2)}) collective-permute-start(f32[66,8,128]{2,1,0:T(8,128)} %get-tuple-element.31), channel_id=1, source_target_pairs={{0,4},{4,0},{8,12},{12,8},{16,20},{20,16},{24,28},{28,24},{1,5},{5... | collective-permute-start | bytes 811016 | tf_op jit(solution)/shard_map/ppermute | solution.py:55
  6.4 0.7 %collective-permute-start.1 = (f32[66,8,128]{2,1,0:T(8,128)}, f32[66,8,128]{2,1,0:T(8,128)S(1)}, u32[]{:S(2)}, u32[]{:S(2)}) collective-permute-start(f32[66,8,128]{2,1,0:T(8,128)} %get-tuple-element.32), channel_id=1, source_target_pairs={{4,8},{8,4},{12,16},{16,12},{20,24},{24,20},{5,9},{9,5},{13,17},{1... | collective-permute-start | bytes 811016 | tf_op jit(solution)/shard_map/ppermute | solution.py:55
  7.1 0.0 copy-done.2
  7.1 0.0 copy-done.1
  7.1 0.0 copy-start
  7.1 0.9 %copy-done = f32[2,2,64,128]{3,2,1,0:T(8,128)S(1)} copy-done((f32[2,2,64,128]{3,2,1,0:T(8,128)S(1)}, f32[2,2,64,128]{3,2,1,0:T(8,128)}, u32[]{:S(2)}) %copy-start) | copy-done | bytes 131096
  8.0 1.9 %shard_map.78 = (f32[64,80,128]{2,1,0:T(8,128)S(1)}, f32[32,80,128]{2,1,0:T(8,128)S(1)}, f32[9,64,128]{2,1,0:T(8,128)S(1)}, f32[9,64,128]{2,1,0:T(8,128)S(1)}, f...) custom-call(bf16[32,2,64,128]{3,2,1,0:T(8,128)(2,1)S(1)} %copy-done.1, ...), custom_call_target="tpu_custom_call" | custom-call | flops 2000000000 | bytes 1000000 | tf_op jit(solution)/shard_map/pallas_call | solution.py:525
  9.9 0.1 collective-permute-start.2
  10.0 0.7 %collective-permute-start.3 = (f32[9,64,128]{2,1,0:T(8,128)S(1)}, f32[9,64,128]{2,1,0:T(8,128)S(1)}, u32[]{:S(2)}, u32[]{:S(2)}) collective-permute-start(f32[9,64,128]{2,1,0:T(8,128)S(1)} %get-tuple-element.42), channel_id=1, source_target_pairs={{1,2},{2,1},{5,6},{6,5},{9,10},{10,9},{13,14},{14,13},{17,18},{18,... | collective-permute-start | bytes 884744 | tf_op jit(solution)/shard_map/ppermute | solution.py:55
  10.7 7.6 %collective-permute-done.from_near = f32[66,8,128]{2,1,0:T(8,128)S(1)} collective-permute-done((f32[66,8,128]{2,1,0:T(8,128)}, f32[66,8,128]{2,1,0:T(8,128)S(1)}, u32[]{:S(2)}, u32[]{:S(2)}) %collective-permute-start) | collective-permute-done | bytes 270368 | tf_op jit(solution)/shard_map/ppermute | solution.py:55
  18.3 0.0 collective-permute-done.1.from_far
  18.3 1.1 %shard_map.79 = (f32[64,80,128]{2,1,0:T(8,128)S(1)}, f32[32,80,128]{2,1,0:T(8,128)S(1)}, f32[2,80,128]{2,1,0:T(8,128)S(1)}, f32[9,16,128]{2,1,0:T(8,128)S(1)}, f32[9,16,128]{2,1,0:T(8,128)S(1)}) custom-call(f32[66,8,128]{2,1,0:T(8,128)S(1)} %collective-permute-done.from_near, ...), custom_call_target="tpu_custom_call", output_to_operand_aliasing={{0}: (3, {}), {1}: (4, {}), {2}: (5, {})} | custom-call | flops 2000000000 | bytes 1000000 | tf_op jit(solution)/shard_map/pallas_call | solution.py:540
  19.3 0.0 collective-permute-start.4
  19.3 0.7 %collective-permute-start.5 = (f32[9,16,128]{2,1,0:T(8,128)S(1)}, f32[9,16,128]{2,1,0:T(8,128)S(1)}, u32[]{:S(2)}, u32[]{:S(2)}) collective-permute-start(f32[9,16,128]{2,1,0:T(8,128)S(1)} %get-tuple-element.44), channel_id=1, source_target_pairs={{1,2},{2,1},{5,6},{6,5},{9,10},{10,9},{13,14},{14,13},{17,18},{18,... | collective-permute-start | bytes 221192 | tf_op jit(solution)/shard_map/ppermute | solution.py:55
  20.0 4.5 %shard_map.80 = (f32[64,72,128]{2,1,0:T(8,128)S(1)}, f32[2,64,128]{2,1,0:T(8,128)S(1)}) custom-call(f32[64,80,128]{2,1,0:T(8,128)S(1)} %get-tuple-element.38.pack.mains, f32[2,80,128]{2,1,0:T(8,128)S(1)} %get-tuple-element.40.g_ext, bf16[2,256,512]{2,1,0:T(8,128)(2,1)S(1)} %get-tuple-element.45.bands), custom_call_target="tpu_custom_call" | custom-call | flops 2000000000 | bytes 1000000 | tf_op jit(solution)/shard_map/pallas_call | solution.py:551
  24.5 0.0 collective-permute-done.2.near
  24.5 0.0 collective-permute-done.3.far
  24.6 0.0 collective-permute-done.4.near_ends
  24.6 0.0 collective-permute-done.5.far_ends
  24.6 2.9 %shard_map.81 = (f32[32,80,128]{2,1,0:T(8,128)S(1)}, f32[32,72,128]{2,1,0:T(8,128)S(1)}, f32[2,64,128]{2,1,0:T(8,128)S(1)}, f32[2,64,128]{2,1,0:T(8,128)S(1)}, f...) custom-call(f32[32,80,128]{2,1,0:T(8,128)S(1)} %get-tuple-element.39, ...), custom_call_target="tpu_custom_call", output_to_operand_aliasing={{0}: (0, {})} | custom-call | flops 2000000000 | bytes 1000000 | tf_op jit(solution)/shard_map/pallas_call | solution.py:554
  27.5 2.4 %collective-permute-start.6 = (f32[3,8,128]{2,1,0:T(8,128)S(1)}, f32[3,8,128]{2,1,0:T(8,128)S(1)}, u32[]{:S(2)}, u32[]{:S(2)}) collective-permute-start(f32[3,8,128]{2,1,0:T(8,128)S(1)} %get-tuple-element.50), channel_id=1, source_target_pairs={{0,4},{4,0},{8,12},{12,8},{16,20},{20,16},{24,28},{28,24},{1,5},{5... | collective-permute-start | bytes 36872 | tf_op jit(solution)/shard_map/ppermute | solution.py:55
  29.9 0.7 %collective-permute-start.7 = (f32[3,8,128]{2,1,0:T(8,128)S(1)}, f32[3,8,128]{2,1,0:T(8,128)S(1)}, u32[]{:S(2)}, u32[]{:S(2)}) collective-permute-start(f32[3,8,128]{2,1,0:T(8,128)S(1)} %get-tuple-element.51), channel_id=1, source_target_pairs={{4,8},{8,4},{12,16},{16,12},{20,24},{24,20},{5,9},{9,5},{13,17},{1... | collective-permute-start | bytes 36872 | tf_op jit(solution)/shard_map/ppermute | solution.py:55
  30.6 1.0 %collective-permute-done.6.near = f32[3,8,128]{2,1,0:T(8,128)S(1)} collective-permute-done((f32[3,8,128]{2,1,0:T(8,128)S(1)}, f32[3,8,128]{2,1,0:T(8,128)S(1)}, u32[]{:S(2)}, u32[]{:S(2)}) %collective-permute-start.6) | collective-permute-done | bytes 12320 | tf_op jit(solution)/shard_map/ppermute | solution.py:55
  31.6 0.0 collective-permute-done.7.far
  31.6 7.7 %shard_map.82 = (f32[64,72,128]{2,1,0:T(8,128)S(1)}, f32[2,64,128]{2,1,0:T(8,128)S(1)}, f32[32,128]{1,0:T(8,128)S(1)}, f32[64,72,128]{2,1,0:T(8,128)S(1)}) custom-call(f32[64,80,128]{2,1,0:T(8,128)S(1)} %get-tuple-element.38.pack.mains, f32[32,80,128]{2,1,0:T(8,128)S(1)} %get-tuple-element.47.wins, ...), custom_call_target="tpu_custom_call", output_to_operand_aliasing={{3}: (9, {})} | custom-call | flops 2000000000 | bytes 1000000 | tf_op jit(solution)/shard_map/pallas_call | solution.py:571
  39.3 17.5 %all_to_all.11 = f32[32,1,128]{2,1,0:T(1,128)S(1)} all-to-all(f32[32,1,128]{2,1,0:T(1,128)S(1)} %bitcast.5), channel_id=1, replica_groups=mesh['gy'=8,'gx'=4] {'gy','gx'}, dimensions={0} | all-to-all | bytes 32768 | tf_op jit(solution)/shard_map/all_to_all | solution.py:584
  56.9 1.5 %shard_map.83 = (f32[32,2,64,128]{3,2,1,0:T(8,128)}, f32[2,64,128]{2,1,0:T(8,128)}) custom-call(f32[32,128]{1,0:T(8,128)S(1)} %bitcast.4, f32[64,72,128]{2,1,0:T(8,128)S(1)} %get-tuple-element.56.z_one, f32[64,72,128]{2,1,0:T(8,128)S(1)} %get-tuple-element.57.z_two, f32[2,64,128]{2,1,0:T(8,128)S(1)} %get-tuple-element.58.x_one, ...), custom_call_target="tpu_custom_call" | custom-call | tf_op jit(solution)/shard_map/pallas_call | solution.py:586
Async XLA Ops:
  0.6 6.5 %copy-start.2 = (bf16[4,2,128,512]{3,2,1,0:T(8,128)(2,1)S(1)}, bf16[4,2,128,512]{3,2,1,0:T(8,128)(2,1)}, u32[]{:S(2)}) copy-start(bf16[4,2,128,512]{3,2,1,0:T(8,128)(2,1)} %constant.2.clone.bands_in) | copy-start | bytes 3145732
  0.6 6.5 %copy-start.1 = (bf16[32,2,64,128]{3,2,1,0:T(8,128)(2,1)S(1)}, bf16[32,2,64,128]{3,2,1,0:T(8,128)(2,1)}, u32[]{:S(2)}) copy-start(bf16[32,2,64,128]{3,2,1,0:T(8,128)(2,1)} %ens_in.1) | copy-start | bytes 3145732
  3.4 14.9 %collective-permute-start = (f32[66,8,128]{2,1,0:T(8,128)}, f32[66,8,128]{2,1,0:T(8,128)S(1)}, u32[]{:S(2)}, u32[]{:S(2)}) collective-permute-start(f32[66,8,128]{2,1,0:T(8,128)} %get-tuple-element.31), channel_id=1, source_target_pairs={{0,4},{4,0},{8,12},{12,8},{16,20},{20,16},{24,28},{28,24},{1,5},{5... | collective-permute-start | bytes 811016 | tf_op jit(solution)/shard_map/ppermute | solution.py:55
  6.4 11.9 %collective-permute-start.1 = (f32[66,8,128]{2,1,0:T(8,128)}, f32[66,8,128]{2,1,0:T(8,128)S(1)}, u32[]{:S(2)}, u32[]{:S(2)}) collective-permute-start(f32[66,8,128]{2,1,0:T(8,128)} %get-tuple-element.32), channel_id=1, source_target_pairs={{4,8},{8,4},{12,16},{16,12},{20,24},{24,20},{5,9},{9,5},{13,17},{1... | collective-permute-start | bytes 811016 | tf_op jit(solution)/shard_map/ppermute | solution.py:55
  7.1 0.9 %copy-start = (f32[2,2,64,128]{3,2,1,0:T(8,128)S(1)}, f32[2,2,64,128]{3,2,1,0:T(8,128)}, u32[]{:S(2)}) copy-start(f32[2,2,64,128]{3,2,1,0:T(8,128)} %get-tuple-element.33.grid) | copy-start | bytes 393220
  9.9 14.6 %collective-permute-start.2 = (f32[9,64,128]{2,1,0:T(8,128)S(1)}, f32[9,64,128]{2,1,0:T(8,128)S(1)}, u32[]{:S(2)}, u32[]{:S(2)}) collective-permute-start(f32[9,64,128]{2,1,0:T(8,128)S(1)} %get-tuple-element.41), channel_id=1, source_target_pairs={{0,1},{1,0},{2,3},{3,2},{4,5},{5,4},{6,7},{7,6},{8,9},{9,8},{10,11... | collective-permute-start | bytes 884744 | tf_op jit(solution)/shard_map/ppermute | solution.py:55
  10.0 14.5 %collective-permute-start.3 = (f32[9,64,128]{2,1,0:T(8,128)S(1)}, f32[9,64,128]{2,1,0:T(8,128)S(1)}, u32[]{:S(2)}, u32[]{:S(2)}) collective-permute-start(f32[9,64,128]{2,1,0:T(8,128)S(1)} %get-tuple-element.42), channel_id=1, source_target_pairs={{1,2},{2,1},{5,6},{6,5},{9,10},{10,9},{13,14},{14,13},{17,18},{18,... | collective-permute-start | bytes 884744 | tf_op jit(solution)/shard_map/ppermute | solution.py:55
  19.3 5.2 %collective-permute-start.4 = (f32[9,16,128]{2,1,0:T(8,128)S(1)}, f32[9,16,128]{2,1,0:T(8,128)S(1)}, u32[]{:S(2)}, u32[]{:S(2)}) collective-permute-start(f32[9,16,128]{2,1,0:T(8,128)S(1)} %get-tuple-element.43), channel_id=1, source_target_pairs={{0,1},{1,0},{2,3},{3,2},{4,5},{5,4},{6,7},{7,6},{8,9},{9,8},{10,11... | collective-permute-start | bytes 221192 | tf_op jit(solution)/shard_map/ppermute | solution.py:55
  19.3 5.2 %collective-permute-start.5 = (f32[9,16,128]{2,1,0:T(8,128)S(1)}, f32[9,16,128]{2,1,0:T(8,128)S(1)}, u32[]{:S(2)}, u32[]{:S(2)}) collective-permute-start(f32[9,16,128]{2,1,0:T(8,128)S(1)} %get-tuple-element.44), channel_id=1, source_target_pairs={{1,2},{2,1},{5,6},{6,5},{9,10},{10,9},{13,14},{14,13},{17,18},{18,... | collective-permute-start | bytes 221192 | tf_op jit(solution)/shard_map/ppermute | solution.py:55
  27.5 4.1 %collective-permute-start.6 = (f32[3,8,128]{2,1,0:T(8,128)S(1)}, f32[3,8,128]{2,1,0:T(8,128)S(1)}, u32[]{:S(2)}, u32[]{:S(2)}) collective-permute-start(f32[3,8,128]{2,1,0:T(8,128)S(1)} %get-tuple-element.50), channel_id=1, source_target_pairs={{0,4},{4,0},{8,12},{12,8},{16,20},{20,16},{24,28},{28,24},{1,5},{5... | collective-permute-start | bytes 36872 | tf_op jit(solution)/shard_map/ppermute | solution.py:55
  29.9 1.7 %collective-permute-start.7 = (f32[3,8,128]{2,1,0:T(8,128)S(1)}, f32[3,8,128]{2,1,0:T(8,128)S(1)}, u32[]{:S(2)}, u32[]{:S(2)}) collective-permute-start(f32[3,8,128]{2,1,0:T(8,128)S(1)} %get-tuple-element.51), channel_id=1, source_target_pairs={{4,8},{8,4},{12,16},{16,12},{20,24},{24,20},{5,9},{9,5},{13,17},{1... | collective-permute-start | bytes 36872 | tf_op jit(solution)/shard_map/ppermute | solution.py:55

commit v4 on v3

--- a/solution.py
+++ b/solution.py
@@ -227,7 +227,7 @@
 
 
 def halo_kernel(from_near, from_far, mirror, *refs):
-    mains, wins, g_ext, near, far = refs[3:]
+    mains, wins, g_ext, near, far = refs[4:]
     levels, reach, cols = g_ext.shape
     fields = mirror.shape[1] - levels
     spans = ((0, HALO), (reach - HALO, HALO))
@@ -267,15 +267,101 @@
     lhs[start : start + count, lanes : 2 * lanes] = (x - high.astype(F32)).astype(BF16)
 
 
-def combine(prod, start, src, f, count):
-    def part(k, off):
-        return prod[k, pl.ds(start + off, count), :]
-
-    s = SWEEPS
-    total = src[f, pl.ds(2 * s, count), :] + src[f, pl.ds(0, count), :]
-    for k in range(1, s):
-        total += part(k, s + k) + part(k, s - k)
-    return total + part(0, s)
+def combine(part, src, count):
+    total = src(2 * SWEEPS) + src(0)
+    for k in range(1, SWEEPS):
+        total += part(k, SWEEPS + k) + part(k, SWEEPS - k)
+    return total + part(0, SWEEPS)
+
+
+def rows_of(prod, start, count):
+    return lambda k, off: prod[k, pl.ds(start + off, count), :]
+
+
+def field_rows(ref, f, count, base=0):
+    return lambda off: ref[f, pl.ds(base + off, count), :]
+
+
+def interior(pack, g, bands, z, first_edge, second_edge, xacc, fbuf, prod, lhs, batch, also):
+    count, reach, _ = pack.shape
+    rows = reach - 2 * HALO
+    mid, core = rows - HALO, rows - 2 * HALO
+    per_level = count // g.shape[0]
+    xacc[...] = jnp.zeros_like(xacc)
+
+    def keep(edge, at, start, size):
+        for k in range(SWEEPS):
+            edge[k, at, HALO : 2 * HALO, :] = prod[k, start : start + HALO, :]
+            edge[k, count + at, 0:HALO, :] = prod[k, start + size - HALO : start + size, :]
+
+    def step(b, _):
+        level = b * batch // per_level
+        for i in range(batch):
+            f = pack[b * batch + i, HALO : HALO + rows, :] * g[level]
+            fbuf[i, 0:rows, :] = f
+            split_into(lhs, i * rows, f)
+        band_products(lhs, bands, 0, prod, batch * rows)
+        for i in range(batch):
+            at = b * batch + i
+            v = combine(rows_of(prod, i * rows, mid), field_rows(fbuf, i, mid), mid)
+            z[at, HALO : HALO + mid, :] = v
+            keep(first_edge, at, i * rows, rows)
+            split_into(lhs, i * mid, v)
+            if also is not None:
+                also(b, i)
+        band_products(lhs, bands, 0, prod, batch * mid)
+        for i in range(batch):
+            at = b * batch + i
+            v = combine(rows_of(prod, i * mid, core), field_rows(z, at, core, HALO), core)
+            keep(second_edge, at, i * mid, mid)
+            xacc[level, HALO : HALO + core, :] += v * pack[at, 2 * HALO : 2 * HALO + core, :]
+        return 0
+
+    lax.fori_loop(0, count // batch, step, 0)
+
+
+def edge_rows(pack, g, bands, z, first_edge, second_edge, xacc, ends, lhs):
+    count, reach, lanes = pack.shape
+    rows = reach - 2 * HALO
+    per_level = count // g.shape[0]
+    sides = [(side, f) for side in range(2) for f in range(count)]
+
+    def products(edge):
+        for half in range(SWEEPS // 2):
+            r = jnp.dot(
+                lhs[0 : 2 * count * HALO, :],
+                bands[0, :, half * 2 * lanes : (half + 1) * 2 * lanes],
+                preferred_element_type=F32,
+            )
+            for t in range(2):
+                part = r[:, t * lanes : (t + 1) * lanes].reshape(2 * count, HALO, lanes)
+                edge[2 * half + t, 0:count, 0:HALO, :] = part[:count]
+                edge[2 * half + t, count:, HALO : 2 * HALO, :] = part[count:]
+
+    def near(edge, j):
+        return lambda k, off: edge[k, j, pl.ds(off, HALO), :]
+
+    for side, f in sides:
+        base = side * rows
+        x = pack[f, base : base + 2 * HALO, :] * g[f // per_level, base : base + 2 * HALO, :]
+        j = side * count + f
+        ends[j] = x
+        split_into(lhs, j * HALO, x[side * HALO : (side + 1) * HALO])
+    products(first_edge)
+    for side, f in sides:
+        j = side * count + f
+        v = combine(near(first_edge, j), field_rows(ends, j, HALO), HALO)
+        z[f, side * rows : side * rows + HALO, :] = v
+        split_into(lhs, j * HALO, v)
+    products(second_edge)
+    for side in range(2):
+        for level in range(g.shape[0]):
+            total = jnp.zeros((HALO, lanes), F32)
+            for f in range(level * per_level, (level + 1) * per_level):
+                base = side * (rows - HALO)
+                v = combine(near(second_edge, side * count + f), field_rows(z, f, HALO, base), HALO)
+                total += v * pack[f, HALO + base : 2 * HALO + base, :]
+            xacc[level, base : base + HALO, :] = total
 
 
 def covariance(pack, bands, kind, g, z, xacc, fbuf, prod, lhs, batch, build=None, also=None):
@@ -295,14 +381,14 @@
             split_into(lhs, i * reach, f)
         band_products(lhs, bands, kind, prod, batch * reach)
         for i in range(batch):
-            v = combine(prod, i * reach, fbuf, i, inner)
+            v = combine(rows_of(prod, i * reach, inner), field_rows(fbuf, i, inner), inner)
             z[b * batch + i] = v
             split_into(lhs, i * inner, v)
             if also is not None:
                 also(b, i, v)
         band_products(lhs, bands, kind, prod, batch * inner)
         for i in range(batch):
-            v = combine(prod, i * inner, z, b * batch + i, rows)
+            v = combine(rows_of(prod, i * inner, rows), field_rows(z, b * batch + i, rows), rows)
             xacc[level] += v * pack[b * batch + i, HALO : HALO + rows, :]
         return 0
 
@@ -322,9 +408,37 @@
     return jnp.sum(x.reshape(x.shape[0] // 8, 8, x.shape[1]), axis=0)
 
 
-def main_kernel(pack, g_ext, bands, z, xacc, gbuf, fbuf, prod, lhs, *, batch):
+def interior_kernel(pack, g, bands, z, first_edge, second_edge, xacc, gbuf, fbuf, prod, lhs, *, batch):
+    gbuf[...] = g[0] * KAPPA**SWEEPS
+    interior(pack, gbuf, bands, z, first_edge, second_edge, xacc, fbuf, prod, lhs, batch, None)
+
+
+def edge_kernel(pack, g_ext, bands, *refs):
+    z, first_edge, second_edge, xacc, gbuf, ends, lhs = refs[4:]
     gbuf[...] = g_ext[...] * KAPPA**SWEEPS
-    covariance(pack, bands, 0, gbuf, z, xacc, fbuf, prod, lhs, batch)
+    edge_rows(pack, gbuf, bands, z, first_edge, second_edge, xacc, ends, lhs)
+
+
+def put_edges(old, win, q):
+    lane = lanes_of(old)
+    cols = old.shape[1]
+    new = jnp.where(lane < HALO, turn(win, -WIDE - PAIR * q), old)
+    return jnp.where(lane < cols - HALO, new, turn(win, cols - 3 * WIDE - PAIR * q))
+
+
+def second_interior_kernel(
+    pack, p, bands, z_one, zw_one,
+    z, first_edge, second_edge, xacc, z_out,
+    gbuf, fbuf, prod, lhs, *, batch,
+):
+    del z_one
+    gbuf[...] = p[...] * KAPPA**SWEEPS
+
+    def first_edges(b, i):
+        at = b * batch + i
+        z_out[at] = put_edges(z_out[at], zw_one[b * (batch // 2) + i // 2], i % 2)
+
+    interior(pack, gbuf, bands, z, first_edge, second_edge, xacc, fbuf, prod, lhs, batch, first_edges)
 
 
 def join(main, win, cols):
@@ -388,11 +502,11 @@
 
 
 def second_kernel(
-    mains, wins, p, side, near, far, grid, bands, sums, z_one, zw_one,
-    zm, x, share, z_out,
-    ext, gbuf, fbuf, prod, lhs, xacc, zw, *, batch,
+    mains, wins, p, side, near, far, grid, bands, sums, z_in, first_in, second_in, xmain_in,
+    x, share, zm, first_edge, second_edge, xmain,
+    ext, gbuf, fbuf, prod, lhs, xacc, zw, ends, *, batch,
 ):
-    del z_one
+    del z_in, first_in, second_in, xmain_in
     levels, rows, cols = p.shape
     reach = rows + 2 * HALO
     for l in range(levels + 1):
@@ -414,27 +528,18 @@
         west = jnp.where(lane < HALO, 0.0, turn(ext[levels], HALO - WIDE * l))
         east = jnp.where(lane < HALO, turn(ext[levels], -HALO - WIDE * l), 0.0)
         gbuf[1, l] = window_grid(ext[l], west, east)
-    place = lax.broadcasted_iota(jnp.int32, (rows + HALO, cols), 1)
-
-    def edges(old, win, q):
-        new = jnp.where(place < HALO, turn(win, -WIDE - PAIR * q), old)
-        return jnp.where(place < cols - HALO, new, turn(win, cols - 3 * WIDE - PAIR * q))
-
-    def first_edges(b, i, _):
-        at = b * batch + i
-        z_out[at] = edges(z_out[at], zw_one[b * (batch // 2) + i // 2], i % 2)
 
     def second_edges(b, i, v):
         for q in range(2):
             at = 2 * (b * batch + i) + q
-            zm[at] = edges(zm[at], v, q)
-
-    covariance(mains, bands, 0, gbuf.at[0], zm, xacc.at[0], fbuf, prod, lhs, batch, None, first_edges)
-    covariance(wins, bands, 1, gbuf.at[1], zw, xacc.at[1], fbuf, prod, lhs, batch, None, second_edges)
+            zm[at] = put_edges(zm[at], v, q)
+
+    edge_rows(mains, gbuf.at[0], bands, zm, first_edge, second_edge, xmain, ends, lhs)
+    covariance(wins, bands, 1, gbuf.at[1], zw, xacc, fbuf, prod, lhs, batch, None, second_edges)
     cross = jnp.zeros((8, cols), F32)
     curve = cross
     for l in range(levels):
-        state, _ = join(xacc[0, l], xacc[1, l], cols)
+        state, _ = join(xmain[l], xacc[l], cols)
         x[l] = state
         cross += fold(p[l] * state)
         curve += fold(grid[1, l] * state * state)
@@ -537,20 +642,30 @@
         [pltpu.VMEM(ensemble.shape, BF16), pltpu.SemaphoreType.DMA((3,))],
     )(ensemble, grid, bands)
     near_own, far_own = swap(near_own, "gx", 0), swap(far_own, "gx", 1)
-    mains, wins, g_ext, near, far = call(
-        halo_kernel, (main_shape, win_shape, g_shape, end_shape, end_shape), 6, input_output_aliases={3: 0, 4: 1, 5: 2}
-    )(near, far, mirror, mains, wins, g_ext)
-    near, far = swap(near, "gx", 0), swap(far, "gx", 1)
     work = (
         pltpu.VMEM((batch, reach, cols), F32),
         pltpu.VMEM((SWEEPS, batch * reach, cols), F32),
         pltpu.VMEM((batch * reach, 2 * cols), BF16),
     )
+    zm_shape, zw_shape = struct(fields, reach - HALO, cols), struct(fields // 2, reach - HALO, cols)
+    state_shape = struct(levels, rows, cols)
+    edge_shape = struct(SWEEPS, 2 * fields, 2 * HALO, cols)
+    part_shapes = (zm_shape, edge_shape, edge_shape, state_shape)
+    ends = pltpu.VMEM((2 * fields, 2 * HALO, cols), F32)
+    part = call(
+        functools.partial(interior_kernel, batch=batch),
+        part_shapes,
+        3,
+        (pltpu.VMEM((levels, rows, cols), F32), *work),
+    )(mains, grid, bands)
+    mains, wins, g_ext, near, far = call(
+        halo_kernel, (main_shape, win_shape, g_shape, end_shape, end_shape), 7, input_output_aliases={3: 0, 4: 1, 5: 2}
+    )(near, far, mirror, mains, wins, g_ext, part[3])
+    near, far = swap(near, "gx", 0), swap(far, "gx", 1)
     gbuf = pltpu.VMEM((levels, reach, cols), F32)
-    zm_shape, zw_shape = struct(fields, reach - HALO, cols), struct(fields // 2, reach - HALO, cols)
-    zm_one, xmain = call(
-        functools.partial(main_kernel, batch=batch), (zm_shape, struct(levels, rows, cols)), 3, (gbuf, *work)
-    )(mains, g_ext, bands)
+    zm_one, _, _, xmain = call(
+        edge_kernel, part_shapes, 7, (gbuf, ends, work[2]), input_output_aliases={3: 0, 4: 1, 5: 2, 6: 3}
+    )(mains, g_ext, bands, *part)
     wins, zw_one, x_one, p, near, far, side, sums = call(
         functools.partial(first_kernel, batch=batch),
         (
@@ -568,19 +683,27 @@
         input_output_aliases={0: 0},
     )(wins, g_ext, grid, near_own, far_own, near, far, bands, xmain)
     near, far = swap(near, "gy", 0), swap(far, "gy", 1)
-    zm_two, x_two, share, zm_one = call(
+    *part, zm_one = call(
+        functools.partial(second_interior_kernel, batch=batch),
+        (*part_shapes, zm_shape),
+        5,
+        (pltpu.VMEM((levels, rows, cols), F32), *work),
+        input_output_aliases={3: 4},
+    )(mains, p, bands, zm_one, zw_one)
+    x_two, share, zm_two, _, _, _ = call(
         functools.partial(second_kernel, batch=batch),
-        (zm_shape, struct(levels, rows, cols), struct(devices, cols), zm_shape),
-        11,
+        (state_shape, struct(devices, cols), *part_shapes),
+        13,
         (
             pltpu.VMEM((levels + 1, reach, cols), F32),
             pltpu.VMEM((2, levels, reach, cols), F32),
             *work,
-            pltpu.VMEM((2, levels, rows, cols), F32),
+            pltpu.VMEM((levels, rows, cols), F32),
             pltpu.VMEM((fields // 2, reach - HALO, cols), F32),
+            ends,
         ),
-        input_output_aliases={9: 3},
-    )(mains, wins, p, side, near, far, grid, bands, sums, zm_one, zw_one)
+        input_output_aliases={9: 2, 10: 3, 11: 4, 12: 5},
+    )(mains, wins, p, side, near, far, grid, bands, sums, *part)
     share = lax.all_to_all(share, ("gy", "gx"), 0, 0, tiled=True)
     chunks = 8
     return pl.pallas_call(

time: 58.7 us -> 54.2 us (0.923)
  waiting for transfers between devices: 8.58 us -> 3.85 us
  starting transfers between devices: 8.2 us -> 8.86 us
    ppermute x8, waiting for transfers between devices: 8.58 us -> 3.85 us  [swap(): lax.ppermute(x, axis, [(i + a, i + 1 - a) for i in range(odd, count - 1,...]
    ppermute x8, starting transfers between devices: 8.2 us -> 8.86 us  [swap(): lax.ppermute(x, axis, [(i + a, i + 1 - a) for i in range(odd, count - 1,...]
    pallas_call x2 -> x4, Pallas kernels: 12.3 us -> 12.3 us  [the longest x1 3.88 us: on_device(): call(functools.partial(second_interior_kernel, batch=batch), (*part_shape...]
  transfers between devices with their start and end apart: 8 -> 8, of which waited for: 2 -> 1; matrix products, arithmetic and copies ran while one was open for 0% -> 0% of each run, Pallas kernels for 13% -> 21%
where the time goes in v4:
time: 54.2 us; the launch traced here: 53.9 us
  Pallas kernels  22.5 us (42%)
  blocking collectives  17 us (31%)
  starting transfers between devices  8.86 us (16%)
  waiting for transfers between devices  3.85 us (7%)
  local copies, waits for them, and re-layouts  0.91 us (2%)
  between operations  0.81 us (1%)
    all_to_all x1, blocking collectives, on_device(): share = lax.all_to_all(share, ('gy', 'gx'), 0, 0, tiled=True)  17 us
    ppermute x8, starting transfers between devices, swap(): lax.ppermute(x, axis, [(i + a, i + 1 - a) for i in range(odd, count - 1,...  8.86 us
    pallas_call x1, Pallas kernels, on_device(): call(functools.partial(second_interior_kernel, batch=batch), (*part_shape...  3.88 us
    ppermute x8, waiting for transfers between devices, swap(): lax.ppermute(x, axis, [(i + a, i + 1 - a) for i in range(odd, count - 1,...  3.85 us
    pallas_call x1, Pallas kernels, on_device(): call(functools.partial(second_kernel, batch=batch), (state_shape, struct(...  3.85 us
    pallas_call x1, Pallas kernels, on_device(): call(functools.partial(interior_kernel, batch=batch), part_shapes, 3, (pl...  3.71 us
    pallas_call x1, Pallas kernels, on_device(): call(functools.partial(first_kernel, batch=batch), (win_shape, zw_shape,...  2.91 us
    pallas_call x1, Pallas kernels, on_device(): call(scatter_kernel, (struct(2, levels, rows, cols), struct(fields + leve...  2.73 us
  transfers between devices with their start and end apart: 8, of which 1 were waited for; matrix products, arithmetic and copies ran while one was open for 0% of the time, Pallas kernels for 21%

profile of v4, /device:TPU:0, one launch (start us, length us, event | category | flops | bytes accessed | tf_op | source)
XLA Modules:
  0.0 53.9 jit_solution(4635098110679755198)
XLA Ops:
  0.6 0.0 copy-start.2
  0.6 0.0 copy-start.1
  0.7 2.7 %shard_map.77 = (f32[2,2,64,128]{3,2,1,0:T(8,128)}, f32[66,8,128]{2,1,0:T(8,128)}, f32[66,8,128]{2,1,0:T(8,128)}) custom-call(bf16[32,2,64,128]{3,2,1,0:T(8,128)(2,1)} %ens_in.1, s32[1,1,2048]{2,1,0:T(1,128)} %cell_in.1, s32[1,1,2048]{2,1,0:T(1,128)} %level_in.1, f32[1,1,2048]{2,1,0:T(1,128)} %innov_in.1, f32[1,1,2048]{2,1,0:T(1,128)} %weight_in.1), custom_call_target="tpu_custom_call" | custom-call | flops 2000000000 | bytes 1000000 | tf_op jit(solution)/shard_map/pallas_call | solution.py:619
  3.4 3.0 %collective-permute-start = (f32[66,8,128]{2,1,0:T(8,128)}, f32[66,8,128]{2,1,0:T(8,128)S(1)}, u32[]{:S(2)}, u32[]{:S(2)}) collective-permute-start(f32[66,8,128]{2,1,0:T(8,128)} %get-tuple-element.39), channel_id=1, source_target_pairs={{0,4},{4,0},{8,12},{12,8},{16,20},{20,16},{24,28},{28,24},{1,5},{5... | collective-permute-start | bytes 811016 | tf_op jit(solution)/shard_map/ppermute | solution.py:55
  6.4 0.7 %collective-permute-start.1 = (f32[66,8,128]{2,1,0:T(8,128)}, f32[66,8,128]{2,1,0:T(8,128)S(1)}, u32[]{:S(2)}, u32[]{:S(2)}) collective-permute-start(f32[66,8,128]{2,1,0:T(8,128)} %get-tuple-element.40), channel_id=1, source_target_pairs={{4,8},{8,4},{12,16},{16,12},{20,24},{24,20},{5,9},{9,5},{13,17},{1... | collective-permute-start | bytes 811016 | tf_op jit(solution)/shard_map/ppermute | solution.py:55
  7.1 0.0 copy-done.2
  7.1 0.0 copy-done.1
  7.1 0.0 copy-start
  7.1 0.9 %copy-done = f32[2,2,64,128]{3,2,1,0:T(8,128)S(1)} copy-done((f32[2,2,64,128]{3,2,1,0:T(8,128)S(1)}, f32[2,2,64,128]{3,2,1,0:T(8,128)}, u32[]{:S(2)}) %copy-start) | copy-done | bytes 131096
  8.0 1.9 %shard_map.78 = (f32[64,80,128]{2,1,0:T(8,128)S(1)}, f32[32,80,128]{2,1,0:T(8,128)S(1)}, f32[9,64,128]{2,1,0:T(8,128)S(1)}, f32[9,64,128]{2,1,0:T(8,128)S(1)}, f...) custom-call(bf16[32,2,64,128]{3,2,1,0:T(8,128)(2,1)S(1)} %copy-done.1, ...), custom_call_target="tpu_custom_call" | custom-call | flops 2000000000 | bytes 1000000 | tf_op jit(solution)/shard_map/pallas_call | solution.py:630
  10.0 0.1 collective-permute-start.2
  10.0 0.7 %collective-permute-start.3 = (f32[9,64,128]{2,1,0:T(8,128)S(1)}, f32[9,64,128]{2,1,0:T(8,128)S(1)}, u32[]{:S(2)}, u32[]{:S(2)}) collective-permute-start(f32[9,64,128]{2,1,0:T(8,128)S(1)} %get-tuple-element.52), channel_id=1, source_target_pairs={{1,2},{2,1},{5,6},{6,5},{9,10},{10,9},{13,14},{14,13},{17,18},{18,... | collective-permute-start | bytes 884744 | tf_op jit(solution)/shard_map/ppermute | solution.py:55
  10.7 3.7 %shard_map.79 = (f32[64,72,128]{2,1,0:T(8,128)S(1)}, f32[4,128,16,128]{3,2,1,0:T(8,128)S(1)}, f32[4,128,16,128]{3,2,1,0:T(8,128)S(1)}, f32[2,64,128]{2,1,0:T(8,128)S(1)}) custom-call(f32[64,80,128]{2,1,0:T(8,128)S(1)} %get-tuple-element.43.pack.refs_0_, f32[2,2,64,128]{3,2,1,0:T(8,128)S(1)} %copy-done, bf16[2,256,512]{2,1,0:T(8,128)(2,1)S(1)} %get-tuple-element.46.bands), custom_call_target="tpu_custom_call" | custom-call | flops 2000000000 | bytes 1000000 | tf_op jit(solution)/shard_map/pallas_call | solution.py:655
  14.4 3.8 %collective-permute-done.from_near = f32[66,8,128]{2,1,0:T(8,128)S(1)} collective-permute-done((f32[66,8,128]{2,1,0:T(8,128)}, f32[66,8,128]{2,1,0:T(8,128)S(1)}, u32[]{:S(2)}, u32[]{:S(2)}) %collective-permute-start) | collective-permute-done | bytes 270368 | tf_op jit(solution)/shard_map/ppermute | solution.py:55
  18.3 0.0 collective-permute-done.1.from_far
  18.3 1.1 %shard_map.80 = (f32[64,80,128]{2,1,0:T(8,128)S(1)}, f32[32,80,128]{2,1,0:T(8,128)S(1)}, f32[2,80,128]{2,1,0:T(8,128)S(1)}, f32[9,16,128]{2,1,0:T(8,128)S(1)}, f32[9,16,128]{2,1,0:T(8,128)S(1)}) custom-call(f32[66,8,128]{2,1,0:T(8,128)S(1)} %collective-permute-done.from_near, ...), custom_call_target="tpu_custom_call", output_to_operand_aliasing={{0}: (3, {}), {1}: (4, {}), {2}: (5, {})} | custom-call | flops 2000000000 | bytes 1000000 | tf_op jit(solution)/shard_map/pallas_call | solution.py:661
  19.3 0.0 collective-permute-start.4
  19.4 0.7 %collective-permute-start.5 = (f32[9,16,128]{2,1,0:T(8,128)S(1)}, f32[9,16,128]{2,1,0:T(8,128)S(1)}, u32[]{:S(2)}, u32[]{:S(2)}) collective-permute-start(f32[9,16,128]{2,1,0:T(8,128)S(1)} %get-tuple-element.54), channel_id=1, source_target_pairs={{1,2},{2,1},{5,6},{6,5},{9,10},{10,9},{13,14},{14,13},{17,18},{18,... | collective-permute-start | bytes 221192 | tf_op jit(solution)/shard_map/ppermute | solution.py:55
  20.0 0.9 %shard_map.81 = (f32[64,72,128]{2,1,0:T(8,128)S(1)}, f32[4,128,16,128]{3,2,1,0:T(8,128)S(1)}, f32[4,128,16,128]{3,2,1,0:T(8,128)S(1)}, f32[2,64,128]{2,1,0:T(8,128)S(1)}) custom-call(f32[64,80,128]{2,1,0:T(8,128)S(1)} %get-tuple-element.48.pack.mains, ...), custom_call_target="tpu_custom_call", output_to_operand_aliasing={{0}: (3, {}), {1}: (4, {}), {2}: (5, {}), {3}: (6, {})} | custom-call | flops 2000000000 | bytes 1000000 | tf_op jit(solution)/shard_map/pallas_call | solution.py:666
  20.9 0.0 collective-permute-done.2.near
  20.9 0.0 collective-permute-done.3.far
  21.0 0.0 collective-permute-done.4.near_ends
  21.0 0.0 collective-permute-done.5.far_ends
  21.0 2.9 %shard_map.82 = (f32[32,80,128]{2,1,0:T(8,128)S(1)}, f32[32,72,128]{2,1,0:T(8,128)S(1)}, f32[2,64,128]{2,1,0:T(8,128)S(1)}, f32[2,64,128]{2,1,0:T(8,128)S(1)}, f...) custom-call(f32[32,80,128]{2,1,0:T(8,128)S(1)} %get-tuple-element.49, ...), custom_call_target="tpu_custom_call", output_to_operand_aliasing={{0}: (0, {})} | custom-call | flops 2000000000 | bytes 1000000 | tf_op jit(solution)/shard_map/pallas_call | solution.py:669
  23.9 3.1 %collective-permute-start.6 = (f32[3,8,128]{2,1,0:T(8,128)S(1)}, f32[3,8,128]{2,1,0:T(8,128)S(1)}, u32[]{:S(2)}, u32[]{:S(2)}) collective-permute-start(f32[3,8,128]{2,1,0:T(8,128)S(1)} %get-tuple-element.62), channel_id=1, source_target_pairs={{0,4},{4,0},{8,12},{12,8},{16,20},{20,16},{24,28},{28,24},{1,5},{5... | collective-permute-start | bytes 36872 | tf_op jit(solution)/shard_map/ppermute | solution.py:55
  27.0 0.7 %collective-permute-start.7 = (f32[3,8,128]{2,1,0:T(8,128)S(1)}, f32[3,8,128]{2,1,0:T(8,128)S(1)}, u32[]{:S(2)}, u32[]{:S(2)}) collective-permute-start(f32[3,8,128]{2,1,0:T(8,128)S(1)} %get-tuple-element.63), channel_id=1, source_target_pairs={{4,8},{8,4},{12,16},{16,12},{20,24},{24,20},{5,9},{9,5},{13,17},{1... | collective-permute-start | bytes 36872 | tf_op jit(solution)/shard_map/ppermute | solution.py:55
  27.6 3.9 %shard_map.83 = (f32[64,72,128]{2,1,0:T(8,128)S(1)}, f32[4,128,16,128]{3,2,1,0:T(8,128)S(1)}, f32[4,128,16,128]{3,2,1,0:T(8,128)S(1)}, f32[2,64,128]{2,1,0:T(8,128)S(1)}, f32[64,72,128]{2,1,0:T(8,128)S(1)}) custom-call(f32[64,80,128]{2,1,0:T(8,128)S(1)} %get-tuple-element.48.pack.mains, ...), custom_call_target="tpu_custom_call", output_to_operand_aliasing={{4}: (3, {})} | custom-call | flops 2000000000 | bytes 1000000 | tf_op jit(solution)/shard_map/pallas_call | solution.py:686
  31.5 0.0 collective-permute-done.6.near
  31.5 0.0 collective-permute-done.7.far
  31.5 3.8 %shard_map.84 = (f32[2,64,128]{2,1,0:T(8,128)S(1)}, f32[32,128]{1,0:T(8,128)S(1)}, f32[64,72,128]{2,1,0:T(8,128)S(1)}, f32[4,128,16,128]{3,2,1,0:T(8,128)S(1)}, ...) custom-call(f32[64,80,128]{2,1,0:T(8,128)S(1)} %get-tuple-element.48, ...), custom_call_target="tpu_custom_call", output_to_operand_aliasing={{2}: (9, {}), {3}: (10, {}), {4}: (11, {}), {5}: (12, {})} | custom-call | flops 2000000000 | bytes 1000000 | tf_op jit(solution)/shard_map/pallas_call | solution.py:693
  35.4 17.0 %all_to_all.11 = f32[32,1,128]{2,1,0:T(1,128)S(1)} all-to-all(f32[32,1,128]{2,1,0:T(1,128)S(1)} %bitcast.5), channel_id=1, replica_groups=mesh['gy'=8,'gx'=4] {'gy','gx'}, dimensions={0} | all-to-all | bytes 32768 | tf_op jit(solution)/shard_map/all_to_all | solution.py:707
  52.4 1.5 %shard_map.85 = (f32[32,2,64,128]{3,2,1,0:T(8,128)}, f32[2,64,128]{2,1,0:T(8,128)}) custom-call(f32[32,128]{1,0:T(8,128)S(1)} %bitcast.4, f32[64,72,128]{2,1,0:T(8,128)S(1)} %get-tuple-element.72.z_one, f32[64,72,128]{2,1,0:T(8,128)S(1)} %get-tuple-element.73.z_two, f32[2,64,128]{2,1,0:T(8,128)S(1)} %get-tuple-element.74.x_one, ...), custom_call_target="tpu_custom_call" | custom-call | tf_op jit(solution)/shard_map/pallas_call | solution.py:709
Async XLA Ops:
  0.6 6.5 %copy-start.2 = (bf16[4,2,128,512]{3,2,1,0:T(8,128)(2,1)S(1)}, bf16[4,2,128,512]{3,2,1,0:T(8,128)(2,1)}, u32[]{:S(2)}) copy-start(bf16[4,2,128,512]{3,2,1,0:T(8,128)(2,1)} %constant.2.clone.bands_in) | copy-start | bytes 3145732
  0.6 6.5 %copy-start.1 = (bf16[32,2,64,128]{3,2,1,0:T(8,128)(2,1)S(1)}, bf16[32,2,64,128]{3,2,1,0:T(8,128)(2,1)}, u32[]{:S(2)}) copy-start(bf16[32,2,64,128]{3,2,1,0:T(8,128)(2,1)} %ens_in.1) | copy-start | bytes 3145732
  3.4 14.9 %collective-permute-start = (f32[66,8,128]{2,1,0:T(8,128)}, f32[66,8,128]{2,1,0:T(8,128)S(1)}, u32[]{:S(2)}, u32[]{:S(2)}) collective-permute-start(f32[66,8,128]{2,1,0:T(8,128)} %get-tuple-element.39), channel_id=1, source_target_pairs={{0,4},{4,0},{8,12},{12,8},{16,20},{20,16},{24,28},{28,24},{1,5},{5... | collective-permute-start | bytes 811016 | tf_op jit(solution)/shard_map/ppermute | solution.py:55
  6.4 11.9 %collective-permute-start.1 = (f32[66,8,128]{2,1,0:T(8,128)}, f32[66,8,128]{2,1,0:T(8,128)S(1)}, u32[]{:S(2)}, u32[]{:S(2)}) collective-permute-start(f32[66,8,128]{2,1,0:T(8,128)} %get-tuple-element.40), channel_id=1, source_target_pairs={{4,8},{8,4},{12,16},{16,12},{20,24},{24,20},{5,9},{9,5},{13,17},{1... | collective-permute-start | bytes 811016 | tf_op jit(solution)/shard_map/ppermute | solution.py:55
  7.1 0.9 %copy-start = (f32[2,2,64,128]{3,2,1,0:T(8,128)S(1)}, f32[2,2,64,128]{3,2,1,0:T(8,128)}, u32[]{:S(2)}) copy-start(f32[2,2,64,128]{3,2,1,0:T(8,128)} %get-tuple-element.41.grid.g) | copy-start | bytes 393220
  10.0 11.0 %collective-permute-start.2 = (f32[9,64,128]{2,1,0:T(8,128)S(1)}, f32[9,64,128]{2,1,0:T(8,128)S(1)}, u32[]{:S(2)}, u32[]{:S(2)}) collective-permute-start(f32[9,64,128]{2,1,0:T(8,128)S(1)} %get-tuple-element.51), channel_id=1, source_target_pairs={{0,1},{1,0},{2,3},{3,2},{4,5},{5,4},{6,7},{7,6},{8,9},{9,8},{10,11... | collective-permute-start | bytes 884744 | tf_op jit(solution)/shard_map/ppermute | solution.py:55
  10.0 10.9 %collective-permute-start.3 = (f32[9,64,128]{2,1,0:T(8,128)S(1)}, f32[9,64,128]{2,1,0:T(8,128)S(1)}, u32[]{:S(2)}, u32[]{:S(2)}) collective-permute-start(f32[9,64,128]{2,1,0:T(8,128)S(1)} %get-tuple-element.52), channel_id=1, source_target_pairs={{1,2},{2,1},{5,6},{6,5},{9,10},{10,9},{13,14},{14,13},{17,18},{18,... | collective-permute-start | bytes 884744 | tf_op jit(solution)/shard_map/ppermute | solution.py:55
  19.3 1.6 %collective-permute-start.4 = (f32[9,16,128]{2,1,0:T(8,128)S(1)}, f32[9,16,128]{2,1,0:T(8,128)S(1)}, u32[]{:S(2)}, u32[]{:S(2)}) collective-permute-start(f32[9,16,128]{2,1,0:T(8,128)S(1)} %get-tuple-element.53), channel_id=1, source_target_pairs={{0,1},{1,0},{2,3},{3,2},{4,5},{5,4},{6,7},{7,6},{8,9},{9,8},{10,11... | collective-permute-start | bytes 221192 | tf_op jit(solution)/shard_map/ppermute | solution.py:55
  19.4 1.6 %collective-permute-start.5 = (f32[9,16,128]{2,1,0:T(8,128)S(1)}, f32[9,16,128]{2,1,0:T(8,128)S(1)}, u32[]{:S(2)}, u32[]{:S(2)}) collective-permute-start(f32[9,16,128]{2,1,0:T(8,128)S(1)} %get-tuple-element.54), channel_id=1, source_target_pairs={{1,2},{2,1},{5,6},{6,5},{9,10},{10,9},{13,14},{14,13},{17,18},{18,... | collective-permute-start | bytes 221192 | tf_op jit(solution)/shard_map/ppermute | solution.py:55
  23.9 7.6 %collective-permute-start.6 = (f32[3,8,128]{2,1,0:T(8,128)S(1)}, f32[3,8,128]{2,1,0:T(8,128)S(1)}, u32[]{:S(2)}, u32[]{:S(2)}) collective-permute-start(f32[3,8,128]{2,1,0:T(8,128)S(1)} %get-tuple-element.62), channel_id=1, source_target_pairs={{0,4},{4,0},{8,12},{12,8},{16,20},{20,16},{24,28},{28,24},{1,5},{5... | collective-permute-start | bytes 36872 | tf_op jit(solution)/shard_map/ppermute | solution.py:55
  27.0 4.6 %collective-permute-start.7 = (f32[3,8,128]{2,1,0:T(8,128)S(1)}, f32[3,8,128]{2,1,0:T(8,128)S(1)}, u32[]{:S(2)}, u32[]{:S(2)}) collective-permute-start(f32[3,8,128]{2,1,0:T(8,128)S(1)} %get-tuple-element.63), channel_id=1, source_target_pairs={{4,8},{8,4},{12,16},{16,12},{20,24},{24,20},{5,9},{9,5},{13,17},{1... | collective-permute-start | bytes 36872 | tf_op jit(solution)/shard_map/ppermute | solution.py:55

commit v5 on v4

--- a/solution.py
+++ b/solution.py
@@ -364,6 +364,10 @@
             xacc[level, base : base + HALO, :] = total
 
 
+def level_at(b, i, batch, per_level):
+    return b * batch // per_level if batch <= per_level else i // per_level
+
+
 def covariance(pack, bands, kind, g, z, xacc, fbuf, prod, lhs, batch, build=None, also=None):
     count, reach, _ = pack.shape
     inner, rows = reach - HALO, reach - 2 * HALO
@@ -371,9 +375,9 @@
     xacc[...] = jnp.zeros_like(xacc)
 
     def step(b, _):
-        level = b * batch // per_level
         for i in range(batch):
             at = b * batch + i
+            level = level_at(b, i, batch, per_level)
             if build is not None:
                 pack[at] = build(b, i, pack[at])
             f = pack[at] * g[level]
@@ -388,6 +392,7 @@
                 also(b, i, v)
         band_products(lhs, bands, kind, prod, batch * inner)
         for i in range(batch):
+            level = level_at(b, i, batch, per_level)
             v = combine(rows_of(prod, i * inner, rows), field_rows(z, b * batch + i, rows), rows)
             xacc[level] += v * pack[b * batch + i, HALO : HALO + rows, :]
         return 0
@@ -593,7 +598,7 @@
     members, levels, rows, cols = ensemble.shape
     fields = members * levels
     reach = rows + 2 * HALO
-    batch = 16
+    batch = 32
     strips = fields // 8 + 1
     devices = lax.axis_size("gy") * lax.axis_size("gx")
     hbm = pl.BlockSpec(memory_space=pltpu.HBM)
@@ -601,7 +606,7 @@
     def struct(*shape):
         return jax.ShapeDtypeStruct(shape, F32)
 
-    def call(kernel, outs, ins, scratch=(), limit=16, work=2, **kw):
+    def call(kernel, outs, ins, scratch=(), limit=24, work=2, **kw):
         return pl.pallas_call(
             kernel,
             out_shape=outs,

time: 54.2 us -> 53 us (0.978)
  Pallas kernels: 22.5 us -> 21.1 us
    pallas_call x1, Pallas kernels: 3.85 us -> 3.24 us  [on_device(): call(functools.partial(second_kernel, batch=batch), (state_shape, struct(...]
where the time goes in v5:
time: 53 us; the launch traced here: 52.8 us
  Pallas kernels  21.1 us (40%)
  blocking collectives  17.3 us (33%)
  starting transfers between devices  8.59 us (16%)
  waiting for transfers between devices  4.11 us (8%)
  local copies, waits for them, and re-layouts  0.91 us (2%)
  between operations  0.82 us (2%)
    all_to_all x1, blocking collectives, on_device(): share = lax.all_to_all(share, ('gy', 'gx'), 0, 0, tiled=True)  17.3 us
    ppermute x8, starting transfers between devices, swap(): lax.ppermute(x, axis, [(i + a, i + 1 - a) for i in range(odd, count - 1,...  8.59 us
    ppermute x8, waiting for transfers between devices, swap(): lax.ppermute(x, axis, [(i + a, i + 1 - a) for i in range(odd, count - 1,...  4.11 us
    pallas_call x1, Pallas kernels, on_device(): call(functools.partial(second_interior_kernel, batch=batch), (*part_shape...  3.61 us
    pallas_call x1, Pallas kernels, on_device(): call(functools.partial(interior_kernel, batch=batch), part_shapes, 3, (pl...  3.45 us
    pallas_call x1, Pallas kernels, on_device(): call(functools.partial(second_kernel, batch=batch), (state_shape, struct(...  3.24 us
    pallas_call x1, Pallas kernels, on_device(): call(scatter_kernel, (struct(2, levels, rows, cols), struct(fields + leve...  2.73 us
    pallas_call x1, Pallas kernels, on_device(): call(functools.partial(first_kernel, batch=batch), (win_shape, zw_shape,...  2.65 us
  transfers between devices with their start and end apart: 8, of which 1 were waited for; matrix products, arithmetic and copies ran while one was open for 0% of the time, Pallas kernels for 21%

profile of v5, /device:TPU:0, one launch (start us, length us, event | category | flops | bytes accessed | tf_op | source)
XLA Modules:
  0.0 52.8 jit_solution(10407702153465550176)
XLA Ops:
  0.6 0.0 copy-start.3
  0.6 0.0 copy-start.2
  0.7 2.7 %shard_map.77 = (f32[2,2,64,128]{3,2,1,0:T(8,128)}, f32[66,8,128]{2,1,0:T(8,128)}, f32[66,8,128]{2,1,0:T(8,128)}) custom-call(bf16[32,2,64,128]{3,2,1,0:T(8,128)(2,1)} %ens_in.1, s32[1,1,2048]{2,1,0:T(1,128)} %cell_in.1, s32[1,1,2048]{2,1,0:T(1,128)} %level_in.1, f32[1,1,2048]{2,1,0:T(1,128)} %innov_in.1, f32[1,1,2048]{2,1,0:T(1,128)} %weight_in.1), custom_call_target="tpu_custom_call" | custom-call | flops 2000000000 | bytes 1000000 | tf_op jit(solution)/shard_map/pallas_call | solution.py:624
  3.4 3.0 %collective-permute-start = (f32[66,8,128]{2,1,0:T(8,128)}, f32[66,8,128]{2,1,0:T(8,128)S(1)}, u32[]{:S(2)}, u32[]{:S(2)}) collective-permute-start(f32[66,8,128]{2,1,0:T(8,128)} %get-tuple-element.39), channel_id=1, source_target_pairs={{0,4},{4,0},{8,12},{12,8},{16,20},{20,16},{24,28},{28,24},{1,5},{5... | collective-permute-start | bytes 811016 | tf_op jit(solution)/shard_map/ppermute | solution.py:55
  6.4 0.7 %collective-permute-start.1 = (f32[66,8,128]{2,1,0:T(8,128)}, f32[66,8,128]{2,1,0:T(8,128)S(1)}, u32[]{:S(2)}, u32[]{:S(2)}) collective-permute-start(f32[66,8,128]{2,1,0:T(8,128)} %get-tuple-element.40), channel_id=1, source_target_pairs={{4,8},{8,4},{12,16},{16,12},{20,24},{24,20},{5,9},{9,5},{13,17},{1... | collective-permute-start | bytes 811016 | tf_op jit(solution)/shard_map/ppermute | solution.py:55
  7.1 0.0 copy-done.3
  7.1 0.0 copy-done.2
  7.1 0.9 %copy-done = f32[2,2,64,128]{3,2,1,0:T(8,128)S(1)} copy-done((f32[2,2,64,128]{3,2,1,0:T(8,128)S(1)}, f32[2,2,64,128]{3,2,1,0:T(8,128)}, u32[]{:S(2)}) %copy-start) | copy-done | bytes 131096
  8.0 1.9 %shard_map.78 = (f32[64,80,128]{2,1,0:T(8,128)S(1)}, f32[32,80,128]{2,1,0:T(8,128)S(1)}, f32[9,64,128]{2,1,0:T(8,128)S(1)}, f32[9,64,128]{2,1,0:T(8,128)S(1)}, f...) custom-call(bf16[32,2,64,128]{3,2,1,0:T(8,128)(2,1)S(1)} %copy-done.2, ...), custom_call_target="tpu_custom_call" | custom-call | flops 2000000000 | bytes 1000000 | tf_op jit(solution)/shard_map/pallas_call | solution.py:635
  9.9 0.1 collective-permute-start.2
  10.0 0.7 %collective-permute-start.3 = (f32[9,64,128]{2,1,0:T(8,128)S(1)}, f32[9,64,128]{2,1,0:T(8,128)S(1)}, u32[]{:S(2)}, u32[]{:S(2)}) collective-permute-start(f32[9,64,128]{2,1,0:T(8,128)S(1)} %get-tuple-element.52), channel_id=1, source_target_pairs={{1,2},{2,1},{5,6},{6,5},{9,10},{10,9},{13,14},{14,13},{17,18},{18,... | collective-permute-start | bytes 884744 | tf_op jit(solution)/shard_map/ppermute | solution.py:55
  10.7 3.5 %shard_map.79 = (f32[64,72,128]{2,1,0:T(8,128)S(1)}, f32[4,128,16,128]{3,2,1,0:T(8,128)S(1)}, f32[4,128,16,128]{3,2,1,0:T(8,128)S(1)}, f32[2,64,128]{2,1,0:T(8,128)S(1)}) custom-call(f32[64,80,128]{2,1,0:T(8,128)S(1)} %get-tuple-element.43.pack.refs_0_, f32[2,2,64,128]{3,2,1,0:T(8,128)S(1)} %copy-done, bf16[2,256,512]{2,1,0:T(8,128)(2,1)S(1)} %get-tuple-element.46.bands), custom_call_target="tpu_custom_call" | custom-call | flops 2000000000 | bytes 1000000 | tf_op jit(solution)/shard_map/pallas_call | solution.py:660
  14.2 4.1 %collective-permute-done.from_near = f32[66,8,128]{2,1,0:T(8,128)S(1)} collective-permute-done((f32[66,8,128]{2,1,0:T(8,128)}, f32[66,8,128]{2,1,0:T(8,128)S(1)}, u32[]{:S(2)}, u32[]{:S(2)}) %collective-permute-start) | collective-permute-done | bytes 270368 | tf_op jit(solution)/shard_map/ppermute | solution.py:55
  18.3 0.0 collective-permute-done.1.from_far
  18.3 1.1 %shard_map.80 = (f32[64,80,128]{2,1,0:T(8,128)S(1)}, f32[32,80,128]{2,1,0:T(8,128)S(1)}, f32[2,80,128]{2,1,0:T(8,128)S(1)}, f32[9,16,128]{2,1,0:T(8,128)S(1)}, f32[9,16,128]{2,1,0:T(8,128)S(1)}) custom-call(f32[66,8,128]{2,1,0:T(8,128)S(1)} %collective-permute-done.from_near, ...), custom_call_target="tpu_custom_call", output_to_operand_aliasing={{0}: (3, {}), {1}: (4, {}), {2}: (5, {})} | custom-call | flops 2000000000 | bytes 1000000 | tf_op jit(solution)/shard_map/pallas_call | solution.py:666
  19.3 0.0 collective-permute-start.4
  19.3 0.7 %collective-permute-start.5 = (f32[9,16,128]{2,1,0:T(8,128)S(1)}, f32[9,16,128]{2,1,0:T(8,128)S(1)}, u32[]{:S(2)}, u32[]{:S(2)}) collective-permute-start(f32[9,16,128]{2,1,0:T(8,128)S(1)} %get-tuple-element.54), channel_id=1, source_target_pairs={{1,2},{2,1},{5,6},{6,5},{9,10},{10,9},{13,14},{14,13},{17,18},{18,... | collective-permute-start | bytes 221192 | tf_op jit(solution)/shard_map/ppermute | solution.py:55
  20.0 0.9 %shard_map.81 = (f32[64,72,128]{2,1,0:T(8,128)S(1)}, f32[4,128,16,128]{3,2,1,0:T(8,128)S(1)}, f32[4,128,16,128]{3,2,1,0:T(8,128)S(1)}, f32[2,64,128]{2,1,0:T(8,128)S(1)}) custom-call(f32[64,80,128]{2,1,0:T(8,128)S(1)} %get-tuple-element.48.pack.mains, ...), custom_call_target="tpu_custom_call", output_to_operand_aliasing={{0}: (3, {}), {1}: (4, {}), {2}: (5, {}), {3}: (6, {})} | custom-call | flops 2000000000 | bytes 1000000 | tf_op jit(solution)/shard_map/pallas_call | solution.py:671
  20.9 0.0 collective-permute-done.2.near
  20.9 0.0 collective-permute-done.3.far
  21.0 0.0 collective-permute-done.4.near_ends
  21.0 0.0 collective-permute-done.5.far_ends
  21.0 2.7 %shard_map.82 = (f32[32,80,128]{2,1,0:T(8,128)S(1)}, f32[32,72,128]{2,1,0:T(8,128)S(1)}, f32[2,64,128]{2,1,0:T(8,128)S(1)}, f32[2,64,128]{2,1,0:T(8,128)S(1)}, f...) custom-call(f32[32,80,128]{2,1,0:T(8,128)S(1)} %get-tuple-element.49, ...), custom_call_target="tpu_custom_call", output_to_operand_aliasing={{0}: (0, {})} | custom-call | flops 2000000000 | bytes 1000000 | tf_op jit(solution)/shard_map/pallas_call | solution.py:674
  23.6 2.8 %collective-permute-start.6 = (f32[3,8,128]{2,1,0:T(8,128)S(1)}, f32[3,8,128]{2,1,0:T(8,128)S(1)}, u32[]{:S(2)}, u32[]{:S(2)}) collective-permute-start(f32[3,8,128]{2,1,0:T(8,128)S(1)} %get-tuple-element.62), channel_id=1, source_target_pairs={{0,4},{4,0},{8,12},{12,8},{16,20},{20,16},{24,28},{28,24},{1,5},{5... | collective-permute-start | bytes 36872 | tf_op jit(solution)/shard_map/ppermute | solution.py:55
  26.4 0.7 %collective-permute-start.7 = (f32[3,8,128]{2,1,0:T(8,128)S(1)}, f32[3,8,128]{2,1,0:T(8,128)S(1)}, u32[]{:S(2)}, u32[]{:S(2)}) collective-permute-start(f32[3,8,128]{2,1,0:T(8,128)S(1)} %get-tuple-element.63), channel_id=1, source_target_pairs={{4,8},{8,4},{12,16},{16,12},{20,24},{24,20},{5,9},{9,5},{13,17},{1... | collective-permute-start | bytes 36872 | tf_op jit(solution)/shard_map/ppermute | solution.py:55
  27.1 3.6 %shard_map.83 = (f32[64,72,128]{2,1,0:T(8,128)S(1)}, f32[4,128,16,128]{3,2,1,0:T(8,128)S(1)}, f32[4,128,16,128]{3,2,1,0:T(8,128)S(1)}, f32[2,64,128]{2,1,0:T(8,128)S(1)}, f32[64,72,128]{2,1,0:T(8,128)S(1)}) custom-call(f32[64,80,128]{2,1,0:T(8,128)S(1)} %get-tuple-element.48.pack.mains, ...), custom_call_target="tpu_custom_call", output_to_operand_aliasing={{4}: (3, {})} | custom-call | flops 2000000000 | bytes 1000000 | tf_op jit(solution)/shard_map/pallas_call | solution.py:691
  30.7 0.0 collective-permute-done.6.near
  30.7 0.0 collective-permute-done.7.far
  30.7 0.0 copy-done.1
  30.8 3.2 %shard_map.84 = (f32[2,64,128]{2,1,0:T(8,128)S(1)}, f32[32,128]{1,0:T(8,128)S(1)}, f32[64,72,128]{2,1,0:T(8,128)S(1)}, f32[4,128,16,128]{3,2,1,0:T(8,128)S(1)}, ...) custom-call(f32[64,80,128]{2,1,0:T(8,128)S(1)} %get-tuple-element.48, ...), custom_call_target="tpu_custom_call", output_to_operand_aliasing={{2}: (9, {}), {3}: (10, {}), {4}: (11, {}), {5}: (12, {})} | custom-call | flops 2000000000 | bytes 1000000 | tf_op jit(solution)/shard_map/pallas_call | solution.py:698
  34.0 17.3 %all_to_all.11 = f32[32,1,128]{2,1,0:T(1,128)S(1)} all-to-all(f32[32,1,128]{2,1,0:T(1,128)S(1)} %bitcast.5), channel_id=1, replica_groups=mesh['gy'=8,'gx'=4] {'gy','gx'}, dimensions={0} | all-to-all | bytes 32768 | tf_op jit(solution)/shard_map/all_to_all | solution.py:712
  51.2 1.5 %shard_map.85 = (f32[32,2,64,128]{3,2,1,0:T(8,128)}, f32[2,64,128]{2,1,0:T(8,128)}) custom-call(f32[32,128]{1,0:T(8,128)S(1)} %bitcast.4, f32[64,72,128]{2,1,0:T(8,128)S(1)} %get-tuple-element.72.z_one, f32[64,72,128]{2,1,0:T(8,128)S(1)} %get-tuple-element.73.z_two, f32[2,64,128]{2,1,0:T(8,128)S(1)} %get-tuple-element.74.x_one, ...), custom_call_target="tpu_custom_call" | custom-call | tf_op jit(solution)/shard_map/pallas_call | solution.py:714
  (2 shorter events, 0.0 us)
Async XLA Ops:
  0.6 6.5 %copy-start.3 = (bf16[4,2,128,512]{3,2,1,0:T(8,128)(2,1)S(1)}, bf16[4,2,128,512]{3,2,1,0:T(8,128)(2,1)}, u32[]{:S(2)}) copy-start(bf16[4,2,128,512]{3,2,1,0:T(8,128)(2,1)} %constant.2.clone.bands_in) | copy-start | bytes 3145732
  0.6 6.5 %copy-start.2 = (bf16[32,2,64,128]{3,2,1,0:T(8,128)(2,1)S(1)}, bf16[32,2,64,128]{3,2,1,0:T(8,128)(2,1)}, u32[]{:S(2)}) copy-start(bf16[32,2,64,128]{3,2,1,0:T(8,128)(2,1)} %ens_in.1) | copy-start | bytes 3145732
  3.4 14.9 %collective-permute-start = (f32[66,8,128]{2,1,0:T(8,128)}, f32[66,8,128]{2,1,0:T(8,128)S(1)}, u32[]{:S(2)}, u32[]{:S(2)}) collective-permute-start(f32[66,8,128]{2,1,0:T(8,128)} %get-tuple-element.39), channel_id=1, source_target_pairs={{0,4},{4,0},{8,12},{12,8},{16,20},{20,16},{24,28},{28,24},{1,5},{5... | collective-permute-start | bytes 811016 | tf_op jit(solution)/shard_map/ppermute | solution.py:55
  6.4 11.9 %collective-permute-start.1 = (f32[66,8,128]{2,1,0:T(8,128)}, f32[66,8,128]{2,1,0:T(8,128)S(1)}, u32[]{:S(2)}, u32[]{:S(2)}) collective-permute-start(f32[66,8,128]{2,1,0:T(8,128)} %get-tuple-element.40), channel_id=1, source_target_pairs={{4,8},{8,4},{12,16},{16,12},{20,24},{24,20},{5,9},{9,5},{13,17},{1... | collective-permute-start | bytes 811016 | tf_op jit(solution)/shard_map/ppermute | solution.py:55
  7.1 0.9 %copy-start = (f32[2,2,64,128]{3,2,1,0:T(8,128)S(1)}, f32[2,2,64,128]{3,2,1,0:T(8,128)}, u32[]{:S(2)}) copy-start(f32[2,2,64,128]{3,2,1,0:T(8,128)} %get-tuple-element.41.grid.g) | copy-start | bytes 393220
  9.9 11.0 %collective-permute-start.2 = (f32[9,64,128]{2,1,0:T(8,128)S(1)}, f32[9,64,128]{2,1,0:T(8,128)S(1)}, u32[]{:S(2)}, u32[]{:S(2)}) collective-permute-start(f32[9,64,128]{2,1,0:T(8,128)S(1)} %get-tuple-element.51), channel_id=1, source_target_pairs={{0,1},{1,0},{2,3},{3,2},{4,5},{5,4},{6,7},{7,6},{8,9},{9,8},{10,11... | collective-permute-start | bytes 884744 | tf_op jit(solution)/shard_map/ppermute | solution.py:55
  10.0 10.9 %collective-permute-start.3 = (f32[9,64,128]{2,1,0:T(8,128)S(1)}, f32[9,64,128]{2,1,0:T(8,128)S(1)}, u32[]{:S(2)}, u32[]{:S(2)}) collective-permute-start(f32[9,64,128]{2,1,0:T(8,128)S(1)} %get-tuple-element.52), channel_id=1, source_target_pairs={{1,2},{2,1},{5,6},{6,5},{9,10},{10,9},{13,14},{14,13},{17,18},{18,... | collective-permute-start | bytes 884744 | tf_op jit(solution)/shard_map/ppermute | solution.py:55
  19.3 1.6 %collective-permute-start.4 = (f32[9,16,128]{2,1,0:T(8,128)S(1)}, f32[9,16,128]{2,1,0:T(8,128)S(1)}, u32[]{:S(2)}, u32[]{:S(2)}) collective-permute-start(f32[9,16,128]{2,1,0:T(8,128)S(1)} %get-tuple-element.53), channel_id=1, source_target_pairs={{0,1},{1,0},{2,3},{3,2},{4,5},{5,4},{6,7},{7,6},{8,9},{9,8},{10,11... | collective-permute-start | bytes 221192 | tf_op jit(solution)/shard_map/ppermute | solution.py:55
  19.3 1.6 %collective-permute-start.5 = (f32[9,16,128]{2,1,0:T(8,128)S(1)}, f32[9,16,128]{2,1,0:T(8,128)S(1)}, u32[]{:S(2)}, u32[]{:S(2)}) collective-permute-start(f32[9,16,128]{2,1,0:T(8,128)S(1)} %get-tuple-element.54), channel_id=1, source_target_pairs={{1,2},{2,1},{5,6},{6,5},{9,10},{10,9},{13,14},{14,13},{17,18},{18,... | collective-permute-start | bytes 221192 | tf_op jit(solution)/shard_map/ppermute | solution.py:55
  23.6 7.1 %collective-permute-start.6 = (f32[3,8,128]{2,1,0:T(8,128)S(1)}, f32[3,8,128]{2,1,0:T(8,128)S(1)}, u32[]{:S(2)}, u32[]{:S(2)}) collective-permute-start(f32[3,8,128]{2,1,0:T(8,128)S(1)} %get-tuple-element.62), channel_id=1, source_target_pairs={{0,4},{4,0},{8,12},{12,8},{16,20},{20,16},{24,28},{28,24},{1,5},{5... | collective-permute-start | bytes 36872 | tf_op jit(solution)/shard_map/ppermute | solution.py:55
  26.4 4.3 %collective-permute-start.7 = (f32[3,8,128]{2,1,0:T(8,128)S(1)}, f32[3,8,128]{2,1,0:T(8,128)S(1)}, u32[]{:S(2)}, u32[]{:S(2)}) collective-permute-start(f32[3,8,128]{2,1,0:T(8,128)S(1)} %get-tuple-element.63), channel_id=1, source_target_pairs={{4,8},{8,4},{12,16},{16,12},{20,24},{24,20},{5,9},{9,5},{13,17},{1... | collective-permute-start | bytes 36872 | tf_op jit(solution)/shard_map/ppermute | solution.py:55
  27.1 3.6 %copy-start.1 = (f32[2,2,64,128]{3,2,1,0:T(8,128)S(1)}, f32[2,2,64,128]{3,2,1,0:T(8,128)}, u32[]{:S(2)}) copy-start(f32[2,2,64,128]{3,2,1,0:T(8,128)} %get-tuple-element.41.grid.g) | copy-start | bytes 393220

commit v6 on v5

--- a/solution.py
+++ b/solution.py
@@ -282,7 +282,7 @@
     return lambda off: ref[f, pl.ds(base + off, count), :]
 
 
-def interior(pack, g, bands, z, first_edge, second_edge, xacc, fbuf, prod, lhs, batch, also):
+def interior(pack, g, bands, kind, z, first_edge, second_edge, xacc, fbuf, prod, lhs, batch, also=None, build=None):
     count, reach, _ = pack.shape
     rows = reach - 2 * HALO
     mid, core = rows - HALO, rows - 2 * HALO
@@ -295,12 +295,13 @@
             edge[k, count + at, 0:HALO, :] = prod[k, start + size - HALO : start + size, :]
 
     def step(b, _):
-        level = b * batch // per_level
         for i in range(batch):
-            f = pack[b * batch + i, HALO : HALO + rows, :] * g[level]
+            if build is not None:
+                pack[b * batch + i, HALO : HALO + rows, :] = build(b, i, pack[b * batch + i, HALO : HALO + rows, :])
+            f = pack[b * batch + i, HALO : HALO + rows, :] * g[level_at(b, i, batch, per_level)]
             fbuf[i, 0:rows, :] = f
             split_into(lhs, i * rows, f)
-        band_products(lhs, bands, 0, prod, batch * rows)
+        band_products(lhs, bands, kind, prod, batch * rows)
         for i in range(batch):
             at = b * batch + i
             v = combine(rows_of(prod, i * rows, mid), field_rows(fbuf, i, mid), mid)
@@ -309,18 +310,19 @@
             split_into(lhs, i * mid, v)
             if also is not None:
                 also(b, i)
-        band_products(lhs, bands, 0, prod, batch * mid)
+        band_products(lhs, bands, kind, prod, batch * mid)
         for i in range(batch):
             at = b * batch + i
             v = combine(rows_of(prod, i * mid, core), field_rows(z, at, core, HALO), core)
             keep(second_edge, at, i * mid, mid)
+            level = level_at(b, i, batch, per_level)
             xacc[level, HALO : HALO + core, :] += v * pack[at, 2 * HALO : 2 * HALO + core, :]
         return 0
 
     lax.fori_loop(0, count // batch, step, 0)
 
 
-def edge_rows(pack, g, bands, z, first_edge, second_edge, xacc, ends, lhs):
+def edge_rows(pack, g, bands, kind, z, first_edge, second_edge, xacc, ends, lhs):
     count, reach, lanes = pack.shape
     rows = reach - 2 * HALO
     per_level = count // g.shape[0]
@@ -330,7 +332,7 @@
         for half in range(SWEEPS // 2):
             r = jnp.dot(
                 lhs[0 : 2 * count * HALO, :],
-                bands[0, :, half * 2 * lanes : (half + 1) * 2 * lanes],
+                bands[kind, :, half * 2 * lanes : (half + 1) * 2 * lanes],
                 preferred_element_type=F32,
             )
             for t in range(2):
@@ -415,13 +417,13 @@
 
 def interior_kernel(pack, g, bands, z, first_edge, second_edge, xacc, gbuf, fbuf, prod, lhs, *, batch):
     gbuf[...] = g[0] * KAPPA**SWEEPS
-    interior(pack, gbuf, bands, z, first_edge, second_edge, xacc, fbuf, prod, lhs, batch, None)
+    interior(pack, gbuf, bands, 0, z, first_edge, second_edge, xacc, fbuf, prod, lhs, batch)
 
 
 def edge_kernel(pack, g_ext, bands, *refs):
     z, first_edge, second_edge, xacc, gbuf, ends, lhs = refs[4:]
     gbuf[...] = g_ext[...] * KAPPA**SWEEPS
-    edge_rows(pack, gbuf, bands, z, first_edge, second_edge, xacc, ends, lhs)
+    edge_rows(pack, gbuf, bands, 0, z, first_edge, second_edge, xacc, ends, lhs)
 
 
 def put_edges(old, win, q):
@@ -443,7 +445,7 @@
         at = b * batch + i
         z_out[at] = put_edges(z_out[at], zw_one[b * (batch // 2) + i // 2], i % 2)
 
-    interior(pack, gbuf, bands, z, first_edge, second_edge, xacc, fbuf, prod, lhs, batch, first_edges)
+    interior(pack, gbuf, bands, 0, z, first_edge, second_edge, xacc, fbuf, prod, lhs, batch, first_edges)
 
 
 def join(main, win, cols):
@@ -453,12 +455,39 @@
     return jnp.where(lane < cols - HALO, state, turn(win, cols - 3 * WIDE)), win
 
 
-def first_kernel(
-    pack_in, g_ext, grid, near, far, near_ends, far_ends, bands, xmain,
-    pack, z, x, p, near_out, far_out, side, sums,
-    gbuf, fbuf, prod, lhs, xacc, west, east, *, batch,
+def window_build(west, east, batch):
+    def build(b, i, old):
+        u = b * (batch // 4) + i // 4
+        at = lanes_of(old) & (PAIR - 1)
+        old = jnp.where(at < WIDE, turn(west(u), -WIDE * (i % 4)), old)
+        return jnp.where(at >= 3 * WIDE, turn(east(u), 3 * WIDE - WIDE * (i % 4)), old)
+
+    return build
+
+
+def window_interior_kernel(
+    pack_in, grid, near, far, bands,
+    pack, z, first_edge, second_edge, xacc,
+    gbuf, fbuf, prod, lhs, *, batch,
 ):
     del pack_in
+    levels = grid.shape[1]
+    last = near.shape[0] - 1
+    west, east = by_parity("gx", far[last], near[last]), by_parity("gx", near[last], far[last])
+    for l in range(levels):
+        gbuf[l] = window_grid(grid[0, l], turn(west, -slot_lane(l)), turn(east, -slot_lane(l)))
+    build = window_build(
+        lambda u: by_parity("gx", far[u], near[u]), lambda u: by_parity("gx", near[u], far[u]), batch
+    )
+    interior(pack, gbuf, bands, 1, z, first_edge, second_edge, xacc, fbuf, prod, lhs, batch, None, build)
+
+
+def first_kernel(
+    pack_in, z_in, first_in, second_in, xacc_in, g_ext, grid, near, far, near_ends, far_ends, bands, xmain,
+    pack, z, first_edge, second_edge, xacc, x, p, near_out, far_out, side, sums,
+    gbuf, lhs, ends, west, east, *, batch,
+):
+    del pack_in, z_in, first_in, second_in, xacc_in
     levels, reach, cols = g_ext.shape
     rows = reach - 2 * HALO
     last = west.shape[0] - 1
@@ -470,15 +499,13 @@
         east[:, start : start + HALO, :] = by_parity("gx", a, b)
     for l in range(levels):
         gbuf[l] = window_grid(g_ext[l], turn(west[last], -slot_lane(l)), turn(east[last], -slot_lane(l)))
+    for start in (0, HALO + rows):
+        span = slice(start, start + HALO)
+        build = window_build(lambda u: west[u, span, :], lambda u: east[u, span, :], batch)
+        for i in range(pack.shape[0]):
+            pack[i, span, :] = build(0, i, pack[i, span, :])
+    edge_rows(pack, gbuf, bands, 1, z, first_edge, second_edge, xacc, ends, lhs)
     lane = lax.broadcasted_iota(jnp.int32, (reach, cols), 1)
-
-    def window(b, i, old):
-        u = b * (batch // 4) + i // 4
-        at = lane & (PAIR - 1)
-        old = jnp.where(at < WIDE, turn(west[u], -WIDE * (i % 4)), old)
-        return jnp.where(at >= 3 * WIDE, turn(east[u], 3 * WIDE - WIDE * (i % 4)), old)
-
-    covariance(pack, bands, 1, gbuf, z, xacc, fbuf, prod, lhs, batch, window)
     norm = jnp.zeros((8, cols), F32)
     curve = norm
     lane = lane[:rows]
@@ -539,7 +566,7 @@
             at = 2 * (b * batch + i) + q
             zm[at] = put_edges(zm[at], v, q)
 
-    edge_rows(mains, gbuf.at[0], bands, zm, first_edge, second_edge, xmain, ends, lhs)
+    edge_rows(mains, gbuf.at[0], bands, 0, zm, first_edge, second_edge, xmain, ends, lhs)
     covariance(wins, bands, 1, gbuf.at[1], zw, xacc, fbuf, prod, lhs, batch, None, second_edges)
     cross = jnp.zeros((8, cols), F32)
     curve = cross
@@ -671,22 +698,35 @@
     zm_one, _, _, xmain = call(
         edge_kernel, part_shapes, 7, (gbuf, ends, work[2]), input_output_aliases={3: 0, 4: 1, 5: 2, 6: 3}
     )(mains, g_ext, bands, *part)
-    wins, zw_one, x_one, p, near, far, side, sums = call(
+    win_edge = struct(SWEEPS, fields, 2 * HALO, cols)
+    win_parts = (win_shape, zw_shape, win_edge, win_edge, state_shape)
+    wins_part = call(
+        functools.partial(window_interior_kernel, batch=batch),
+        win_parts,
+        5,
+        (pltpu.VMEM((levels, rows, cols), F32), *work),
+        input_output_aliases={0: 0},
+    )(wins, grid, near_own, far_own, bands)
+    wins, zw_one, _, _, _, x_one, p, near, far, side, sums = call(
         functools.partial(first_kernel, batch=batch),
         (
-            win_shape,
-            zw_shape,
-            struct(levels, rows, cols),
-            struct(levels, rows, cols),
+            *win_parts,
+            state_shape,
+            state_shape,
             struct(levels + 1, HALO, cols),
             struct(levels + 1, HALO, cols),
             struct(rows, cols),
             struct(2, 8, cols),
         ),
-        9,
-        (gbuf, *work, pltpu.VMEM((levels, rows, cols), F32), *[pltpu.VMEM((strips, reach, cols), F32)] * 2),
-        input_output_aliases={0: 0},
-    )(wins, g_ext, grid, near_own, far_own, near, far, bands, xmain)
+        13,
+        (
+            gbuf,
+            work[2],
+            pltpu.VMEM((fields, 2 * HALO, cols), F32),
+            *[pltpu.VMEM((strips, reach, cols), F32)] * 2,
+        ),
+        input_output_aliases={i: i for i in range(5)},
+    )(*wins_part, g_ext, grid, near_own, far_own, near, far, bands, xmain)
     near, far = swap(near, "gy", 0), swap(far, "gy", 1)
     *part, zm_one = call(
         functools.partial(second_interior_kernel, batch=batch),

time: 53 us -> 51.3 us (0.968)
  blocking collectives: 17.3 us -> 15.2 us
    all_to_all x1, blocking collectives: 17.3 us -> 15.2 us  [on_device(): share = lax.all_to_all(share, ('gy', 'gx'), 0, 0, tiled=True)]
    pallas_call x1 -> x2, Pallas kernels: 2.65 us -> 3.04 us  [the longest x1 2.03 us: on_device(): call(functools.partial(window_interior_kernel, batch=batch), win_parts, 5...]
  transfers between devices with their start and end apart: 8 -> 8, of which waited for: 1 -> 1; matrix products, arithmetic and copies ran while one was open for 0% -> 0% of each run, Pallas kernels for 21% -> 25%
where the time goes in v6:
time: 51.3 us; the launch traced here: 51.1 us
  Pallas kernels  21.5 us (42%)
  blocking collectives  15.2 us (30%)
  starting transfers between devices  8.57 us (17%)
  waiting for transfers between devices  4.1 us (8%)
  local copies, waits for them, and re-layouts  0.91 us (2%)
  between operations  0.83 us (2%)
    all_to_all x1, blocking collectives, on_device(): share = lax.all_to_all(share, ('gy', 'gx'), 0, 0, tiled=True)  15.2 us
    ppermute x8, starting transfers between devices, swap(): lax.ppermute(x, axis, [(i + a, i + 1 - a) for i in range(odd, count - 1,...  8.57 us
    ppermute x8, waiting for transfers between devices, swap(): lax.ppermute(x, axis, [(i + a, i + 1 - a) for i in range(odd, count - 1,...  4.1 us
    pallas_call x1, Pallas kernels, on_device(): call(functools.partial(second_interior_kernel, batch=batch), (*part_shape...  3.59 us
    pallas_call x1, Pallas kernels, on_device(): call(functools.partial(interior_kernel, batch=batch), part_shapes, 3, (pl...  3.46 us
    pallas_call x1, Pallas kernels, on_device(): call(functools.partial(second_kernel, batch=batch), (state_shape, struct(...  3.24 us
    pallas_call x1, Pallas kernels, on_device(): call(scatter_kernel, (struct(2, levels, rows, cols), struct(fields + leve...  2.72 us
    pallas_call x1, Pallas kernels, on_device(): call(functools.partial(window_interior_kernel, batch=batch), win_parts, 5...  2.03 us
  transfers between devices with their start and end apart: 8, of which 1 were waited for; matrix products, arithmetic and copies ran while one was open for 0% of the time, Pallas kernels for 25%

profile of v6, /device:TPU:0, one launch (start us, length us, event | category | flops | bytes accessed | tf_op | source)
XLA Modules:
  0.0 51.1 jit_solution(4305636345042573214)
XLA Ops:
  0.6 0.0 copy-start.3
  0.6 0.0 copy-start.2
  0.7 2.7 %shard_map.77 = (f32[2,2,64,128]{3,2,1,0:T(8,128)}, f32[66,8,128]{2,1,0:T(8,128)}, f32[66,8,128]{2,1,0:T(8,128)}) custom-call(bf16[32,2,64,128]{3,2,1,0:T(8,128)(2,1)} %ens_in.1, s32[1,1,2048]{2,1,0:T(1,128)} %cell_in.1, s32[1,1,2048]{2,1,0:T(1,128)} %level_in.1, f32[1,1,2048]{2,1,0:T(1,128)} %innov_in.1, f32[1,1,2048]{2,1,0:T(1,128)} %weight_in.1), custom_call_target="tpu_custom_call" | custom-call | flops 2000000000 | bytes 1000000 | tf_op jit(solution)/shard_map/pallas_call | solution.py:651
  3.4 3.0 %collective-permute-start = (f32[66,8,128]{2,1,0:T(8,128)}, f32[66,8,128]{2,1,0:T(8,128)S(1)}, u32[]{:S(2)}, u32[]{:S(2)}) collective-permute-start(f32[66,8,128]{2,1,0:T(8,128)} %get-tuple-element.44), channel_id=1, source_target_pairs={{0,4},{4,0},{8,12},{12,8},{16,20},{20,16},{24,28},{28,24},{1,5},{5... | collective-permute-start | bytes 811016 | tf_op jit(solution)/shard_map/ppermute | solution.py:55
  6.4 0.7 %collective-permute-start.1 = (f32[66,8,128]{2,1,0:T(8,128)}, f32[66,8,128]{2,1,0:T(8,128)S(1)}, u32[]{:S(2)}, u32[]{:S(2)}) collective-permute-start(f32[66,8,128]{2,1,0:T(8,128)} %get-tuple-element.45), channel_id=1, source_target_pairs={{4,8},{8,4},{12,16},{16,12},{20,24},{24,20},{5,9},{9,5},{13,17},{1... | collective-permute-start | bytes 811016 | tf_op jit(solution)/shard_map/ppermute | solution.py:55
  7.1 0.0 copy-done.3
  7.1 0.9 %copy-done = f32[2,2,64,128]{3,2,1,0:T(8,128)S(1)} copy-done((f32[2,2,64,128]{3,2,1,0:T(8,128)S(1)}, f32[2,2,64,128]{3,2,1,0:T(8,128)}, u32[]{:S(2)}) %copy-start) | copy-done | bytes 131096
  8.0 1.9 %shard_map.78 = (f32[64,80,128]{2,1,0:T(8,128)S(1)}, f32[32,80,128]{2,1,0:T(8,128)S(1)}, f32[9,64,128]{2,1,0:T(8,128)S(1)}, f32[9,64,128]{2,1,0:T(8,128)S(1)}, f...) custom-call(bf16[32,2,64,128]{3,2,1,0:T(8,128)(2,1)S(1)} %copy-done.2, ...), custom_call_target="tpu_custom_call" | custom-call | flops 2000000000 | bytes 1000000 | tf_op jit(solution)/shard_map/pallas_call | solution.py:662
  9.9 0.1 collective-permute-start.2
  10.0 0.7 %collective-permute-start.3 = (f32[9,64,128]{2,1,0:T(8,128)S(1)}, f32[9,64,128]{2,1,0:T(8,128)S(1)}, u32[]{:S(2)}, u32[]{:S(2)}) collective-permute-start(f32[9,64,128]{2,1,0:T(8,128)S(1)} %get-tuple-element.56), channel_id=1, source_target_pairs={{1,2},{2,1},{5,6},{6,5},{9,10},{10,9},{13,14},{14,13},{17,18},{18,... | collective-permute-start | bytes 884744 | tf_op jit(solution)/shard_map/ppermute | solution.py:55
  10.7 3.5 %shard_map.79 = (f32[64,72,128]{2,1,0:T(8,128)S(1)}, f32[4,128,16,128]{3,2,1,0:T(8,128)S(1)}, f32[4,128,16,128]{3,2,1,0:T(8,128)S(1)}, f32[2,64,128]{2,1,0:T(8,128)S(1)}) custom-call(f32[64,80,128]{2,1,0:T(8,128)S(1)} %get-tuple-element.48.pack.refs_0_, f32[2,2,64,128]{3,2,1,0:T(8,128)S(1)} %copy-done, bf16[2,256,512]{2,1,0:T(8,128)(2,1)S(1)} %get-tuple-element.51.bands), custom_call_target="tpu_custom_call" | custom-call | flops 2000000000 | bytes 1000000 | tf_op jit(solution)/shard_map/pallas_call | solution.py:687
  14.2 4.1 %collective-permute-done.from_near = f32[66,8,128]{2,1,0:T(8,128)S(1)} collective-permute-done((f32[66,8,128]{2,1,0:T(8,128)}, f32[66,8,128]{2,1,0:T(8,128)S(1)}, u32[]{:S(2)}, u32[]{:S(2)}) %collective-permute-start) | collective-permute-done | bytes 270368 | tf_op jit(solution)/shard_map/ppermute | solution.py:55
  18.3 0.0 collective-permute-done.1.from_far
  18.3 1.1 %shard_map.80 = (f32[64,80,128]{2,1,0:T(8,128)S(1)}, f32[32,80,128]{2,1,0:T(8,128)S(1)}, f32[2,80,128]{2,1,0:T(8,128)S(1)}, f32[9,16,128]{2,1,0:T(8,128)S(1)}, f32[9,16,128]{2,1,0:T(8,128)S(1)}) custom-call(f32[66,8,128]{2,1,0:T(8,128)S(1)} %collective-permute-done.from_near, ...), custom_call_target="tpu_custom_call", output_to_operand_aliasing={{0}: (3, {}), {1}: (4, {}), {2}: (5, {})} | custom-call | flops 2000000000 | bytes 1000000 | tf_op jit(solution)/shard_map/pallas_call | solution.py:693
  19.3 0.0 collective-permute-start.4
  19.3 0.7 %collective-permute-start.5 = (f32[9,16,128]{2,1,0:T(8,128)S(1)}, f32[9,16,128]{2,1,0:T(8,128)S(1)}, u32[]{:S(2)}, u32[]{:S(2)}) collective-permute-start(f32[9,16,128]{2,1,0:T(8,128)S(1)} %get-tuple-element.64), channel_id=1, source_target_pairs={{1,2},{2,1},{5,6},{6,5},{9,10},{10,9},{13,14},{14,13},{17,18},{18,... | collective-permute-start | bytes 221192 | tf_op jit(solution)/shard_map/ppermute | solution.py:55
  20.0 0.9 %shard_map.82 = (f32[64,72,128]{2,1,0:T(8,128)S(1)}, f32[4,128,16,128]{3,2,1,0:T(8,128)S(1)}, f32[4,128,16,128]{3,2,1,0:T(8,128)S(1)}, f32[2,64,128]{2,1,0:T(8,128)S(1)}) custom-call(f32[64,80,128]{2,1,0:T(8,128)S(1)} %get-tuple-element.53.pack.mains, ...), custom_call_target="tpu_custom_call", output_to_operand_aliasing={{0}: (3, {}), {1}: (4, {}), {2}: (5, {}), {3}: (6, {})} | custom-call | flops 2000000000 | bytes 1000000 | tf_op jit(solution)/shard_map/pallas_call | solution.py:698
  20.9 0.0 collective-permute-done.2.near
  20.9 0.0 collective-permute-done.3.far
  21.0 2.0 %shard_map.81 = (f32[32,80,128]{2,1,0:T(8,128)S(1)}, f32[32,72,128]{2,1,0:T(8,128)S(1)}, f32[4,64,16,128]{3,2,1,0:T(8,128)S(1)}, f32[4,64,16,128]{3,2,1,0:T(8,128)S(1)}, f32[2,64,128]{2,1,0:T(8,128)S(1)}) custom-call(f32[32,80,128]{2,1,0:T(8,128)S(1)} %get-tuple-element.54.pack_in, f32[2,2,64,128]{3,2,1,0:T(8,128)S(1)} %copy-done, ...), custom_call_target="tpu_custom_call", output_to_operand_aliasing={{0}: (0, {})} | custom-call | flops 2000000000 | bytes 1000000 | tf_op jit(solution)/shard_map/pallas_call | solution.py:703
  23.0 0.0 collective-permute-done.4.near_ends
  23.0 0.0 collective-permute-done.5.far_ends
  23.0 1.0 %shard_map.83 = (f32[32,80,128]{2,1,0:T(8,128)S(1)}, f32[32,72,128]{2,1,0:T(8,128)S(1)}, f32[4,64,16,128]{3,2,1,0:T(8,128)S(1)}, f32[4,64,16,128]{3,2,1,0:T(8,12...) custom-call(f32[32,80,128]{2,1,0:T(8,128)S(1)} %get-tuple-element.57, ...), custom_call_target="tpu_custom_call", output_to_operand_aliasing={{0}: (0, {}), {1}: (1, {}), {2}: (2, {}), {3}: (3, {}), {4}... | custom-call | flops 2000000000 | bytes 1000000 | tf_op jit(solution)/shard_map/pallas_call | solution.py:710
  24.0 2.8 %collective-permute-start.6 = (f32[3,8,128]{2,1,0:T(8,128)S(1)}, f32[3,8,128]{2,1,0:T(8,128)S(1)}, u32[]{:S(2)}, u32[]{:S(2)}) collective-permute-start(f32[3,8,128]{2,1,0:T(8,128)S(1)} %get-tuple-element.72), channel_id=1, source_target_pairs={{0,4},{4,0},{8,12},{12,8},{16,20},{20,16},{24,28},{28,24},{1,5},{5... | collective-permute-start | bytes 36872 | tf_op jit(solution)/shard_map/ppermute | solution.py:55
  26.8 0.7 %collective-permute-start.7 = (f32[3,8,128]{2,1,0:T(8,128)S(1)}, f32[3,8,128]{2,1,0:T(8,128)S(1)}, u32[]{:S(2)}, u32[]{:S(2)}) collective-permute-start(f32[3,8,128]{2,1,0:T(8,128)S(1)} %get-tuple-element.73), channel_id=1, source_target_pairs={{4,8},{8,4},{12,16},{16,12},{20,24},{24,20},{5,9},{9,5},{13,17},{1... | collective-permute-start | bytes 36872 | tf_op jit(solution)/shard_map/ppermute | solution.py:55
  27.5 0.0 copy-start.1
  27.5 3.6 %shard_map.84 = (f32[64,72,128]{2,1,0:T(8,128)S(1)}, f32[4,128,16,128]{3,2,1,0:T(8,128)S(1)}, f32[4,128,16,128]{3,2,1,0:T(8,128)S(1)}, f32[2,64,128]{2,1,0:T(8,128)S(1)}, f32[64,72,128]{2,1,0:T(8,128)S(1)}) custom-call(f32[64,80,128]{2,1,0:T(8,128)S(1)} %get-tuple-element.53.pack.mains, ...), custom_call_target="tpu_custom_call", output_to_operand_aliasing={{4}: (3, {})} | custom-call | flops 2000000000 | bytes 1000000 | tf_op jit(solution)/shard_map/pallas_call | solution.py:731
  31.1 0.0 collective-permute-done.6.near
  31.1 0.0 collective-permute-done.7.far
  31.1 3.2 %shard_map.85 = (f32[2,64,128]{2,1,0:T(8,128)S(1)}, f32[32,128]{1,0:T(8,128)S(1)}, f32[64,72,128]{2,1,0:T(8,128)S(1)}, f32[4,128,16,128]{3,2,1,0:T(8,128)S(1)}, ...) custom-call(f32[64,80,128]{2,1,0:T(8,128)S(1)} %get-tuple-element.53, ...), custom_call_target="tpu_custom_call", output_to_operand_aliasing={{2}: (9, {}), {3}: (10, {}), {4}: (11, {}), {5}: (12, {})} | custom-call | flops 2000000000 | bytes 1000000 | tf_op jit(solution)/shard_map/pallas_call | solution.py:738
  34.4 15.2 %all_to_all.11 = f32[32,1,128]{2,1,0:T(1,128)S(1)} all-to-all(f32[32,1,128]{2,1,0:T(1,128)S(1)} %bitcast.5), channel_id=1, replica_groups=mesh['gy'=8,'gx'=4] {'gy','gx'}, dimensions={0} | all-to-all | bytes 32768 | tf_op jit(solution)/shard_map/all_to_all | solution.py:752
  49.6 1.5 %shard_map.86 = (f32[32,2,64,128]{3,2,1,0:T(8,128)}, f32[2,64,128]{2,1,0:T(8,128)}) custom-call(f32[32,128]{1,0:T(8,128)S(1)} %bitcast.4, f32[64,72,128]{2,1,0:T(8,128)S(1)} %get-tuple-element.82.z_one, f32[64,72,128]{2,1,0:T(8,128)S(1)} %get-tuple-element.83.z_two, f32[2,64,128]{2,1,0:T(8,128)S(1)} %get-tuple-element.84.x_one, ...), custom_call_target="tpu_custom_call" | custom-call | tf_op jit(solution)/shard_map/pallas_call | solution.py:754
  (3 shorter events, 0.0 us)
Async XLA Ops:
  0.6 6.5 %copy-start.3 = (bf16[4,2,128,512]{3,2,1,0:T(8,128)(2,1)S(1)}, bf16[4,2,128,512]{3,2,1,0:T(8,128)(2,1)}, u32[]{:S(2)}) copy-start(bf16[4,2,128,512]{3,2,1,0:T(8,128)(2,1)} %constant.2.clone.bands_in) | copy-start | bytes 3145732
  0.6 6.5 %copy-start.2 = (bf16[32,2,64,128]{3,2,1,0:T(8,128)(2,1)S(1)}, bf16[32,2,64,128]{3,2,1,0:T(8,128)(2,1)}, u32[]{:S(2)}) copy-start(bf16[32,2,64,128]{3,2,1,0:T(8,128)(2,1)} %ens_in.1) | copy-start | bytes 3145732
  3.4 14.9 %collective-permute-start = (f32[66,8,128]{2,1,0:T(8,128)}, f32[66,8,128]{2,1,0:T(8,128)S(1)}, u32[]{:S(2)}, u32[]{:S(2)}) collective-permute-start(f32[66,8,128]{2,1,0:T(8,128)} %get-tuple-element.44), channel_id=1, source_target_pairs={{0,4},{4,0},{8,12},{12,8},{16,20},{20,16},{24,28},{28,24},{1,5},{5... | collective-permute-start | bytes 811016 | tf_op jit(solution)/shard_map/ppermute | solution.py:55
  6.4 11.9 %collective-permute-start.1 = (f32[66,8,128]{2,1,0:T(8,128)}, f32[66,8,128]{2,1,0:T(8,128)S(1)}, u32[]{:S(2)}, u32[]{:S(2)}) collective-permute-start(f32[66,8,128]{2,1,0:T(8,128)} %get-tuple-element.45), channel_id=1, source_target_pairs={{4,8},{8,4},{12,16},{16,12},{20,24},{24,20},{5,9},{9,5},{13,17},{1... | collective-permute-start | bytes 811016 | tf_op jit(solution)/shard_map/ppermute | solution.py:55
  7.1 0.9 %copy-start = (f32[2,2,64,128]{3,2,1,0:T(8,128)S(1)}, f32[2,2,64,128]{3,2,1,0:T(8,128)}, u32[]{:S(2)}) copy-start(f32[2,2,64,128]{3,2,1,0:T(8,128)} %get-tuple-element.46.grid.g) | copy-start | bytes 393220
  9.9 11.0 %collective-permute-start.2 = (f32[9,64,128]{2,1,0:T(8,128)S(1)}, f32[9,64,128]{2,1,0:T(8,128)S(1)}, u32[]{:S(2)}, u32[]{:S(2)}) collective-permute-start(f32[9,64,128]{2,1,0:T(8,128)S(1)} %get-tuple-element.55), channel_id=1, source_target_pairs={{0,1},{1,0},{2,3},{3,2},{4,5},{5,4},{6,7},{7,6},{8,9},{9,8},{10,11... | collective-permute-start | bytes 884744 | tf_op jit(solution)/shard_map/ppermute | solution.py:55
  10.0 10.9 %collective-permute-start.3 = (f32[9,64,128]{2,1,0:T(8,128)S(1)}, f32[9,64,128]{2,1,0:T(8,128)S(1)}, u32[]{:S(2)}, u32[]{:S(2)}) collective-permute-start(f32[9,64,128]{2,1,0:T(8,128)S(1)} %get-tuple-element.56), channel_id=1, source_target_pairs={{1,2},{2,1},{5,6},{6,5},{9,10},{10,9},{13,14},{14,13},{17,18},{18,... | collective-permute-start | bytes 884744 | tf_op jit(solution)/shard_map/ppermute | solution.py:55
  19.3 3.7 %collective-permute-start.4 = (f32[9,16,128]{2,1,0:T(8,128)S(1)}, f32[9,16,128]{2,1,0:T(8,128)S(1)}, u32[]{:S(2)}, u32[]{:S(2)}) collective-permute-start(f32[9,16,128]{2,1,0:T(8,128)S(1)} %get-tuple-element.63), channel_id=1, source_target_pairs={{0,1},{1,0},{2,3},{3,2},{4,5},{5,4},{6,7},{7,6},{8,9},{9,8},{10,11... | collective-permute-start | bytes 221192 | tf_op jit(solution)/shard_map/ppermute | solution.py:55
  19.3 3.7 %collective-permute-start.5 = (f32[9,16,128]{2,1,0:T(8,128)S(1)}, f32[9,16,128]{2,1,0:T(8,128)S(1)}, u32[]{:S(2)}, u32[]{:S(2)}) collective-permute-start(f32[9,16,128]{2,1,0:T(8,128)S(1)} %get-tuple-element.64), channel_id=1, source_target_pairs={{1,2},{2,1},{5,6},{6,5},{9,10},{10,9},{13,14},{14,13},{17,18},{18,... | collective-permute-start | bytes 221192 | tf_op jit(solution)/shard_map/ppermute | solution.py:55
  24.0 7.1 %collective-permute-start.6 = (f32[3,8,128]{2,1,0:T(8,128)S(1)}, f32[3,8,128]{2,1,0:T(8,128)S(1)}, u32[]{:S(2)}, u32[]{:S(2)}) collective-permute-start(f32[3,8,128]{2,1,0:T(8,128)S(1)} %get-tuple-element.72), channel_id=1, source_target_pairs={{0,4},{4,0},{8,12},{12,8},{16,20},{20,16},{24,28},{28,24},{1,5},{5... | collective-permute-start | bytes 36872 | tf_op jit(solution)/shard_map/ppermute | solution.py:55
  26.8 4.3 %collective-permute-start.7 = (f32[3,8,128]{2,1,0:T(8,128)S(1)}, f32[3,8,128]{2,1,0:T(8,128)S(1)}, u32[]{:S(2)}, u32[]{:S(2)}) collective-permute-start(f32[3,8,128]{2,1,0:T(8,128)S(1)} %get-tuple-element.73), channel_id=1, source_target_pairs={{4,8},{8,4},{12,16},{16,12},{20,24},{24,20},{5,9},{9,5},{13,17},{1... | collective-permute-start | bytes 36872 | tf_op jit(solution)/shard_map/ppermute | solution.py:55
  27.5 3.6 %copy-start.1 = (f32[2,2,64,128]{3,2,1,0:T(8,128)S(1)}, f32[2,2,64,128]{3,2,1,0:T(8,128)}, u32[]{:S(2)}) copy-start(f32[2,2,64,128]{3,2,1,0:T(8,128)} %get-tuple-element.46.grid.g) | copy-start | bytes 393220

commit v7 on v6

--- a/solution.py
+++ b/solution.py
@@ -606,7 +606,7 @@
             stage[f] = coef_a * one + coef_b * two
             return 0
 
-        lax.fori_loop(0, part, body, 0, unroll=4)
+        lax.fori_loop(0, part, body, 0, unroll=True)
         level, first = divmod(c * part, members)
         copies.append(
             pltpu.make_async_copy(

time: 51.3 us -> 51.3 us (level)
  no operation moved by 1% of the time
where the time goes in v7:
time: 51.3 us; the launch traced here: 51.1 us
  Pallas kernels  21.5 us (42%)
  blocking collectives  15.2 us (30%)
  starting transfers between devices  8.57 us (17%)
  waiting for transfers between devices  4.1 us (8%)
  local copies, waits for them, and re-layouts  0.91 us (2%)
  between operations  0.83 us (2%)
    all_to_all x1, blocking collectives, on_device(): share = lax.all_to_all(share, ('gy', 'gx'), 0, 0, tiled=True)  15.2 us
    ppermute x8, starting transfers between devices, swap(): lax.ppermute(x, axis, [(i + a, i + 1 - a) for i in range(odd, count - 1,...  8.57 us
    ppermute x8, waiting for transfers between devices, swap(): lax.ppermute(x, axis, [(i + a, i + 1 - a) for i in range(odd, count - 1,...  4.1 us
    pallas_call x1, Pallas kernels, on_device(): call(functools.partial(second_interior_kernel, batch=batch), (*part_shape...  3.59 us
    pallas_call x1, Pallas kernels, on_device(): call(functools.partial(interior_kernel, batch=batch), part_shapes, 3, (pl...  3.46 us
    pallas_call x1, Pallas kernels, on_device(): call(functools.partial(second_kernel, batch=batch), (state_shape, struct(...  3.24 us
    pallas_call x1, Pallas kernels, on_device(): call(scatter_kernel, (struct(2, levels, rows, cols), struct(fields + leve...  2.72 us
    pallas_call x1, Pallas kernels, on_device(): call(functools.partial(window_interior_kernel, batch=batch), win_parts, 5...  2.03 us
  transfers between devices with their start and end apart: 8, of which 1 were waited for; matrix products, arithmetic and copies ran while one was open for 0% of the time, Pallas kernels for 25%

profile of v7, /device:TPU:0, one launch (start us, length us, event | category | flops | bytes accessed | tf_op | source)
XLA Modules:
  0.0 51.1 jit_solution(12953393014707610894)
XLA Ops:
  0.6 0.0 copy-start.3
  0.6 0.0 copy-start.2
  0.7 2.7 %shard_map.77 = (f32[2,2,64,128]{3,2,1,0:T(8,128)}, f32[66,8,128]{2,1,0:T(8,128)}, f32[66,8,128]{2,1,0:T(8,128)}) custom-call(bf16[32,2,64,128]{3,2,1,0:T(8,128)(2,1)} %ens_in.1, s32[1,1,2048]{2,1,0:T(1,128)} %cell_in.1, s32[1,1,2048]{2,1,0:T(1,128)} %level_in.1, f32[1,1,2048]{2,1,0:T(1,128)} %innov_in.1, f32[1,1,2048]{2,1,0:T(1,128)} %weight_in.1), custom_call_target="tpu_custom_call" | custom-call | flops 2000000000 | bytes 1000000 | tf_op jit(solution)/shard_map/pallas_call | solution.py:651
  3.4 3.0 %collective-permute-start = (f32[66,8,128]{2,1,0:T(8,128)}, f32[66,8,128]{2,1,0:T(8,128)S(1)}, u32[]{:S(2)}, u32[]{:S(2)}) collective-permute-start(f32[66,8,128]{2,1,0:T(8,128)} %get-tuple-element.44), channel_id=1, source_target_pairs={{0,4},{4,0},{8,12},{12,8},{16,20},{20,16},{24,28},{28,24},{1,5},{5... | collective-permute-start | bytes 811016 | tf_op jit(solution)/shard_map/ppermute | solution.py:55
  6.4 0.7 %collective-permute-start.1 = (f32[66,8,128]{2,1,0:T(8,128)}, f32[66,8,128]{2,1,0:T(8,128)S(1)}, u32[]{:S(2)}, u32[]{:S(2)}) collective-permute-start(f32[66,8,128]{2,1,0:T(8,128)} %get-tuple-element.45), channel_id=1, source_target_pairs={{4,8},{8,4},{12,16},{16,12},{20,24},{24,20},{5,9},{9,5},{13,17},{1... | collective-permute-start | bytes 811016 | tf_op jit(solution)/shard_map/ppermute | solution.py:55
  7.1 0.0 copy-done.3
  7.1 0.9 %copy-done = f32[2,2,64,128]{3,2,1,0:T(8,128)S(1)} copy-done((f32[2,2,64,128]{3,2,1,0:T(8,128)S(1)}, f32[2,2,64,128]{3,2,1,0:T(8,128)}, u32[]{:S(2)}) %copy-start) | copy-done | bytes 131096
  8.0 1.9 %shard_map.78 = (f32[64,80,128]{2,1,0:T(8,128)S(1)}, f32[32,80,128]{2,1,0:T(8,128)S(1)}, f32[9,64,128]{2,1,0:T(8,128)S(1)}, f32[9,64,128]{2,1,0:T(8,128)S(1)}, f...) custom-call(bf16[32,2,64,128]{3,2,1,0:T(8,128)(2,1)S(1)} %copy-done.2, ...), custom_call_target="tpu_custom_call" | custom-call | flops 2000000000 | bytes 1000000 | tf_op jit(solution)/shard_map/pallas_call | solution.py:662
  9.9 0.1 collective-permute-start.2
  10.0 0.7 %collective-permute-start.3 = (f32[9,64,128]{2,1,0:T(8,128)S(1)}, f32[9,64,128]{2,1,0:T(8,128)S(1)}, u32[]{:S(2)}, u32[]{:S(2)}) collective-permute-start(f32[9,64,128]{2,1,0:T(8,128)S(1)} %get-tuple-element.56), channel_id=1, source_target_pairs={{1,2},{2,1},{5,6},{6,5},{9,10},{10,9},{13,14},{14,13},{17,18},{18,... | collective-permute-start | bytes 884744 | tf_op jit(solution)/shard_map/ppermute | solution.py:55
  10.7 3.5 %shard_map.79 = (f32[64,72,128]{2,1,0:T(8,128)S(1)}, f32[4,128,16,128]{3,2,1,0:T(8,128)S(1)}, f32[4,128,16,128]{3,2,1,0:T(8,128)S(1)}, f32[2,64,128]{2,1,0:T(8,128)S(1)}) custom-call(f32[64,80,128]{2,1,0:T(8,128)S(1)} %get-tuple-element.48.pack.refs_0_, f32[2,2,64,128]{3,2,1,0:T(8,128)S(1)} %copy-done, bf16[2,256,512]{2,1,0:T(8,128)(2,1)S(1)} %get-tuple-element.51.bands), custom_call_target="tpu_custom_call" | custom-call | flops 2000000000 | bytes 1000000 | tf_op jit(solution)/shard_map/pallas_call | solution.py:687
  14.2 4.1 %collective-permute-done.from_near = f32[66,8,128]{2,1,0:T(8,128)S(1)} collective-permute-done((f32[66,8,128]{2,1,0:T(8,128)}, f32[66,8,128]{2,1,0:T(8,128)S(1)}, u32[]{:S(2)}, u32[]{:S(2)}) %collective-permute-start) | collective-permute-done | bytes 270368 | tf_op jit(solution)/shard_map/ppermute | solution.py:55
  18.3 0.0 collective-permute-done.1.from_far
  18.3 1.1 %shard_map.80 = (f32[64,80,128]{2,1,0:T(8,128)S(1)}, f32[32,80,128]{2,1,0:T(8,128)S(1)}, f32[2,80,128]{2,1,0:T(8,128)S(1)}, f32[9,16,128]{2,1,0:T(8,128)S(1)}, f32[9,16,128]{2,1,0:T(8,128)S(1)}) custom-call(f32[66,8,128]{2,1,0:T(8,128)S(1)} %collective-permute-done.from_near, ...), custom_call_target="tpu_custom_call", output_to_operand_aliasing={{0}: (3, {}), {1}: (4, {}), {2}: (5, {})} | custom-call | flops 2000000000 | bytes 1000000 | tf_op jit(solution)/shard_map/pallas_call | solution.py:693
  19.3 0.0 collective-permute-start.4
  19.3 0.7 %collective-permute-start.5 = (f32[9,16,128]{2,1,0:T(8,128)S(1)}, f32[9,16,128]{2,1,0:T(8,128)S(1)}, u32[]{:S(2)}, u32[]{:S(2)}) collective-permute-start(f32[9,16,128]{2,1,0:T(8,128)S(1)} %get-tuple-element.64), channel_id=1, source_target_pairs={{1,2},{2,1},{5,6},{6,5},{9,10},{10,9},{13,14},{14,13},{17,18},{18,... | collective-permute-start | bytes 221192 | tf_op jit(solution)/shard_map/ppermute | solution.py:55
  20.0 0.9 %shard_map.82 = (f32[64,72,128]{2,1,0:T(8,128)S(1)}, f32[4,128,16,128]{3,2,1,0:T(8,128)S(1)}, f32[4,128,16,128]{3,2,1,0:T(8,128)S(1)}, f32[2,64,128]{2,1,0:T(8,128)S(1)}) custom-call(f32[64,80,128]{2,1,0:T(8,128)S(1)} %get-tuple-element.53.pack.mains, ...), custom_call_target="tpu_custom_call", output_to_operand_aliasing={{0}: (3, {}), {1}: (4, {}), {2}: (5, {}), {3}: (6, {})} | custom-call | flops 2000000000 | bytes 1000000 | tf_op jit(solution)/shard_map/pallas_call | solution.py:698
  20.9 0.0 collective-permute-done.2.near
  20.9 0.0 collective-permute-done.3.far
  21.0 2.0 %shard_map.81 = (f32[32,80,128]{2,1,0:T(8,128)S(1)}, f32[32,72,128]{2,1,0:T(8,128)S(1)}, f32[4,64,16,128]{3,2,1,0:T(8,128)S(1)}, f32[4,64,16,128]{3,2,1,0:T(8,128)S(1)}, f32[2,64,128]{2,1,0:T(8,128)S(1)}) custom-call(f32[32,80,128]{2,1,0:T(8,128)S(1)} %get-tuple-element.54.pack_in, f32[2,2,64,128]{3,2,1,0:T(8,128)S(1)} %copy-done, ...), custom_call_target="tpu_custom_call", output_to_operand_aliasing={{0}: (0, {})} | custom-call | flops 2000000000 | bytes 1000000 | tf_op jit(solution)/shard_map/pallas_call | solution.py:703
  23.0 0.0 collective-permute-done.4.near_ends
  23.0 0.0 collective-permute-done.5.far_ends
  23.0 1.0 %shard_map.83 = (f32[32,80,128]{2,1,0:T(8,128)S(1)}, f32[32,72,128]{2,1,0:T(8,128)S(1)}, f32[4,64,16,128]{3,2,1,0:T(8,128)S(1)}, f32[4,64,16,128]{3,2,1,0:T(8,12...) custom-call(f32[32,80,128]{2,1,0:T(8,128)S(1)} %get-tuple-element.57, ...), custom_call_target="tpu_custom_call", output_to_operand_aliasing={{0}: (0, {}), {1}: (1, {}), {2}: (2, {}), {3}: (3, {}), {4}... | custom-call | flops 2000000000 | bytes 1000000 | tf_op jit(solution)/shard_map/pallas_call | solution.py:710
  24.0 2.8 %collective-permute-start.6 = (f32[3,8,128]{2,1,0:T(8,128)S(1)}, f32[3,8,128]{2,1,0:T(8,128)S(1)}, u32[]{:S(2)}, u32[]{:S(2)}) collective-permute-start(f32[3,8,128]{2,1,0:T(8,128)S(1)} %get-tuple-element.72), channel_id=1, source_target_pairs={{0,4},{4,0},{8,12},{12,8},{16,20},{20,16},{24,28},{28,24},{1,5},{5... | collective-permute-start | bytes 36872 | tf_op jit(solution)/shard_map/ppermute | solution.py:55
  26.8 0.7 %collective-permute-start.7 = (f32[3,8,128]{2,1,0:T(8,128)S(1)}, f32[3,8,128]{2,1,0:T(8,128)S(1)}, u32[]{:S(2)}, u32[]{:S(2)}) collective-permute-start(f32[3,8,128]{2,1,0:T(8,128)S(1)} %get-tuple-element.73), channel_id=1, source_target_pairs={{4,8},{8,4},{12,16},{16,12},{20,24},{24,20},{5,9},{9,5},{13,17},{1... | collective-permute-start | bytes 36872 | tf_op jit(solution)/shard_map/ppermute | solution.py:55
  27.5 0.0 copy-start.1
  27.5 3.6 %shard_map.84 = (f32[64,72,128]{2,1,0:T(8,128)S(1)}, f32[4,128,16,128]{3,2,1,0:T(8,128)S(1)}, f32[4,128,16,128]{3,2,1,0:T(8,128)S(1)}, f32[2,64,128]{2,1,0:T(8,128)S(1)}, f32[64,72,128]{2,1,0:T(8,128)S(1)}) custom-call(f32[64,80,128]{2,1,0:T(8,128)S(1)} %get-tuple-element.53.pack.mains, ...), custom_call_target="tpu_custom_call", output_to_operand_aliasing={{4}: (3, {})} | custom-call | flops 2000000000 | bytes 1000000 | tf_op jit(solution)/shard_map/pallas_call | solution.py:731
  31.1 0.0 collective-permute-done.6.near
  31.1 0.0 collective-permute-done.7.far
  31.1 3.2 %shard_map.85 = (f32[2,64,128]{2,1,0:T(8,128)S(1)}, f32[32,128]{1,0:T(8,128)S(1)}, f32[64,72,128]{2,1,0:T(8,128)S(1)}, f32[4,128,16,128]{3,2,1,0:T(8,128)S(1)}, ...) custom-call(f32[64,80,128]{2,1,0:T(8,128)S(1)} %get-tuple-element.53, ...), custom_call_target="tpu_custom_call", output_to_operand_aliasing={{2}: (9, {}), {3}: (10, {}), {4}: (11, {}), {5}: (12, {})} | custom-call | flops 2000000000 | bytes 1000000 | tf_op jit(solution)/shard_map/pallas_call | solution.py:738
  34.4 15.2 %all_to_all.11 = f32[32,1,128]{2,1,0:T(1,128)S(1)} all-to-all(f32[32,1,128]{2,1,0:T(1,128)S(1)} %bitcast.5), channel_id=1, replica_groups=mesh['gy'=8,'gx'=4] {'gy','gx'}, dimensions={0} | all-to-all | bytes 32768 | tf_op jit(solution)/shard_map/all_to_all | solution.py:752
  49.6 1.5 %shard_map.86 = (f32[32,2,64,128]{3,2,1,0:T(8,128)}, f32[2,64,128]{2,1,0:T(8,128)}) custom-call(f32[32,128]{1,0:T(8,128)S(1)} %bitcast.4, f32[64,72,128]{2,1,0:T(8,128)S(1)} %get-tuple-element.82.z_one, f32[64,72,128]{2,1,0:T(8,128)S(1)} %get-tuple-element.83.z_two, f32[2,64,128]{2,1,0:T(8,128)S(1)} %get-tuple-element.84.x_one, ...), custom_call_target="tpu_custom_call" | custom-call | tf_op jit(solution)/shard_map/pallas_call | solution.py:754
  (3 shorter events, 0.0 us)
Async XLA Ops:
  0.6 6.5 %copy-start.3 = (bf16[4,2,128,512]{3,2,1,0:T(8,128)(2,1)S(1)}, bf16[4,2,128,512]{3,2,1,0:T(8,128)(2,1)}, u32[]{:S(2)}) copy-start(bf16[4,2,128,512]{3,2,1,0:T(8,128)(2,1)} %constant.2.clone.bands_in) | copy-start | bytes 3145732
  0.6 6.5 %copy-start.2 = (bf16[32,2,64,128]{3,2,1,0:T(8,128)(2,1)S(1)}, bf16[32,2,64,128]{3,2,1,0:T(8,128)(2,1)}, u32[]{:S(2)}) copy-start(bf16[32,2,64,128]{3,2,1,0:T(8,128)(2,1)} %ens_in.1) | copy-start | bytes 3145732
  3.4 14.9 %collective-permute-start = (f32[66,8,128]{2,1,0:T(8,128)}, f32[66,8,128]{2,1,0:T(8,128)S(1)}, u32[]{:S(2)}, u32[]{:S(2)}) collective-permute-start(f32[66,8,128]{2,1,0:T(8,128)} %get-tuple-element.44), channel_id=1, source_target_pairs={{0,4},{4,0},{8,12},{12,8},{16,20},{20,16},{24,28},{28,24},{1,5},{5... | collective-permute-start | bytes 811016 | tf_op jit(solution)/shard_map/ppermute | solution.py:55
  6.4 11.9 %collective-permute-start.1 = (f32[66,8,128]{2,1,0:T(8,128)}, f32[66,8,128]{2,1,0:T(8,128)S(1)}, u32[]{:S(2)}, u32[]{:S(2)}) collective-permute-start(f32[66,8,128]{2,1,0:T(8,128)} %get-tuple-element.45), channel_id=1, source_target_pairs={{4,8},{8,4},{12,16},{16,12},{20,24},{24,20},{5,9},{9,5},{13,17},{1... | collective-permute-start | bytes 811016 | tf_op jit(solution)/shard_map/ppermute | solution.py:55
  7.1 0.9 %copy-start = (f32[2,2,64,128]{3,2,1,0:T(8,128)S(1)}, f32[2,2,64,128]{3,2,1,0:T(8,128)}, u32[]{:S(2)}) copy-start(f32[2,2,64,128]{3,2,1,0:T(8,128)} %get-tuple-element.46.grid.g) | copy-start | bytes 393220
  9.9 11.0 %collective-permute-start.2 = (f32[9,64,128]{2,1,0:T(8,128)S(1)}, f32[9,64,128]{2,1,0:T(8,128)S(1)}, u32[]{:S(2)}, u32[]{:S(2)}) collective-permute-start(f32[9,64,128]{2,1,0:T(8,128)S(1)} %get-tuple-element.55), channel_id=1, source_target_pairs={{0,1},{1,0},{2,3},{3,2},{4,5},{5,4},{6,7},{7,6},{8,9},{9,8},{10,11... | collective-permute-start | bytes 884744 | tf_op jit(solution)/shard_map/ppermute | solution.py:55
  10.0 10.9 %collective-permute-start.3 = (f32[9,64,128]{2,1,0:T(8,128)S(1)}, f32[9,64,128]{2,1,0:T(8,128)S(1)}, u32[]{:S(2)}, u32[]{:S(2)}) collective-permute-start(f32[9,64,128]{2,1,0:T(8,128)S(1)} %get-tuple-element.56), channel_id=1, source_target_pairs={{1,2},{2,1},{5,6},{6,5},{9,10},{10,9},{13,14},{14,13},{17,18},{18,... | collective-permute-start | bytes 884744 | tf_op jit(solution)/shard_map/ppermute | solution.py:55
  19.3 3.7 %collective-permute-start.4 = (f32[9,16,128]{2,1,0:T(8,128)S(1)}, f32[9,16,128]{2,1,0:T(8,128)S(1)}, u32[]{:S(2)}, u32[]{:S(2)}) collective-permute-start(f32[9,16,128]{2,1,0:T(8,128)S(1)} %get-tuple-element.63), channel_id=1, source_target_pairs={{0,1},{1,0},{2,3},{3,2},{4,5},{5,4},{6,7},{7,6},{8,9},{9,8},{10,11... | collective-permute-start | bytes 221192 | tf_op jit(solution)/shard_map/ppermute | solution.py:55
  19.3 3.7 %collective-permute-start.5 = (f32[9,16,128]{2,1,0:T(8,128)S(1)}, f32[9,16,128]{2,1,0:T(8,128)S(1)}, u32[]{:S(2)}, u32[]{:S(2)}) collective-permute-start(f32[9,16,128]{2,1,0:T(8,128)S(1)} %get-tuple-element.64), channel_id=1, source_target_pairs={{1,2},{2,1},{5,6},{6,5},{9,10},{10,9},{13,14},{14,13},{17,18},{18,... | collective-permute-start | bytes 221192 | tf_op jit(solution)/shard_map/ppermute | solution.py:55
  24.0 7.1 %collective-permute-start.6 = (f32[3,8,128]{2,1,0:T(8,128)S(1)}, f32[3,8,128]{2,1,0:T(8,128)S(1)}, u32[]{:S(2)}, u32[]{:S(2)}) collective-permute-start(f32[3,8,128]{2,1,0:T(8,128)S(1)} %get-tuple-element.72), channel_id=1, source_target_pairs={{0,4},{4,0},{8,12},{12,8},{16,20},{20,16},{24,28},{28,24},{1,5},{5... | collective-permute-start | bytes 36872 | tf_op jit(solution)/shard_map/ppermute | solution.py:55
  26.8 4.3 %collective-permute-start.7 = (f32[3,8,128]{2,1,0:T(8,128)S(1)}, f32[3,8,128]{2,1,0:T(8,128)S(1)}, u32[]{:S(2)}, u32[]{:S(2)}) collective-permute-start(f32[3,8,128]{2,1,0:T(8,128)S(1)} %get-tuple-element.73), channel_id=1, source_target_pairs={{4,8},{8,4},{12,16},{16,12},{20,24},{24,20},{5,9},{9,5},{13,17},{1... | collective-permute-start | bytes 36872 | tf_op jit(solution)/shard_map/ppermute | solution.py:55
  27.5 3.6 %copy-start.1 = (f32[2,2,64,128]{3,2,1,0:T(8,128)S(1)}, f32[2,2,64,128]{3,2,1,0:T(8,128)}, u32[]{:S(2)}) copy-start(f32[2,2,64,128]{3,2,1,0:T(8,128)} %get-tuple-element.46.grid.g) | copy-start | bytes 393220
